TPU v7x, 128 devices: a whole 4x4x4 slice. The times are simulated.
128 devices in a mesh: gx: 8 (over x, z_lo), gy: 16 (over z_hi, y, core).
Axes of the slice: x: 4, y: 4, z: 4 (z_hi: 2, z_lo: 2; z = z_hi * 2 + z_lo), core: 2. Of those that a mesh axis runs over, the one named last changes fastest.
Arguments:
- velocity: float32 [2, 4096, 8192], P(None, 'gx', 'gy'), may hold values from -3 to 3
- stress: float32 [3, 4096, 8192], P(None, 'gx', 'gy'), may hold values from -3 to 3
- strength: float32 [4096, 8192], P('gx', 'gy'), may hold values from 0.5 to 4
- ice_mass: float32 [4096, 8192], P('gx', 'gy'), may hold values from 0.3 to 20, as said below
- wind_stress: float32 [2, 4096, 8192], P(None, 'gx', 'gy'), may hold values from -6 to 6
- current: float32 [2, 4096, 8192], P(None, 'gx', 'gy'), may hold values from -3 to 3
- ice_mask: int32 [4096, 8192], P('gx', 'gy'), may hold values from 0 to 1, as said below
- open_water: int32 [4096, 8192], P('gx', 'gy'), may hold values 0 or 1
Outputs:
- new_velocity: float32 [2, 4096, 8192], P(None, 'gx', 'gy')
- new_stress: float32 [3, 4096, 8192], P(None, 'gx', 'gy')
- residual: float32 [], replicated
- kinetic_energy: float32 [], replicated
Inputs may be any that keep to these rules, and one draw needn't show every extreme that they name: `ice_mask`: 1 marks an ocean cell, 0 a land cell. `ice_mass`: positive everywhere.
All inputs are finite; a program needn't handle non-finite values. No bound on the sum of `open_water` on one device may be relied on, other than what follows from the above.
Results may differ from a plain program's by a relative error of at most 0.00002.
Values sent between devices are 32-bit elements; how exact they have to be, the bound alone decides.
No kernel may reach another device: no remote copies, remote signals or barrier semaphores. Data moves between devices by JAX's collectives and lax.ppermute only.
A program may use at most 128 MiB of HBM per device.

v0:
```python
import functools

import jax
import jax.numpy as jnp
from jax import lax
from jax.experimental import pallas as pl
from jax.experimental.pallas import tpu as pltpu
from jax.sharding import PartitionSpec as P

ITERS = 4
RELAX = 0.8
GROW = 1.0 / (1.0 + RELAX)
KAPPA = RELAX / (1.0 + RELAX)
PAD = 8
F32 = jnp.float32
(U_, V_, H1, H2, H12, K_, M8, FU, FV, CA, CB) = range(11)
NS = 9
NF = 11
ALL = ("gx", "gy")


def weight_of(mask, openw):
    return mask.astype(F32) * (1.0 - openw.astype(F32))


def consts(strength, mass, wind, cur, weight):
    return (KAPPA * strength) * weight, mass * 8.0, 4.0 * (wind[0] + cur[0]), 4.0 * (wind[1] + cur[1])


def coefs(m8, weight):
    a = m8 * 0.25 + 1.0
    b = m8 * 0.0375
    scale = (0.25 * weight) / (a * a + b * b)
    return a * scale, b * scale


def strain(u, v, um, vm):
    su = u + um
    du = u - um
    sv = v + vm
    dv = v - vm
    return su + dv, su - dv, du + sv, du - sv


def stress_rate(alpha, beta, gamma, alpha_m, beta_m, delta_m, k):
    d = alpha - beta_m
    t = beta - alpha_m
    s = gamma + delta_m
    q = d * d + 0.25 * (t * t + s * s) + 0.01
    r = lax.rsqrt(q)
    z = k * r
    z4 = 0.25 * z
    return z * (d - q * r), z4 * t, z4 * s


def mixes(h1, h2, h12):
    e = h1 + h2
    g = h1 - h2
    return e + h12, e - h12, h12 + g, h12 - g


def drift(u, v, fx, fy, m8, fu, fv, ca, cb):
    ru = m8 * u + (fx + fu)
    rv = m8 * v + (fy + fv)
    return ca * ru + cb * rv, ca * rv - cb * ru


def pair_rows(parts, high):
    half = lax.broadcasted_iota(jnp.int32, parts[0].shape, 0) < 4
    tiles = []
    for f in range(0, NS, 2):
        a = parts[f]
        b = parts[f + 1] if f + 1 < NS else jnp.zeros_like(a)
        if high:
            tiles.append(jnp.where(half, pltpu.roll(a, 4, 0), b))
        else:
            tiles.append(jnp.where(half, a, pltpu.roll(b, 4, 0)))
    return jnp.concatenate(tiles, 0)


def unpair(tiles, f, high):
    x = tiles[8 * (f // 2) : 8 * (f // 2) + 8]
    return x if (f % 2 == 1) == high else pltpu.roll(x, 4, 0)


def is_even(axis):
    return lax.axis_index(axis) % 2 == 0


def strip_fields(vel, strs, strength, mass, wind, cur, mask, openw):
    w = weight_of(mask[...], openw[...])
    k, m8, fu, fv = consts(strength[...], mass[...], (wind[0], wind[1]), (cur[0], cur[1]), w)
    return [vel[0], vel[1], strs[0], strs[1], 2.0 * strs[2], k, m8, fu, fv]


def rows_kernel(*refs):
    own, msg_a, msg_b = refs[16:]
    top = strip_fields(*refs[:8])
    bot = strip_fields(*refs[8:16])
    for f in range(NS):
        own[f, 0:8, :] = top[f]
        own[f, 8:16, :] = bot[f]
    low = pair_rows(top, False)
    high = pair_rows(bot, True)
    even = is_even("gx")
    msg_a[...] = jnp.where(even, high, low)
    msg_b[...] = jnp.where(even, low, high)


def cols_kernel(*refs):
    out = refs[16]
    lane = lax.broadcasted_iota(jnp.int32, (128, 128), 1)
    for side in range(2):
        fields = strip_fields(*refs[8 * side : 8 * side + 8])
        x = jnp.zeros((128, 128), F32)
        for f in range(NS):
            shift = (8 * f - 120 * side) % 128
            y = pltpu.roll(fields[f], shift, 1) if shift else fields[f]
            x = jnp.where((lane >= 8 * f) & (lane < 8 * f + 8), y, x)
        out[8 * NS * side : 8 * NS * (side + 1), :] = x.T[0 : 8 * NS]


def corners_kernel(cols, xa, xb, ya, yb, ext):
    even = is_even("gx")
    a, b = xa[...], xb[...]
    top = jnp.where(even, b, a)
    bot = jnp.where(even, a, b)
    C = cols.shape[1]
    lane = lax.broadcasted_iota(jnp.int32, (8, 128), 1)
    strips = []
    for side in range(2):
        at = side * (C - 128)
        t = jnp.concatenate([top[:, at : at + 128], bot[:, at : at + 128], jnp.zeros((48, 128), F32)], 0).T
        t = t[120 * side : 120 * side + 8]
        own = []
        for f in range(NS):
            e = jnp.where(lane >= 124, pltpu.roll(t, 124 - 4 * f, 1), 0.0)
            e = jnp.where(lane < 4, pltpu.roll(t, 128 - 40 - 4 * f, 1), e)
            base = 8 * (NS * side + f)
            ext[base : base + 8, :] = e
            own.append(jnp.concatenate([cols[base : base + 8, :], e], 1))
        strips.append(pair_rows(own, side == 1))
    low, high = strips
    even = is_even("gy")
    ya[...] = jnp.where(even, high, low)
    yb[...] = jnp.where(even, low, high)


def interior_kernel(vel, strs, strength, mass, wind, cur, mask, openw, nvel, nstr, sums, buf, ibuf, al, be, ga, de, tx, ty, nx, ny, insem, outsem, *, RB, NCH):
    R = vel.shape[1]
    NT = vel.shape[2] // 128
    CH = R // NCH

    srcs = [(vel, 0, U_), (vel, 1, V_), (strs, 0, H1), (strs, 1, H2), (strs, 2, H12), (strength, None, K_), (mass, None, M8),
            (wind, 0, FU), (wind, 1, FV), (cur, 0, CA), (cur, 1, CB)]

    for c in range(NCH):
        rows = pl.ds(c * CH, CH)
        rows_b = pl.ds(PAD + c * CH, CH)
        for t in range(NT):
            cols = pl.ds(t * 128, 128)
            for ref, lead, f in srcs:
                src = ref.at[rows, cols] if lead is None else ref.at[lead, rows, cols]
                pltpu.make_async_copy(src, buf.at[f, t, rows_b, :], insem.at[c]).start()
            for n, ref in enumerate((mask, openw)):
                pltpu.make_async_copy(ref.at[rows, cols], ibuf.at[n, t, rows, :], insem.at[NCH + c]).start()
    zero = jnp.zeros((8, 128), F32)
    for t in range(NT):
        for ref in (al, be, de):
            ref[t, 0:PAD, :] = zero
        for ref in (tx, ty):
            ref[t, PAD + R : PAD + R + 8, :] = zero
    lane = lax.broadcasted_iota(jnp.int32, (RB, 128), 1)
    row_in = lax.broadcasted_iota(jnp.int32, (RB, 128), 0)
    first = lane == 0
    last = lane == 127

    def shift_m(x):
        r = [pltpu.roll(a, 1, 1) for a in x]
        return [jnp.where(first, r[(t - 1) % NT], r[t]) for t in range(NT)]

    def shift_p(x):
        r = [pltpu.roll(a, 127, 1) for a in x]
        return [jnp.where(last, r[(t + 1) % NT], r[t]) for t in range(NT)]

    def prepare(r0):
        rows = pl.ds(PAD + r0, RB)
        irows = pl.ds(r0, RB)
        for t in range(NT):
            w = weight_of(ibuf[0, t, irows, :], ibuf[1, t, irows, :])
            wind_t = (buf[FU, t, rows, :], buf[FV, t, rows, :])
            cur_t = (buf[CA, t, rows, :], buf[CB, t, rows, :])
            k, m8, fu, fv = consts(buf[K_, t, rows, :], buf[M8, t, rows, :], wind_t, cur_t, w)
            ca, cb = coefs(m8, w)
            buf[K_, t, rows, :] = k
            buf[M8, t, rows, :] = m8
            buf[FU, t, rows, :] = fu
            buf[FV, t, rows, :] = fv
            buf[CA, t, rows, :] = ca
            buf[CB, t, rows, :] = cb
            buf[H12, t, rows, :] = buf[H12, t, rows, :] * 2.0

    def strain_rows(r0):
        rows = pl.ds(PAD + r0, RB)
        u = [buf[U_, t, rows, :] for t in range(NT)]
        v = [buf[V_, t, rows, :] for t in range(NT)]
        um, vm = shift_m(u), shift_m(v)
        for t in range(NT):
            a, b, g, d = strain(u[t], v[t], um[t], vm[t])
            al[t, rows, :] = a
            be[t, rows, :] = b
            ga[t, rows, :] = g
            de[t, rows, :] = d

    def rate_rows(r0, final):
        rows = pl.ds(PAD + r0, RB)
        above = pl.ds(PAD + r0 - 1, RB)
        mx = []
        for t in range(NT):
            d1, d2, d12 = stress_rate(al[t, rows, :], be[t, rows, :], ga[t, rows, :], al[t, above, :], be[t, above, :], de[t, above, :], buf[K_, t, rows, :])
            h1 = buf[H1, t, rows, :] * GROW + d1
            h2 = buf[H2, t, rows, :] * GROW + d2
            h12 = buf[H12, t, rows, :] * GROW + d12
            buf[H1, t, rows, :] = h1
            buf[H2, t, rows, :] = h2
            buf[H12, t, rows, :] = 0.5 * h12 if final else h12
            mx.append(mixes(h1, h2, h12))
        up, wp, xp, yp = (shift_p([m[i] for m in mx]) for i in range(4))
        for t in range(NT):
            tx[t, rows, :] = up[t] + mx[t][1]
            nx[t, rows, :] = mx[t][0] + wp[t]
            ty[t, rows, :] = xp[t] + mx[t][3]
            ny[t, rows, :] = mx[t][2] + yp[t]

    def velocity_rows(r0, acc):
        rows = pl.ds(PAD + r0, RB)
        below = pl.ds(PAD + r0 + 1, RB)
        for t in range(NT):
            u, v, m8 = buf[U_, t, rows, :], buf[V_, t, rows, :], buf[M8, t, rows, :]
            fx = tx[t, below, :] - nx[t, rows, :]
            fy = ty[t, below, :] - ny[t, rows, :]
            nu, nv = drift(u, v, fx, fy, m8, buf[FU, t, rows, :], buf[FV, t, rows, :], buf[CA, t, rows, :], buf[CB, t, rows, :])
            buf[U_, t, rows, :] = nu
            buf[V_, t, rows, :] = nv
            if acc is not None:
                keep = (buf[K_, t, rows, :] > 0.0) & (row_in + r0 >= ITERS) & (row_in + r0 < R - ITERS)
                if t == 0:
                    keep = keep & (lane >= ITERS)
                if t == NT - 1:
                    keep = keep & (lane < 128 - ITERS)
                cu, cv = nu - u, nv - v
                acc = (acc[0] + jnp.where(keep, cu * cu + cv * cv, 0.0), acc[1] + jnp.where(keep, m8 * (nu * nu + nv * nv), 0.0))
        return acc

    NB = R // RB
    nbc = CH // RB
    LV = 3

    def step(r0, acc, lo, hi, prep, final):
        if lo <= 0 < hi:
            if prep:
                prepare(r0)
            strain_rows(r0)
        if lo <= 1 < hi:
            rate_rows(r0 - RB, final)
        if lo <= LV < hi:
            acc = velocity_rows(r0 - LV * RB, acc)
        return acc

    def sweep(acc, begin, end, prep=False, final=False):
        i = begin
        while i < min(end, LV):
            acc = step(i * RB, acc, 0, i + 1, prep, final)
            i += 1
        stop = min(end, NB)
        if i < stop:
            if acc is None:

                def body(j, c):
                    step(pl.multiple_of(j * RB, RB), None, 0, LV + 1, prep, final)
                    return c

                lax.fori_loop(i, stop, body, 0)
            else:
                acc = lax.fori_loop(i, stop, lambda j, c: step(pl.multiple_of(j * RB, RB), c, 0, LV + 1, prep, final), acc)
            i = stop
        while i < end:
            acc = step(i * RB, acc, i - NB + 1, LV + 1, prep, final)
            i += 1
        return acc

    for c in range(NCH):
        whole = buf.at[:, :, pl.ds(PAD + c * CH, CH), :]
        pltpu.make_async_copy(whole, whole, insem.at[c]).wait()
        whole = ibuf.at[:, :, pl.ds(c * CH, CH), :]
        pltpu.make_async_copy(whole, whole, insem.at[NCH + c]).wait()
        sweep(None, c * nbc, (c + 1) * nbc if c < NCH - 1 else NB + LV, prep=True)
    for _ in range(1, ITERS - 1):
        sweep(None, 0, NB + LV)
    acc = (jnp.zeros((RB, 128), F32), jnp.zeros((RB, 128), F32))
    for c in range(NCH):
        acc = sweep(acc, c * nbc + (LV if c else 0), (c + 1) * nbc + LV, final=True)
        rows = pl.ds(c * CH, CH)
        rows_b = pl.ds(PAD + c * CH, CH)
        for ref, lead, f in ((nvel, 0, U_), (nvel, 1, V_), (nstr, 0, H1), (nstr, 1, H2), (nstr, 2, H12)):
            for t in range(NT):
                pltpu.make_async_copy(buf.at[f, t, rows_b, :], ref.at[lead, rows, pl.ds(t * 128, 128)], outsem.at[c]).start()
    for n in range(2):
        sums[n] = acc[n].reshape(RB // 8, 8, 128).sum(0)
    for c in range(NCH):
        whole = buf.at[pl.ds(0, 5), :, pl.ds(PAD + c * CH, CH), :]
        pltpu.make_async_copy(whole, whole, outsem.at[c]).wait()


def strip_subcycles(ref, acc_ref, rows_axis, keep):
    cols_axis = 1 - rows_axis
    back = lambda x, axis: pltpu.roll(x, 1, axis)
    ahead = lambda x, axis: pltpu.roll(x, x.shape[axis] - 1, axis)
    w = jnp.where(ref[K_] > 0.0, 1.0, 0.0)
    ca, cb = coefs(ref[M8], w)
    ref[CA] = ca
    ref[CB] = cb

    def body(_, carry):
        u, v = ref[U_], ref[V_]
        a, b, g, d = strain(u, v, back(u, cols_axis), back(v, cols_axis))
        d1, d2, d12 = stress_rate(a, b, g, back(a, rows_axis), back(b, rows_axis), back(d, rows_axis), ref[K_])
        h1 = ref[H1] * GROW + d1
        h2 = ref[H2] * GROW + d2
        h12 = ref[H12] * GROW + d12
        ref[H1] = h1
        ref[H2] = h2
        ref[H12] = h12
        up, wp, xp, yp = mixes(h1, h2, h12)
        fx = ahead(ahead(up, cols_axis) + wp, rows_axis) - (up + ahead(wp, cols_axis))
        fy = ahead(ahead(xp, cols_axis) + yp, rows_axis) - (xp + ahead(yp, cols_axis))
        m8 = ref[M8]
        nu, nv = drift(u, v, fx, fy, m8, ref[FU], ref[FV], ref[CA], ref[CB])
        ref[U_] = nu
        ref[V_] = nv
        cu, cv = nu - u, nv - v
        inside = keep & (ref[K_] > 0.0)
        acc_ref[0] = jnp.where(inside, cu * cu + cv * cv, 0.0)
        acc_ref[1] = jnp.where(inside, m8 * (nu * nu + nv * nv), 0.0)
        return carry

    lax.fori_loop(0, ITERS, body, 0)
    return [jnp.sum(acc_ref[0]), jnp.sum(acc_ref[1])]


def frame_kernel(own, cols, ext, xa, xb, ya, yb, isums, nvel_in, nstr_in, nvel, nstr, msg, cs, rs, cacc, racc, edge, mid, sem):
    R, C = nvel.shape[1:]
    outs = ((nvel, 0), (nvel, 1), (nstr, 0), (nstr, 1), (nstr, 2))

    def places(f):
        ref, lead = outs[f]
        full = ref.at[lead]
        inner = pl.ds(128, C - 256)
        return (
            (full.at[:, pl.ds(0, 128)], edge.at[0, f]),
            (full.at[:, pl.ds(C - 128, 128)], edge.at[1, f]),
            (full.at[pl.ds(0, 8), inner], mid.at[0, f]),
            (full.at[pl.ds(R - 8, 8), inner], mid.at[1, f]),
        )

    for f in range(5):
        for n, (there, here) in enumerate(places(f)):
            pltpu.make_async_copy(there, here, sem.at[0, n // 2]).start()
    even = is_even("gx")
    a, b = xa[...], xb[...]
    top = jnp.where(even, b, a)
    bot = jnp.where(even, a, b)
    even = is_even("gy")
    a, b = ya[...], yb[...]
    left = jnp.where(even, b, a)
    right = jnp.where(even, a, b)
    for f in range(NS):
        rs[f, 0:8, :] = unpair(top, f, True)
        rs[f, 8:16, :] = own[f, 0:8, :]
        rs[f, 16:24, :] = own[f, 8:16, :]
        rs[f, 24:32, :] = unpair(bot, f, False)
        cs[f, 0:8, :] = unpair(left, f, True)
        for side in range(2):
            base = 8 * (NS * side + f)
            cs[f, 8 + 8 * side : 16 + 8 * side, 0:R] = cols[base : base + 8, :]
            cs[f, 8 + 8 * side : 16 + 8 * side, R : R + 128] = ext[base : base + 8, :]
        cs[f, 24:32, :] = unpair(right, f, False)

    def rim(shape):
        sub = lax.broadcasted_iota(jnp.int32, shape, 0)
        return ((sub >= 8) & (sub < 12)) | ((sub >= 20) & (sub < 24)), lax.broadcasted_iota(jnp.int32, shape, 1)

    band, lane = rim(rs.shape[1:])
    row_sums = strip_subcycles(rs, racc, 0, band & (lane >= ITERS) & (lane < C - ITERS))
    band, lane = rim(cs.shape[1:])
    col_sums = strip_subcycles(cs, cacc, 1, band & (lane < R))
    lane = lax.broadcasted_iota(jnp.int32, msg.shape, 1)
    totals = [jnp.sum(isums[n]) + row_sums[n] + col_sums[n] for n in range(2)]
    msg[...] = jnp.where(lane == 0, totals[0], jnp.where(lane == 1, totals[1], 0.0))

    for n in range(2):
        buf = (edge, mid)[n]
        pltpu.make_async_copy(buf, buf, sem.at[0, n]).wait()
    halves = (1.0, 1.0, 1.0, 1.0, 0.5)
    low8 = lax.broadcasted_iota(jnp.int32, (8, 128), 0) < 4
    for f in range(5):
        for part, sub in ((0, 8), (1, 16)):
            x = rs[f, sub : sub + 8, 128 : C - 128] * halves[f]
            half = lax.broadcasted_iota(jnp.int32, x.shape, 0) < 4
            mid[part, f] = jnp.where(half if part == 0 else ~half, x, mid[part, f])
        for side in range(2):
            at = side * (C - 128)
            x = rs[f, 8:16, at : at + 128] * halves[f]
            edge[side, f, 0:8, :] = jnp.where(low8, x, edge[side, f, 0:8, :])
            x = rs[f, 16:24, at : at + 128] * halves[f]
            edge[side, f, R - 8 : R, :] = jnp.where(low8, edge[side, f, R - 8 : R, :], x)
    lane = lax.broadcasted_iota(jnp.int32, (128, 128), 1)
    for c in range(R // 128):
        rows = slice(c * 128, c * 128 + 128)
        parts = [cs[f, 8 + 8 * side : 16 + 8 * side, rows] * halves[f] for side in range(2) for f in range(5)]
        x = jnp.concatenate(parts + [jnp.zeros((48, 128), F32)], 0).T
        for side in range(2):
            for f in range(5):
                shift = (120 * side - 8 * (5 * side + f)) % 128
                y = pltpu.roll(x, shift, 1) if shift else x
                hit = lane >= 124 if side else lane < 4
                edge[side, f, rows, :] = jnp.where(hit, y, edge[side, f, rows, :])
    for f in range(5):
        for n, (there, here) in enumerate(places(f)):
            pltpu.make_async_copy(here, there, sem.at[1, n // 2]).start()
    for n in range(2):
        buf = (edge, mid)[n]
        pltpu.make_async_copy(buf, buf, sem.at[1, n]).wait()


def swaps(count):
    first = [(i, i ^ 1) for i in range(count)]
    second = [(i, i + 1) for i in range(1, count - 1, 2)] + [(i + 1, i) for i in range(1, count - 1, 2)]
    return first, second


def exchange(a, b, axis):
    first, second = swaps(lax.axis_size(axis))
    return lax.ppermute(a, axis, first), lax.ppermute(b, axis, second)


def sds(*shape):
    return jax.ShapeDtypeStruct(shape, F32)


def per_device(velocity, stress, strength, ice_mass, wind_stress, current, ice_mask, open_water):
    args = (velocity, stress, strength, ice_mass, wind_stress, current, ice_mask, open_water)
    R, C = strength.shape
    anyspace = pl.BlockSpec(memory_space=pl.ANY)
    vmem = pl.BlockSpec(memory_space=pltpu.VMEM)
    limit = pltpu.CompilerParams(vmem_limit_bytes=48 * 2**20)

    def blocks(shape, where):
        return [pl.BlockSpec((x.shape[0],) * (x.ndim - 2) + shape, functools.partial(lambda nd, *g: (0,) * (nd - 2) + where(*g), x.ndim)) for x in args]

    own, xa, xb = pl.pallas_call(
        rows_kernel,
        grid=(1,),
        in_specs=blocks((8, C), lambda i: (0, 0)) + blocks((8, C), lambda i: (R // 8 - 1, 0)),
        out_specs=[pl.BlockSpec((NS, 16, C), lambda i: (0, 0, 0)), pl.BlockSpec((40, C), lambda i: (0, 0)), pl.BlockSpec((40, C), lambda i: (0, 0))],
        out_shape=[sds(NS, 16, C), sds(40, C), sds(40, C)],
        name="row_edges",
    )(*args, *args)
    xa, xb = exchange(xa, xb, "gx")
    cols = pl.pallas_call(
        cols_kernel,
        grid=(R // 128,),
        in_specs=blocks((128, 128), lambda i: (i, 0)) + blocks((128, 128), lambda i: (i, C // 128 - 1)),
        out_specs=pl.BlockSpec((16 * NS, 128), lambda i: (0, i)),
        out_shape=sds(16 * NS, R),
        name="col_edges",
    )(*args, *args)
    ya, yb, ext = pl.pallas_call(
        corners_kernel,
        in_specs=[vmem] * 3,
        out_specs=[vmem] * 3,
        out_shape=[sds(40, R + 128), sds(40, R + 128), sds(16 * NS, 128)],
        name="corners",
    )(cols, xa, xb)
    ya, yb = exchange(ya, yb, "gy")
    NT = C // 128
    RP = R + 2 * PAD
    NCH = 4
    nvel, nstr, isums = pl.pallas_call(
        functools.partial(interior_kernel, RB=32, NCH=NCH),
        in_specs=[anyspace] * 8,
        out_specs=(anyspace, anyspace, vmem),
        out_shape=(sds(2, R, C), sds(3, R, C), sds(2, 8, 128)),
        scratch_shapes=[pltpu.VMEM((NF, NT, RP, 128), F32), pltpu.VMEM((2, NT, R, 128), jnp.int32)]
        + [pltpu.VMEM((NT, RP, 128), F32)] * 8
        + [pltpu.SemaphoreType.DMA((2 * NCH,)), pltpu.SemaphoreType.DMA((NCH,))],
        compiler_params=limit,
        name="interior",
    )(*args)
    ND = lax.axis_size(ALL)
    nvel, nstr, msg = pl.pallas_call(
        frame_kernel,
        in_specs=[vmem] * 8 + [anyspace] * 2,
        out_specs=(anyspace, anyspace, vmem),
        out_shape=(sds(2, R, C), sds(3, R, C), sds(ND, 128)),
        scratch_shapes=[
            pltpu.VMEM((NF, 32, R + 128), F32),
            pltpu.VMEM((NF, 32, C), F32),
            pltpu.VMEM((2, 32, R + 128), F32),
            pltpu.VMEM((2, 32, C), F32),
            pltpu.VMEM((2, 5, R, 128), F32),
            pltpu.VMEM((2, 5, 8, C - 256), F32),
            pltpu.SemaphoreType.DMA((2, 2)),
        ],
        input_output_aliases={8: 0, 9: 1},
        compiler_params=limit,
        name="frame",
    )(own, cols, ext, xa, xb, ya, yb, isums, nvel, nstr)
    parts = lax.all_to_all(msg, ALL, 0, 0, tiled=True)
    total = jnp.sum(parts, axis=0)
    cells = R * lax.axis_size("gx") * C * lax.axis_size("gy")
    return nvel, nstr, total[0] / cells, total[1] * (0.0625 / cells)


def solution(mesh):
    whole, plane = P(None, "gx", "gy"), P("gx", "gy")
    return jax.shard_map(
        per_device,
        mesh=mesh,
        in_specs=(whole, whole, plane, plane, whole, whole, plane, plane),
        out_specs=(whole, whole, P(), P()),
        check_vma=False,
    )
```

profile of v0, /device:TPU:1, one launch (start us, length us, event | category | flops | bytes accessed | tf_op | source)
XLA Modules:
  0.0 67.9 jit_solution(5466333535800222059)
XLA Ops:
  0.6 1.8 %row_edges.1 = (f32[9,16,512]{2,1,0:T(8,128)}, f32[40,512]{1,0:T(8,128)}, f32[40,512]{1,0:T(8,128)}) custom-call(f32[2,512,512]{2,1,0:T(8,128)} %vel.1, f32[3,512,512]{2,1,0:T(8,128)} %strs.1, f32[512,512]{1,0:T(8,128)} %strength.1, f32[512,512]{1,0:T(8,128)} %mass.1, f32[2,512,512]{2,1,0:T(8,128)} %wind.1, f32[2,512,512]{2,1,0:T(8,128)} %cur.1, ...), custom_call_target="tpu_custom_call" | custom-call | tf_op jit(solution)/shard_map/row_edges/pallas_call | solution.py:461
  2.4 2.5 %collective-permute-start = (f32[40,512]{1,0:T(8,128)}, f32[40,512]{1,0:T(8,128)S(1)}, u32[]{:S(2)}, u32[]{:S(2)}) collective-permute-start(f32[40,512]{1,0:T(8,128)} %get-tuple-element.17), channel_id=1, source_target_pairs={{0,16},{16,0},{32,48},{48,32},{64,80},{80,64},{96,112},{112,96},{1... | collective-permute-start | bytes 245768 | tf_op jit(solution)/shard_map/ppermute | solution.py:444
  4.9 0.8 %collective-permute-start.1 = (f32[40,512]{1,0:T(8,128)}, f32[40,512]{1,0:T(8,128)S(1)}, u32[]{:S(2)}, u32[]{:S(2)}) collective-permute-start(f32[40,512]{1,0:T(8,128)} %get-tuple-element.18), channel_id=1, source_target_pairs={{16,32},{48,64},{80,96},{32,16},{64,48},{96,80},{17,33},{49,65},{8... | collective-permute-start | bytes 245768 | tf_op jit(solution)/shard_map/ppermute | solution.py:444
  5.7 5.2 %col_edges.1.cols = f32[144,512]{1,0:T(8,128)} custom-call(f32[2,512,512]{2,1,0:T(8,128)} %vel.1, f32[3,512,512]{2,1,0:T(8,128)} %strs.1, f32[512,512]{1,0:T(8,128)} %strength.1, f32[512,512]{1,0:T(8,128)} %mass.1, f32[2,512,512]{2,1,0:T(8,128)} %wind.1, f32[2,512,512]{2,1,0:T(8,128)} %cur.1, s32[512,512]{1,0:T(8,128)} %mask.1, s32[512,512]{1,0:T(8,128)} %openw.1, ...), custom_call_target="tpu_custom_call" | custom-call | tf_op jit(solution)/shard_map/col_edges/pallas_call | solution.py:470
  10.9 0.0 collective-permute-done.xa
  10.9 0.0 copy-start.5
  10.9 0.0 collective-permute-done.1.xb
  10.9 0.6 copy-done.5
  11.5 0.6 copy-done.7
  12.2 1.9 %corners.1 = (f32[40,640]{1,0:T(8,128)}, f32[40,640]{1,0:T(8,128)}, f32[144,128]{1,0:T(8,128)}) custom-call(f32[144,512]{1,0:T(8,128)} %col_edges.1.cols, f32[40,512]{1,0:T(8,128)} %copy-done.5, f32[40,512]{1,0:T(8,128)} %copy-done.7), custom_call_target="tpu_custom_call" | custom-call | tf_op jit(solution)/shard_map/corners/pallas_call | solution.py:478
  14.1 1.0 %collective-permute-start.2 = (f32[40,640]{1,0:T(8,128)}, f32[40,640]{1,0:T(8,128)S(1)}, u32[]{:S(2)}, u32[]{:S(2)}) collective-permute-start(f32[40,640]{1,0:T(8,128)} %get-tuple-element.20), channel_id=1, source_target_pairs={{0,1},{1,0},{2,3},{3,2},{4,5},{5,4},{6,7},{7,6},{8,9},{9,8},{10,11... | collective-permute-start | bytes 307208 | tf_op jit(solution)/shard_map/ppermute | solution.py:444
  15.1 3.1 %collective-permute-start.3 = (f32[40,640]{1,0:T(8,128)}, f32[40,640]{1,0:T(8,128)S(1)}, u32[]{:S(2)}, u32[]{:S(2)}) collective-permute-start(f32[40,640]{1,0:T(8,128)} %get-tuple-element.21), channel_id=1, source_target_pairs={{1,2},{3,4},{5,6},{7,8},{9,10},{11,12},{13,14},{2,1},{4,3},{6,5},{... | collective-permute-start | bytes 307208 | tf_op jit(solution)/shard_map/ppermute | solution.py:444
  18.2 0.0 copy-done
  18.2 0.0 copy-done.1
  18.2 0.0 copy-start.3
  18.2 1.2 %copy-done.3 = s32[512,512]{1,0:T(8,128)S(1)} copy-done((s32[512,512]{1,0:T(8,128)S(1)}, s32[512,512]{1,0:T(8,128)}, u32[]{:S(2)}) %copy-start.3) | copy-done | bytes 1048600
  19.4 0.0 copy-start.10
  19.5 17.2 %interior.1 = (f32[2,512,512]{2,1,0:T(8,128)}, f32[3,512,512]{2,1,0:T(8,128)}, f32[2,8,128]{2,1,0:T(8,128)S(1)}) custom-call(f32[2,512,512]{2,1,0:T(8,128)} %vel.1, f32[3,512,512]{2,1,0:T(8,128)} %strs.1, f32[512,512]{1,0:T(8,128)S(1)} %copy-done, f32[512,512]{1,0:T(8,128)S(1)} %copy-done.1, f32[2,512,512]{2,1,0:T(8,128)} %wind.1, f32[2,512,512]{2,1,0:T(8,128)} %cur.1, ...), custom_call_target="tpu_custom_call" | custom-call | tf_op jit(solution)/shard_map/interior/pallas_call | solution.py:489
  36.7 0.0 collective-permute-done.2.ya
  36.7 0.0 collective-permute-done.3.yb
  36.8 5.3 %frame.1 = (f32[2,512,512]{2,1,0:T(8,128)}, f32[3,512,512]{2,1,0:T(8,128)}, f32[128,128]{1,0:T(8,128)S(1)}) custom-call(f32[9,16,512]{2,1,0:T(8,128)S(1)} %copy-done.9, f32[144,512]{1,0:T(8,128)S(1)} %copy-done.4, f32[144,128]{1,0:T(8,128)S(1)} %copy-done.10, f32[40,512]{1,0:T(8,128)S(1)} %copy-done.6, ...), custom_call_target="tpu_custom_call", output_to_operand_aliasing={{0}: (8, {}), {1}: (9, {})} | custom-call | tf_op jit(solution)/shard_map/frame/pallas_call | solution.py:501
  42.1 21.5 %all_to_all.9 = f32[128,1,128]{2,1,0:T(1,128)S(1)} all-to-all(f32[128,1,128]{2,1,0:T(1,128)S(1)} %bitcast.5), channel_id=1, replica_groups=mesh['gx'=8,'gy'=16] {'gx','gy'}, dimensions={0} | all-to-all | bytes 131072 | tf_op jit(solution)/shard_map/all_to_all | solution.py:519
  63.6 0.2 reduce_sum.9
  63.7 0.6 fusion
  (14 shorter events, 0.0 us)
Async XLA Ops:
  2.4 8.5 %collective-permute-start = (f32[40,512]{1,0:T(8,128)}, f32[40,512]{1,0:T(8,128)S(1)}, u32[]{:S(2)}, u32[]{:S(2)}) collective-permute-start(f32[40,512]{1,0:T(8,128)} %get-tuple-element.17), channel_id=1, source_target_pairs={{0,16},{16,0},{32,48},{48,32},{64,80},{80,64},{96,112},{112,96},{1... | collective-permute-start | bytes 245768 | tf_op jit(solution)/shard_map/ppermute | solution.py:444
  4.9 13.3 %copy-start = (f32[512,512]{1,0:T(8,128)S(1)}, f32[512,512]{1,0:T(8,128)}, u32[]{:S(2)}) copy-start(f32[512,512]{1,0:T(8,128)} %strength.1) | copy-start | bytes 3145732
  4.9 13.3 %copy-start.1 = (f32[512,512]{1,0:T(8,128)S(1)}, f32[512,512]{1,0:T(8,128)}, u32[]{:S(2)}) copy-start(f32[512,512]{1,0:T(8,128)} %mass.1) | copy-start | bytes 3145732
  4.9 13.3 %copy-start.2 = (s32[512,512]{1,0:T(8,128)S(1)}, s32[512,512]{1,0:T(8,128)}, u32[]{:S(2)}) copy-start(s32[512,512]{1,0:T(8,128)} %mask.1) | copy-start | bytes 3145732
  4.9 6.1 %collective-permute-start.1 = (f32[40,512]{1,0:T(8,128)}, f32[40,512]{1,0:T(8,128)S(1)}, u32[]{:S(2)}, u32[]{:S(2)}) collective-permute-start(f32[40,512]{1,0:T(8,128)} %get-tuple-element.18), channel_id=1, source_target_pairs={{16,32},{48,64},{80,96},{32,16},{64,48},{96,80},{17,33},{49,65},{8... | collective-permute-start | bytes 245768 | tf_op jit(solution)/shard_map/ppermute | solution.py:444
  10.9 0.6 copy-start.5
  11.5 0.7 copy-start.7
  14.1 22.6 %collective-permute-start.2 = (f32[40,640]{1,0:T(8,128)}, f32[40,640]{1,0:T(8,128)S(1)}, u32[]{:S(2)}, u32[]{:S(2)}) collective-permute-start(f32[40,640]{1,0:T(8,128)} %get-tuple-element.20), channel_id=1, source_target_pairs={{0,1},{1,0},{2,3},{3,2},{4,5},{5,4},{6,7},{7,6},{8,9},{9,8},{10,11... | collective-permute-start | bytes 307208 | tf_op jit(solution)/shard_map/ppermute | solution.py:444
  15.1 21.6 %collective-permute-start.3 = (f32[40,640]{1,0:T(8,128)}, f32[40,640]{1,0:T(8,128)S(1)}, u32[]{:S(2)}, u32[]{:S(2)}) collective-permute-start(f32[40,640]{1,0:T(8,128)} %get-tuple-element.21), channel_id=1, source_target_pairs={{1,2},{3,4},{5,6},{7,8},{9,10},{11,12},{13,14},{2,1},{4,3},{6,5},{... | collective-permute-start | bytes 307208 | tf_op jit(solution)/shard_map/ppermute | solution.py:444
  18.2 1.2 %copy-start.3 = (s32[512,512]{1,0:T(8,128)S(1)}, s32[512,512]{1,0:T(8,128)}, u32[]{:S(2)}) copy-start(s32[512,512]{1,0:T(8,128)} %openw.1) | copy-start | bytes 3145732
  19.4 17.3 %copy-start.4 = (f32[144,512]{1,0:T(8,128)S(1)}, f32[144,512]{1,0:T(8,128)}, u32[]{:S(2)}) copy-start(f32[144,512]{1,0:T(8,128)} %col_edges.1.cols) | copy-start | bytes 884740
  19.4 17.3 %copy-start.6 = (f32[40,512]{1,0:T(8,128)S(1)}, f32[40,512]{1,0:T(8,128)}, u32[]{:S(2)}) copy-start(f32[40,512]{1,0:T(8,128)} %copy-done.5) | copy-start | bytes 245764
  19.4 17.3 %copy-start.8 = (f32[40,512]{1,0:T(8,128)S(1)}, f32[40,512]{1,0:T(8,128)}, u32[]{:S(2)}) copy-start(f32[40,512]{1,0:T(8,128)} %copy-done.7) | copy-start | bytes 245764
  19.4 17.3 %copy-start.9 = (f32[9,16,512]{2,1,0:T(8,128)S(1)}, f32[9,16,512]{2,1,0:T(8,128)}, u32[]{:S(2)}) copy-start(f32[9,16,512]{2,1,0:T(8,128)} %get-tuple-element.16.own) | copy-start | bytes 884740
  19.4 17.3 %copy-start.10 = (f32[144,128]{1,0:T(8,128)S(1)}, f32[144,128]{1,0:T(8,128)}, u32[]{:S(2)}) copy-start(f32[144,128]{1,0:T(8,128)} %get-tuple-element.19.ext) | copy-start | bytes 221188
where the time goes:
time: 68.2 us; the launch traced here: 67.9 us
  Pallas kernels  31.5 us (46%)
  blocking collectives  21.5 us (32%)
  starting transfers between devices  7.28 us (11%)
  between operations  4.35 us (6%)
  local copies, waits for them, and re-layouts  3.09 us (5%)
    all_to_all x1, blocking collectives, per_device(): parts = lax.all_to_all(msg, ALL, 0, 0, tiled=True)  21.5 us
    pallas_call x1, Pallas kernels, per_device(): pl.pallas_call(functools.partial(interior_kernel, RB=32, NCH=NCH), in_spe...  17.2 us
    ppermute x4, starting transfers between devices, exchange(): return (lax.ppermute(a, axis, first), lax.ppermute(b, axis, second))  7.28 us
    pallas_call x1, Pallas kernels, per_device(): pl.pallas_call(frame_kernel, in_specs=[vmem] * 8 + [anyspace] * 2, out_sp...  5.3 us
    pallas_call x1, Pallas kernels, per_device(): pl.pallas_call(cols_kernel, grid=(R // 128,), in_specs=blocks((128, 128),...  5.24 us
    unnamed x22, local copies, waits for them, and re-layouts  2.51 us
    pallas_call x1, Pallas kernels, per_device(): pl.pallas_call(corners_kernel, in_specs=[vmem] * 3, out_specs=[vmem] * 3,...  1.93 us
    pallas_call x1, Pallas kernels, per_device(): pl.pallas_call(rows_kernel, grid=(1,), in_specs=blocks((8, C), lambda i:...  1.78 us
  transfers between devices with their start and end apart: 4, of which 0 were waited for; matrix products, arithmetic and copies ran while one was open for 0% of the time, Pallas kernels for 33%

commit v1 on v0

v1 whole, which is shorter than its diff:
```python
import functools

import jax
import jax.numpy as jnp
from jax import lax
from jax.experimental import pallas as pl
from jax.experimental.pallas import tpu as pltpu
from jax.sharding import PartitionSpec as P

ITERS = 4
RELAX = 0.8
GROW = 1.0 / (1.0 + RELAX)
KAPPA = RELAX / (1.0 + RELAX)
PAD = 8
F32 = jnp.float32
(U_, V_, H1, H2, H12, K_, M8, FU, FV, CA, CB) = range(11)
NS = 9
NF = 11
ALL = ("gx", "gy")


def weight_of(mask, openw):
    return mask.astype(F32) * (1.0 - openw.astype(F32))


def consts(strength, mass, wind, cur, weight):
    return (KAPPA * strength) * weight, mass * 8.0, 4.0 * (wind[0] + cur[0]), 4.0 * (wind[1] + cur[1])


def coefs(m8, weight):
    a = m8 * 0.25 + 1.0
    b = m8 * 0.0375
    scale = (0.25 * weight) / (a * a + b * b)
    return a * scale, b * scale


def strain(u, v, um, vm):
    su = u + um
    du = u - um
    sv = v + vm
    dv = v - vm
    return su + dv, su - dv, du + sv, du - sv


def stress_rate(alpha, beta, gamma, alpha_m, beta_m, delta_m, k):
    d = alpha - beta_m
    t = beta - alpha_m
    s = gamma + delta_m
    q = d * d + 0.25 * (t * t + s * s) + 0.01
    r = lax.rsqrt(q)
    z = k * r
    z4 = 0.25 * z
    return z * (d - q * r), z4 * t, z4 * s


def mixes(h1, h2, h12):
    e = h1 + h2
    g = h1 - h2
    return e + h12, e - h12, h12 + g, h12 - g


def drift(u, v, fx, fy, m8, fu, fv, ca, cb):
    ru = m8 * u + (fx + fu)
    rv = m8 * v + (fy + fv)
    return ca * ru + cb * rv, ca * rv - cb * ru


def pair_rows(parts, high):
    half = lax.broadcasted_iota(jnp.int32, parts[0].shape, 0) < 4
    tiles = []
    for f in range(0, NS, 2):
        a = parts[f]
        b = parts[f + 1] if f + 1 < NS else jnp.zeros_like(a)
        if high:
            tiles.append(jnp.where(half, pltpu.roll(a, 4, 0), b))
        else:
            tiles.append(jnp.where(half, a, pltpu.roll(b, 4, 0)))
    return jnp.concatenate(tiles, 0)


def unpair(tiles, f, high):
    x = tiles[8 * (f // 2) : 8 * (f // 2) + 8]
    return x if (f % 2 == 1) == high else pltpu.roll(x, 4, 0)


def is_even(axis):
    return lax.axis_index(axis) % 2 == 0


def strip_fields(vel, strs, strength, mass, wind, cur, mask, openw):
    w = weight_of(mask[...], openw[...])
    k, m8, fu, fv = consts(strength[...], mass[...], (wind[0], wind[1]), (cur[0], cur[1]), w)
    return [vel[0], vel[1], strs[0], strs[1], 2.0 * strs[2], k, m8, fu, fv]


def rows_kernel(*refs):
    own, msg_a, msg_b = refs[16:]
    top = strip_fields(*refs[:8])
    bot = strip_fields(*refs[8:16])
    for f in range(NS):
        own[f, 0:8, :] = top[f]
        own[f, 8:16, :] = bot[f]
    low = pair_rows(top, False)
    high = pair_rows(bot, True)
    even = is_even("gx")
    msg_a[...] = jnp.where(even, high, low)
    msg_b[...] = jnp.where(even, low, high)


def load_kernel(vel, strs, strength, mass, wind, cur, mask, openw, x, cols, ibuf, sem, *, NCH):
    R, C = strength.shape
    CH = R // NCH
    srcs = [(vel, 0, U_), (vel, 1, V_), (strs, 0, H1), (strs, 1, H2), (strs, 2, H12), (strength, None, K_), (mass, None, M8),
            (wind, 0, FU), (wind, 1, FV), (cur, 0, CA), (cur, 1, CB)]
    for c in range(NCH):
        rows = pl.ds(c * CH, CH)
        for ref, lead, f in srcs:
            src = ref.at[rows] if lead is None else ref.at[lead, rows]
            pltpu.make_async_copy(src, x.at[f, rows], sem.at[c]).start()
        for n, ref in enumerate((mask, openw)):
            pltpu.make_async_copy(ref.at[rows], ibuf.at[n, rows], sem.at[NCH + c]).start()
    lane = lax.broadcasted_iota(jnp.int32, (128, 128), 1)

    def prepare(r0):
        rows = pl.ds(r0, 8)
        w = weight_of(ibuf[0, rows, :], ibuf[1, rows, :])
        k, m8, fu, fv = consts(x[K_, rows, :], x[M8, rows, :], (x[FU, rows, :], x[FV, rows, :]), (x[CA, rows, :], x[CB, rows, :]), w)
        ca, cb = coefs(m8, w)
        x[H12, rows, :] = 2.0 * x[H12, rows, :]
        for f, value in ((K_, k), (M8, m8), (FU, fu), (FV, fv), (CA, ca), (CB, cb)):
            x[f, rows, :] = value

    for c in range(NCH):
        whole = x.at[:, pl.ds(c * CH, CH), :]
        pltpu.make_async_copy(whole, whole, sem.at[c]).wait()
        whole = ibuf.at[:, pl.ds(c * CH, CH), :]
        pltpu.make_async_copy(whole, whole, sem.at[NCH + c]).wait()

        def body(i, carry):
            for n in range(4):
                prepare(pl.multiple_of(i * 32 + 8 * n, 8))
            return carry

        lax.fori_loop(c * CH // 32, (c + 1) * CH // 32, body, 0)
        for p in range(c * CH // 128, (c + 1) * CH // 128):
            rows = pl.ds(p * 128, 128)
            for side in range(2):
                packed = jnp.zeros((128, 128), F32)
                for f in range(NS):
                    shift = (8 * f - 120 * side) % 128
                    y = x[f, rows, side * (C - 128) : side * (C - 128) + 128]
                    y = pltpu.roll(y, shift, 1) if shift else y
                    packed = jnp.where((lane >= 8 * f) & (lane < 8 * f + 8), y, packed)
                cols[8 * NS * side : 8 * NS * (side + 1), p * 128 : p * 128 + 128] = packed.T[0 : 8 * NS]


def corners_kernel(cols, xa, xb, ya, yb, ext):
    even = is_even("gx")
    a, b = xa[...], xb[...]
    top = jnp.where(even, b, a)
    bot = jnp.where(even, a, b)
    C = cols.shape[1]
    lane = lax.broadcasted_iota(jnp.int32, (8, 128), 1)
    strips = []
    for side in range(2):
        at = side * (C - 128)
        t = jnp.concatenate([top[:, at : at + 128], bot[:, at : at + 128], jnp.zeros((48, 128), F32)], 0).T
        t = t[120 * side : 120 * side + 8]
        own = []
        for f in range(NS):
            e = jnp.where(lane >= 124, pltpu.roll(t, 124 - 4 * f, 1), 0.0)
            e = jnp.where(lane < 4, pltpu.roll(t, 128 - 40 - 4 * f, 1), e)
            base = 8 * (NS * side + f)
            ext[base : base + 8, :] = e
            own.append(jnp.concatenate([cols[base : base + 8, :], e], 1))
        strips.append(pair_rows(own, side == 1))
    low, high = strips
    even = is_even("gy")
    ya[...] = jnp.where(even, high, low)
    yb[...] = jnp.where(even, low, high)


def interior_kernel(x_in, x, sums, al, be, ga, de, tx, ty, nx, ny, *, RB):
    R, C = x.shape[1:]
    NT = C // 128
    NB = R // RB
    LV = 3
    zero = jnp.zeros((8, 128), F32)
    for t in range(NT):
        for ref in (al, be, de):
            ref[t, 0:PAD, :] = zero
        for ref in (tx, ty):
            ref[t, PAD + R : PAD + R + 8, :] = zero
    lane = lax.broadcasted_iota(jnp.int32, (RB, 128), 1)
    row_in = lax.broadcasted_iota(jnp.int32, (RB, 128), 0)
    first = lane == 0
    last = lane == 127

    def tile(t):
        return slice(128 * t, 128 * t + 128)

    def shift_m(v):
        r = [pltpu.roll(a, 1, 1) for a in v]
        return [jnp.where(first, r[(t - 1) % NT], r[t]) for t in range(NT)]

    def shift_p(v):
        r = [pltpu.roll(a, 127, 1) for a in v]
        return [jnp.where(last, r[(t + 1) % NT], r[t]) for t in range(NT)]

    def strain_rows(r0):
        own = pl.ds(r0, RB)
        rows = pl.ds(PAD + r0, RB)
        u = [x[U_, own, tile(t)] for t in range(NT)]
        v = [x[V_, own, tile(t)] for t in range(NT)]
        um, vm = shift_m(u), shift_m(v)
        for t in range(NT):
            a, b, g, d = strain(u[t], v[t], um[t], vm[t])
            al[t, rows, :] = a
            be[t, rows, :] = b
            ga[t, rows, :] = g
            de[t, rows, :] = d

    def rate_rows(r0, final):
        own = pl.ds(r0, RB)
        rows = pl.ds(PAD + r0, RB)
        above = pl.ds(PAD + r0 - 1, RB)
        mx = []
        for t in range(NT):
            d1, d2, d12 = stress_rate(al[t, rows, :], be[t, rows, :], ga[t, rows, :], al[t, above, :], be[t, above, :], de[t, above, :], x[K_, own, tile(t)])
            h1 = x[H1, own, tile(t)] * GROW + d1
            h2 = x[H2, own, tile(t)] * GROW + d2
            h12 = x[H12, own, tile(t)] * GROW + d12
            x[H1, own, tile(t)] = h1
            x[H2, own, tile(t)] = h2
            x[H12, own, tile(t)] = 0.5 * h12 if final else h12
            mx.append(mixes(h1, h2, h12))
        up, wp, xp, yp = (shift_p([m[i] for m in mx]) for i in range(4))
        for t in range(NT):
            tx[t, rows, :] = up[t] + mx[t][1]
            nx[t, rows, :] = mx[t][0] + wp[t]
            ty[t, rows, :] = xp[t] + mx[t][3]
            ny[t, rows, :] = mx[t][2] + yp[t]

    def velocity_rows(r0, acc):
        own = pl.ds(r0, RB)
        rows = pl.ds(PAD + r0, RB)
        below = pl.ds(PAD + r0 + 1, RB)
        for t in range(NT):
            u, v, m8 = x[U_, own, tile(t)], x[V_, own, tile(t)], x[M8, own, tile(t)]
            fx = tx[t, below, :] - nx[t, rows, :]
            fy = ty[t, below, :] - ny[t, rows, :]
            nu, nv = drift(u, v, fx, fy, m8, x[FU, own, tile(t)], x[FV, own, tile(t)], x[CA, own, tile(t)], x[CB, own, tile(t)])
            x[U_, own, tile(t)] = nu
            x[V_, own, tile(t)] = nv
            if acc is not None:
                keep = (x[K_, own, tile(t)] > 0.0) & (row_in + r0 >= ITERS) & (row_in + r0 < R - ITERS)
                if t == 0:
                    keep = keep & (lane >= ITERS)
                if t == NT - 1:
                    keep = keep & (lane < 128 - ITERS)
                cu, cv = nu - u, nv - v
                acc = (acc[0] + jnp.where(keep, cu * cu + cv * cv, 0.0), acc[1] + jnp.where(keep, m8 * (nu * nu + nv * nv), 0.0))
        return acc

    zeros = (jnp.zeros((RB, 128), F32), jnp.zeros((RB, 128), F32))
    for it in range(ITERS):
        final = it == ITERS - 1
        for i in range(LV):
            strain_rows(i * RB)
            if i:
                rate_rows((i - 1) * RB, final)
            elif it:
                rate_rows((NB - 1) * RB, False)
            if it:
                velocity_rows((NB + i - LV) * RB, None)

        def body(j, acc):
            r0 = pl.multiple_of(j * RB, RB)
            strain_rows(r0)
            rate_rows(r0 - RB, final)
            return velocity_rows(r0 - LV * RB, acc if final else None) if final else (velocity_rows(r0 - LV * RB, None), acc)[1]

        acc = lax.fori_loop(LV, NB, body, zeros if final else 0)
    rate_rows((NB - 1) * RB, True)
    for i in range(LV):
        acc = velocity_rows((NB + i - LV) * RB, acc)
    for n in range(2):
        sums[n] = acc[n].reshape(RB // 8, 8, 128).sum(0)


def strip_subcycles(ref, acc_ref, rows_axis, keep):
    cols_axis = 1 - rows_axis
    back = lambda x, axis: pltpu.roll(x, 1, axis)
    ahead = lambda x, axis: pltpu.roll(x, x.shape[axis] - 1, axis)
    w = jnp.where(ref[K_] > 0.0, 1.0, 0.0)
    ca, cb = coefs(ref[M8], w)
    ref[CA] = ca
    ref[CB] = cb

    def body(_, carry):
        u, v = ref[U_], ref[V_]
        a, b, g, d = strain(u, v, back(u, cols_axis), back(v, cols_axis))
        d1, d2, d12 = stress_rate(a, b, g, back(a, rows_axis), back(b, rows_axis), back(d, rows_axis), ref[K_])
        h1 = ref[H1] * GROW + d1
        h2 = ref[H2] * GROW + d2
        h12 = ref[H12] * GROW + d12
        ref[H1] = h1
        ref[H2] = h2
        ref[H12] = h12
        up, wp, xp, yp = mixes(h1, h2, h12)
        fx = ahead(ahead(up, cols_axis) + wp, rows_axis) - (up + ahead(wp, cols_axis))
        fy = ahead(ahead(xp, cols_axis) + yp, rows_axis) - (xp + ahead(yp, cols_axis))
        m8 = ref[M8]
        nu, nv = drift(u, v, fx, fy, m8, ref[FU], ref[FV], ref[CA], ref[CB])
        ref[U_] = nu
        ref[V_] = nv
        cu, cv = nu - u, nv - v
        inside = keep & (ref[K_] > 0.0)
        acc_ref[0] = jnp.where(inside, cu * cu + cv * cv, 0.0)
        acc_ref[1] = jnp.where(inside, m8 * (nu * nu + nv * nv), 0.0)
        return carry

    lax.fori_loop(0, ITERS, body, 0)
    return [jnp.sum(acc_ref[0]), jnp.sum(acc_ref[1])]


def frame_kernel(own, cols, ext, xa, xb, ya, yb, isums, x_in, x, nvel, nstr, msg, cs, rs, cacc, racc, sem):
    R, C = nvel.shape[1:]
    outs = ((nvel, 0), (nvel, 1), (nstr, 0), (nstr, 1), (nstr, 2))
    inner = (slice(8, R - 8), slice(128, C - 128))
    sides = ((slice(0, R), slice(0, 128)), (slice(0, R), slice(C - 128, C)), (slice(0, 8), inner[1]), (slice(R - 8, R), inner[1]))

    def copies(f, where):
        ref, lead = outs[f]
        return [pltpu.make_async_copy(x.at[(f, *w)], ref.at[(lead, *w)], sem.at[f, n]) for n, w in where]

    for f in range(5):
        for cp in copies(f, [(0, inner)]):
            cp.start()
    even = is_even("gx")
    a, b = xa[...], xb[...]
    top = jnp.where(even, b, a)
    bot = jnp.where(even, a, b)
    even = is_even("gy")
    a, b = ya[...], yb[...]
    left = jnp.where(even, b, a)
    right = jnp.where(even, a, b)
    for f in range(NS):
        rs[f, 0:8, :] = unpair(top, f, True)
        rs[f, 8:16, :] = own[f, 0:8, :]
        rs[f, 16:24, :] = own[f, 8:16, :]
        rs[f, 24:32, :] = unpair(bot, f, False)
        cs[f, 0:8, :] = unpair(left, f, True)
        for side in range(2):
            base = 8 * (NS * side + f)
            cs[f, 8 + 8 * side : 16 + 8 * side, 0:R] = cols[base : base + 8, :]
            cs[f, 8 + 8 * side : 16 + 8 * side, R : R + 128] = ext[base : base + 8, :]
        cs[f, 24:32, :] = unpair(right, f, False)

    def rim(shape):
        sub = lax.broadcasted_iota(jnp.int32, shape, 0)
        return ((sub >= 8) & (sub < 12)) | ((sub >= 20) & (sub < 24)), lax.broadcasted_iota(jnp.int32, shape, 1)

    band, lane = rim(rs.shape[1:])
    row_sums = strip_subcycles(rs, racc, 0, band & (lane >= ITERS) & (lane < C - ITERS))
    band, lane = rim(cs.shape[1:])
    col_sums = strip_subcycles(cs, cacc, 1, band & (lane < R))
    lane = lax.broadcasted_iota(jnp.int32, msg.shape, 1)
    totals = [jnp.sum(isums[n]) + row_sums[n] + col_sums[n] for n in range(2)]
    msg[...] = jnp.where(lane == 0, totals[0], jnp.where(lane == 1, totals[1], 0.0))

    halves = (1.0, 1.0, 1.0, 1.0, 0.5)
    low8 = lax.broadcasted_iota(jnp.int32, (8, C), 0) < 4
    for f in range(5):
        x[f, 0:8, :] = jnp.where(low8, rs[f, 8:16, :] * halves[f], x[f, 0:8, :])
        x[f, R - 8 : R, :] = jnp.where(low8, x[f, R - 8 : R, :], rs[f, 16:24, :] * halves[f])
    lane = lax.broadcasted_iota(jnp.int32, (128, 128), 1)
    for c in range(R // 128):
        rows = slice(c * 128, c * 128 + 128)
        parts = [cs[f, 8 + 8 * side : 16 + 8 * side, rows] * halves[f] for side in range(2) for f in range(5)]
        y = jnp.concatenate(parts + [jnp.zeros((48, 128), F32)], 0).T
        for side in range(2):
            at = slice(side * (C - 128), side * (C - 128) + 128)
            for f in range(5):
                shift = (120 * side - 8 * (5 * side + f)) % 128
                z = pltpu.roll(y, shift, 1) if shift else y
                hit = lane >= 124 if side else lane < 4
                x[f, rows, at] = jnp.where(hit, z, x[f, rows, at])
    edges = list(enumerate(sides, 1))
    for f in range(5):
        for cp in copies(f, edges):
            cp.start()
    for f in range(5):
        for cp in copies(f, [(0, inner)] + edges):
            cp.wait()


def swaps(count):
    first = [(i, i ^ 1) for i in range(count)]
    second = [(i, i + 1) for i in range(1, count - 1, 2)] + [(i + 1, i) for i in range(1, count - 1, 2)]
    return first, second


def exchange(a, b, axis):
    first, second = swaps(lax.axis_size(axis))
    return lax.ppermute(a, axis, first), lax.ppermute(b, axis, second)


def sds(*shape):
    return jax.ShapeDtypeStruct(shape, F32)


def interior(x, RB=32, flags=None):
    _, R, C = x.shape
    vmem = pl.BlockSpec(memory_space=pltpu.VMEM)
    return pl.pallas_call(
        functools.partial(interior_kernel, RB=RB),
        in_specs=[vmem],
        out_specs=(vmem, vmem),
        out_shape=(sds(*x.shape), sds(2, 8, 128)),
        scratch_shapes=[pltpu.VMEM((C // 128, R + 2 * PAD, 128), F32)] * 8,
        input_output_aliases={0: 0},
        compiler_params=pltpu.CompilerParams(vmem_limit_bytes=30 * 2**20, flags=flags),
        name="interior",
    )(x)


def per_device(velocity, stress, strength, ice_mass, wind_stress, current, ice_mask, open_water):
    args = (velocity, stress, strength, ice_mass, wind_stress, current, ice_mask, open_water)
    args = tuple(pltpu.with_memory_space_constraint(v, pltpu.HBM) for v in args)
    R, C = strength.shape
    anyspace = pl.BlockSpec(memory_space=pltpu.HBM)
    vmem = pl.BlockSpec(memory_space=pltpu.VMEM)

    def limit(mib):
        return pltpu.CompilerParams(vmem_limit_bytes=mib * 2**20)

    def blocks(shape, where):
        return [pl.BlockSpec((v.shape[0],) * (v.ndim - 2) + shape, functools.partial(lambda nd, *g: (0,) * (nd - 2) + where(*g), v.ndim)) for v in args]

    own, xa, xb = pl.pallas_call(
        rows_kernel,
        grid=(1,),
        in_specs=blocks((8, C), lambda i: (0, 0)) + blocks((8, C), lambda i: (R // 8 - 1, 0)),
        out_specs=[pl.BlockSpec((NS, 16, C), lambda i: (0, 0, 0)), pl.BlockSpec((40, C), lambda i: (0, 0)), pl.BlockSpec((40, C), lambda i: (0, 0))],
        out_shape=[sds(NS, 16, C), sds(40, C), sds(40, C)],
        compiler_params=limit(6),
        name="row_edges",
    )(*args, *args)
    xa, xb = exchange(xa, xb, "gx")
    NCH = 4
    x, cols = pl.pallas_call(
        functools.partial(load_kernel, NCH=NCH),
        in_specs=[anyspace] * 8,
        out_specs=(vmem, vmem),
        out_shape=(sds(NF, R, C), sds(16 * NS, R)),
        scratch_shapes=[pltpu.VMEM((2, R, C), jnp.int32), pltpu.SemaphoreType.DMA((2 * NCH,))],
        compiler_params=limit(16),
        name="load",
    )(*args)
    ya, yb, ext = pl.pallas_call(
        corners_kernel,
        in_specs=[vmem] * 3,
        out_specs=[vmem] * 3,
        out_shape=[sds(40, R + 128), sds(40, R + 128), sds(16 * NS, 128)],
        compiler_params=limit(6),
        name="corners",
    )(cols, xa, xb)
    ya, yb = exchange(ya, yb, "gy")
    x, isums = interior(x)
    ND = lax.axis_size(ALL)
    x, nvel, nstr, msg = pl.pallas_call(
        frame_kernel,
        in_specs=[vmem] * 9,
        out_specs=(vmem, anyspace, anyspace, vmem),
        out_shape=(sds(NF, R, C), sds(2, R, C), sds(3, R, C), sds(ND, 128)),
        scratch_shapes=[
            pltpu.VMEM((NF, 32, R + 128), F32),
            pltpu.VMEM((NF, 32, C), F32),
            pltpu.VMEM((2, 32, R + 128), F32),
            pltpu.VMEM((2, 32, C), F32),
            pltpu.SemaphoreType.DMA((5, 5)),
        ],
        input_output_aliases={8: 0},
        compiler_params=limit(20),
        name="frame",
    )(own, cols, ext, xa, xb, ya, yb, isums, x)
    parts = lax.all_to_all(msg, ALL, 0, 0, tiled=True)
    total = jnp.sum(parts, axis=0)
    cells = R * lax.axis_size("gx") * C * lax.axis_size("gy")
    return nvel, nstr, total[0] / cells, total[1] * (0.0625 / cells)


def solution(mesh):
    whole, plane = P(None, "gx", "gy"), P("gx", "gy")
    return jax.shard_map(
        per_device,
        mesh=mesh,
        in_specs=(whole, whole, plane, plane, whole, whole, plane, plane),
        out_specs=(whole, whole, P(), P()),
        check_vma=False,
    )
```

time: 68.2 us -> 62.2 us (0.912)
  Pallas kernels: 31.5 us -> 28.2 us
  local copies, waits for them, and re-layouts: 3.09 us -> 0.59 us
    unnamed x22 -> x0, local copies, waits for them, and re-layouts: 2.51 us -> none
    pallas_call x1, Pallas kernels: 1.93 us -> 0.21 us  [per_device(): pl.pallas_call(corners_kernel, in_specs=[vmem] * 3, out_specs=[vmem] * 3,...]
    pallas_call x3, Pallas kernels: 27.8 us -> 27 us  [the longest x1 15.9 us: interior(): pl.pallas_call(functools.partial(interior_kernel, RB=RB), in_specs=[vmem]...]
    pallas_call x1, Pallas kernels: 1.78 us -> 1.03 us  [per_device(): pl.pallas_call(rows_kernel, grid=(1,), in_specs=blocks((8, C), lambda i:...]
  transfers between devices with their start and end apart: 4 -> 4, of which waited for: 0 -> 0; matrix products, arithmetic and copies ran while one was open for 0% -> 0% of each run, Pallas kernels for 33% -> 35%
where the time goes in v1:
time: 62.2 us; the launch traced here: 61.9 us
  Pallas kernels  28.2 us (45%)
  blocking collectives  21.4 us (34%)
  starting transfers between devices  7.33 us (12%)
  between operations  4.27 us (7%)
    all_to_all x1, blocking collectives, per_device(): parts = lax.all_to_all(msg, ALL, 0, 0, tiled=True)  21.4 us
    pallas_call x1, Pallas kernels, interior(): pl.pallas_call(functools.partial(interior_kernel, RB=RB), in_specs=[vmem]...  15.9 us
    ppermute x4, starting transfers between devices, exchange(): return (lax.ppermute(a, axis, first), lax.ppermute(b, axis, second))  7.33 us
    pallas_call x1, Pallas kernels, per_device(): pl.pallas_call(functools.partial(load_kernel, NCH=NCH), in_specs=[anyspac...  5.7 us
    pallas_call x1, Pallas kernels, per_device(): pl.pallas_call(frame_kernel, in_specs=[vmem] * 9, out_specs=(vmem, anyspa...  5.38 us
  transfers between devices with their start and end apart: 4, of which 0 were waited for; matrix products, arithmetic and copies ran while one was open for 0% of the time, Pallas kernels for 35%

profile of v1, /device:TPU:1, one launch (start us, length us, event | category | flops | bytes accessed | tf_op | source)
XLA Modules:
  0.0 61.9 jit_solution(16832285368396802246)
XLA Ops:
  0.6 1.0 %row_edges.1 = (f32[9,16,512]{2,1,0:T(8,128)S(1)}, f32[40,512]{1,0:T(8,128)S(1)}, f32[40,512]{1,0:T(8,128)S(1)}) custom-call(f32[2,512,512]{2,1,0:T(8,128)} %vel.1, f32[3,512,512]{2,1,0:T(8,128)} %strs.1, f32[512,512]{1,0:T(8,128)} %strength.1, f32[512,512]{1,0:T(8,128)} %mass.1, f32[2,512,512]{2,1,0:T(8,128)} %wind.1, f32[2,512,512]{2,1,0:T(8,128)} %cur.1, ...), custom_call_target="tpu_custom_call" | custom-call | tf_op jit(solution)/shard_map/row_edges/pallas_call | solution.py:441
  1.7 2.5 %collective-permute-start = (f32[40,512]{1,0:T(8,128)S(1)}, f32[40,512]{1,0:T(8,128)S(1)}, u32[]{:S(2)}, u32[]{:S(2)}) collective-permute-start(f32[40,512]{1,0:T(8,128)S(1)} %get-tuple-element.19), channel_id=1, source_target_pairs={{0,16},{16,0},{32,48},{48,32},{64,80},{80,64},{96,112},{112,96},{1... | collective-permute-start | bytes 245768 | tf_op jit(solution)/shard_map/ppermute | solution.py:406
  4.2 0.7 %collective-permute-start.1 = (f32[40,512]{1,0:T(8,128)S(1)}, f32[40,512]{1,0:T(8,128)S(1)}, u32[]{:S(2)}, u32[]{:S(2)}) collective-permute-start(f32[40,512]{1,0:T(8,128)S(1)} %get-tuple-element.20), channel_id=1, source_target_pairs={{16,32},{48,64},{80,96},{32,16},{64,48},{96,80},{17,33},{49,65},{8... | collective-permute-start | bytes 245768 | tf_op jit(solution)/shard_map/ppermute | solution.py:406
  4.9 5.7 %load.1 = (f32[11,512,512]{2,1,0:T(8,128)S(1)}, f32[144,512]{1,0:T(8,128)S(1)}) custom-call(f32[2,512,512]{2,1,0:T(8,128)} %vel.1, f32[3,512,512]{2,1,0:T(8,128)} %strs.1, f32[512,512]{1,0:T(8,128)} %strength.1, f32[512,512]{1,0:T(8,128)} %mass.1, f32[2,512,512]{2,1,0:T(8,128)} %wind.1, f32[2,512,512]{2,1,0:T(8,128)} %cur.1, s32[512,512]{1,0:T(8,128)} %mask.1, ...), custom_call_target="tpu_custom_call" | custom-call | tf_op jit(solution)/shard_map/load/pallas_call | solution.py:452
  10.6 0.0 collective-permute-done.xa
  10.6 0.0 collective-permute-done.1.xb
  10.6 0.2 corners.1
  10.8 1.0 %collective-permute-start.2 = (f32[40,640]{1,0:T(8,128)S(1)}, f32[40,640]{1,0:T(8,128)S(1)}, u32[]{:S(2)}, u32[]{:S(2)}) collective-permute-start(f32[40,640]{1,0:T(8,128)S(1)} %get-tuple-element.22), channel_id=1, source_target_pairs={{0,1},{1,0},{2,3},{3,2},{4,5},{5,4},{6,7},{7,6},{8,9},{9,8},{10,11... | collective-permute-start | bytes 307208 | tf_op jit(solution)/shard_map/ppermute | solution.py:406
  11.8 3.1 %collective-permute-start.3 = (f32[40,640]{1,0:T(8,128)S(1)}, f32[40,640]{1,0:T(8,128)S(1)}, u32[]{:S(2)}, u32[]{:S(2)}) collective-permute-start(f32[40,640]{1,0:T(8,128)S(1)} %get-tuple-element.23), channel_id=1, source_target_pairs={{1,2},{3,4},{5,6},{7,8},{9,10},{11,12},{13,14},{2,1},{4,3},{6,5},{... | collective-permute-start | bytes 307208 | tf_op jit(solution)/shard_map/ppermute | solution.py:406
  14.9 15.9 %interior.1 = (f32[11,512,512]{2,1,0:T(8,128)S(1)}, f32[2,8,128]{2,1,0:T(8,128)S(1)}) custom-call(f32[11,512,512]{2,1,0:T(8,128)S(1)} %get-tuple-element.24.x_in), custom_call_target="tpu_custom_call", output_to_operand_aliasing={{0}: (0, {})} | custom-call | tf_op jit(solution)/shard_map/interior/pallas_call | solution.py:416
  30.8 0.0 collective-permute-done.2.ya
  30.8 0.0 collective-permute-done.3.yb
  30.8 5.4 %frame.1 = (f32[11,512,512]{2,1,0:T(8,128)S(1)}, f32[2,512,512]{2,1,0:T(8,128)}, f32[3,512,512]{2,1,0:T(8,128)}, f32[128,128]{1,0:T(8,128)S(1)}) custom-call(f32[9,16,512]{2,1,0:T(8,128)S(1)} %get-tuple-element.17.own, f32[144,512]{1,0:T(8,128)S(1)} %get-tuple-element.18.cols, ...), custom_call_target="tpu_custom_call", output_to_operand_aliasing={{0}: (8, {})} | custom-call | tf_op jit(solution)/shard_map/frame/pallas_call | solution.py:472
  36.2 21.4 %all_to_all.9 = f32[128,1,128]{2,1,0:T(1,128)S(1)} all-to-all(f32[128,1,128]{2,1,0:T(1,128)S(1)} %bitcast.5), channel_id=1, replica_groups=mesh['gx'=8,'gy'=16] {'gx','gy'}, dimensions={0} | all-to-all | bytes 131072 | tf_op jit(solution)/shard_map/all_to_all | solution.py:488
  57.7 0.2 reduce_sum.9
  57.8 0.6 fusion
Async XLA Ops:
  1.7 8.9 %collective-permute-start = (f32[40,512]{1,0:T(8,128)S(1)}, f32[40,512]{1,0:T(8,128)S(1)}, u32[]{:S(2)}, u32[]{:S(2)}) collective-permute-start(f32[40,512]{1,0:T(8,128)S(1)} %get-tuple-element.19), channel_id=1, source_target_pairs={{0,16},{16,0},{32,48},{48,32},{64,80},{80,64},{96,112},{112,96},{1... | collective-permute-start | bytes 245768 | tf_op jit(solution)/shard_map/ppermute | solution.py:406
  4.2 6.4 %collective-permute-start.1 = (f32[40,512]{1,0:T(8,128)S(1)}, f32[40,512]{1,0:T(8,128)S(1)}, u32[]{:S(2)}, u32[]{:S(2)}) collective-permute-start(f32[40,512]{1,0:T(8,128)S(1)} %get-tuple-element.20), channel_id=1, source_target_pairs={{16,32},{48,64},{80,96},{32,16},{64,48},{96,80},{17,33},{49,65},{8... | collective-permute-start | bytes 245768 | tf_op jit(solution)/shard_map/ppermute | solution.py:406
  10.8 20.0 %collective-permute-start.2 = (f32[40,640]{1,0:T(8,128)S(1)}, f32[40,640]{1,0:T(8,128)S(1)}, u32[]{:S(2)}, u32[]{:S(2)}) collective-permute-start(f32[40,640]{1,0:T(8,128)S(1)} %get-tuple-element.22), channel_id=1, source_target_pairs={{0,1},{1,0},{2,3},{3,2},{4,5},{5,4},{6,7},{7,6},{8,9},{9,8},{10,11... | collective-permute-start | bytes 307208 | tf_op jit(solution)/shard_map/ppermute | solution.py:406
  11.8 19.0 %collective-permute-start.3 = (f32[40,640]{1,0:T(8,128)S(1)}, f32[40,640]{1,0:T(8,128)S(1)}, u32[]{:S(2)}, u32[]{:S(2)}) collective-permute-start(f32[40,640]{1,0:T(8,128)S(1)} %get-tuple-element.23), channel_id=1, source_target_pairs={{1,2},{3,4},{5,6},{7,8},{9,10},{11,12},{13,14},{2,1},{4,3},{6,5},{... | collective-permute-start | bytes 307208 | tf_op jit(solution)/shard_map/ppermute | solution.py:406

commit v2 on v1

v2 whole, which is shorter than its diff:
```python
import functools

import jax
import jax.numpy as jnp
from jax import lax
from jax.experimental import pallas as pl
from jax.experimental.pallas import tpu as pltpu
from jax.sharding import PartitionSpec as P

ITERS = 4
RELAX = 0.8
GROW = 1.0 / (1.0 + RELAX)
KAPPA = RELAX / (1.0 + RELAX)
PAD = 8
F32 = jnp.float32
(U_, V_, H1, H2, H12, K_, M8, FU, FV, CA, CB) = range(11)
NS = 9
NF = 11
ALL = ("gx", "gy")


def weight_of(mask, openw):
    return mask.astype(F32) * (1.0 - openw.astype(F32))


def consts(strength, mass, wind, cur, weight):
    return (KAPPA * strength) * weight, mass * 8.0, 4.0 * (wind[0] + cur[0]), 4.0 * (wind[1] + cur[1])


def coefs(m8, weight):
    a = m8 * 0.25 + 1.0
    b = m8 * 0.0375
    scale = (0.25 * weight) / (a * a + b * b)
    return a * scale, b * scale


def strain(u, v, um, vm):
    su = u + um
    du = u - um
    sv = v + vm
    dv = v - vm
    return su + dv, su - dv, du + sv, du - sv


def stress_rate(alpha, beta, gamma, alpha_m, beta_m, delta_m, k):
    d = alpha - beta_m
    t = beta - alpha_m
    s = gamma + delta_m
    q = d * d + 0.25 * (t * t + s * s) + 0.01
    r = lax.rsqrt(q)
    z = k * r
    z4 = 0.25 * z
    return z * (d - q * r), z4 * t, z4 * s


def mixes(h1, h2, h12):
    return h1 + h2, h1 - h2, h12


def spread(m, p):
    xs, xd = p[0] + m[0], p[2] - m[2]
    ys, yd = p[2] + m[2], p[1] - m[1]
    return xs + xd, xs - xd, ys + yd, ys - yd


def drift(u, v, fx, fy, m8, fu, fv, ca, cb):
    ru = m8 * u + (fx + fu)
    rv = m8 * v + (fy + fv)
    return ca * ru + cb * rv, ca * rv - cb * ru


def pair_rows(parts, high):
    half = lax.broadcasted_iota(jnp.int32, parts[0].shape, 0) < 4
    tiles = []
    for f in range(0, NS, 2):
        a = parts[f]
        b = parts[f + 1] if f + 1 < NS else jnp.zeros_like(a)
        if high:
            tiles.append(jnp.where(half, pltpu.roll(a, 4, 0), b))
        else:
            tiles.append(jnp.where(half, a, pltpu.roll(b, 4, 0)))
    return jnp.concatenate(tiles, 0)


def unpair(tiles, f, high):
    x = tiles[8 * (f // 2) : 8 * (f // 2) + 8]
    return x if (f % 2 == 1) == high else pltpu.roll(x, 4, 0)


def is_even(axis):
    return lax.axis_index(axis) % 2 == 0


def strip_fields(vel, strs, strength, mass, wind, cur, mask, openw):
    w = weight_of(mask[...], openw[...])
    k, m8, fu, fv = consts(strength[...], mass[...], (wind[0], wind[1]), (cur[0], cur[1]), w)
    return [vel[0], vel[1], strs[0], strs[1], 2.0 * strs[2], k, m8, fu, fv]


def rows_kernel(*refs):
    own, msg_a, msg_b = refs[16:]
    top = strip_fields(*refs[:8])
    bot = strip_fields(*refs[8:16])
    for f in range(NS):
        own[f, 0:8, :] = top[f]
        own[f, 8:16, :] = bot[f]
    low = pair_rows(top, False)
    high = pair_rows(bot, True)
    even = is_even("gx")
    msg_a[...] = jnp.where(even, high, low)
    msg_b[...] = jnp.where(even, low, high)


def load_kernel(vel, strs, strength, mass, wind, cur, mask, openw, x, cols):
    R, C = strength.shape
    lane = lax.broadcasted_iota(jnp.int32, (128, 128), 1)

    def prepare(r0):
        rows = pl.ds(r0, 8)
        for t in range(C // 128):
            at = (rows, slice(128 * t, 128 * t + 128))
            w = weight_of(mask[at], openw[at])
            k, m8, fu, fv = consts(strength[at], mass[at], (wind[(0, *at)], wind[(1, *at)]), (cur[(0, *at)], cur[(1, *at)]), w)
            ca, cb = coefs(m8, w)
            values = (vel[(0, *at)], vel[(1, *at)], strs[(0, *at)], strs[(1, *at)], 2.0 * strs[(2, *at)], k, m8, fu, fv, ca, cb)
            for f in range(NF):
                x[(f, *at)] = values[f]

    def body(i, carry):
        for n in range(4):
            prepare(pl.multiple_of(i * 32 + 8 * n, 8))
        return carry

    lax.fori_loop(0, R // 32, body, 0)

    def pack(p, side):
        rows = pl.ds(p * 128, 128)
        packed = jnp.zeros((128, 128), F32)
        for f in range(NS):
            shift = (8 * f - 120 * side) % 128
            y = x[f, rows, side * (C - 128) : side * (C - 128) + 128]
            y = pltpu.roll(y, shift, 1) if shift else y
            packed = jnp.where((lane >= 8 * f) & (lane < 8 * f + 8), y, packed)
        cols[8 * NS * side : 8 * NS * (side + 1), p * 128 : p * 128 + 128] = packed.T[0 : 8 * NS]

    for p in range(R // 128):
        for side in range(2):
            pack(p, side)


def corners_kernel(cols, xa, xb, ya, yb, ext):
    even = is_even("gx")
    a, b = xa[...], xb[...]
    top = jnp.where(even, b, a)
    bot = jnp.where(even, a, b)
    C = cols.shape[1]
    lane = lax.broadcasted_iota(jnp.int32, (8, 128), 1)
    strips = []
    for side in range(2):
        at = side * (C - 128)
        t = jnp.concatenate([top[:, at : at + 128], bot[:, at : at + 128], jnp.zeros((48, 128), F32)], 0).T
        t = t[120 * side : 120 * side + 8]
        own = []
        for f in range(NS):
            e = jnp.where(lane >= 124, pltpu.roll(t, 124 - 4 * f, 1), 0.0)
            e = jnp.where(lane < 4, pltpu.roll(t, 128 - 40 - 4 * f, 1), e)
            base = 8 * (NS * side + f)
            ext[base : base + 8, :] = e
            own.append(jnp.concatenate([cols[base : base + 8, :], e], 1))
        strips.append(pair_rows(own, side == 1))
    low, high = strips
    even = is_even("gy")
    ya[...] = jnp.where(even, high, low)
    yb[...] = jnp.where(even, low, high)


def interior_kernel(x_in, x, nvel, nstr, sums, al, be, ga, de, tx, ty, nx, ny, sem, *, RB, L1, L2):
    R, C = x.shape[1:]
    NT = C // 128
    zero = jnp.zeros((8, 128), F32)
    for t in range(NT):
        for ref in (al, be, de):
            ref[t, 0:PAD, :] = zero
        for ref in (tx, ty):
            ref[t, PAD + R : PAD + R + 8, :] = zero
    lane = lax.broadcasted_iota(jnp.int32, (8, 128), 1)
    row_in = lax.broadcasted_iota(jnp.int32, (8, 128), 0)
    first = lane == 0
    last = lane == 127

    def tile(t):
        return slice(128 * t, 128 * t + 128)

    def strain_rows(r0):
        own = pl.ds(r0, 8)
        rows = pl.ds(PAD + r0, 8)
        ru = rv = None
        for t in range(NT):
            u, v = x[U_, own, tile(t)], x[V_, own, tile(t)]
            qu, qv = pltpu.roll(u, 1, 1), pltpu.roll(v, 1, 1)
            um = jnp.where(first, ru, qu) if t else qu
            vm = jnp.where(first, rv, qv) if t else qv
            ru, rv = qu, qv
            al[t, rows, :], be[t, rows, :], ga[t, rows, :], de[t, rows, :] = strain(u, v, um, vm)

    def rate_rows(r0, final):
        own = pl.ds(r0, 8)
        rows = pl.ds(PAD + r0, 8)
        above = pl.ds(PAD + r0 - 1, 8)

        def emit(t, m, q, nq):
            p = [jnp.where(last, nq[i], q[i]) if nq else q[i] for i in range(3)]
            tx[t, rows, :], nx[t, rows, :], ty[t, rows, :], ny[t, rows, :] = spread(m, p)

        held = None
        for t in range(NT):
            d1, d2, d12 = stress_rate(al[t, rows, :], be[t, rows, :], ga[t, rows, :], al[t, above, :], be[t, above, :], de[t, above, :], x[K_, own, tile(t)])
            h1 = x[H1, own, tile(t)] * GROW + d1
            h2 = x[H2, own, tile(t)] * GROW + d2
            h12 = x[H12, own, tile(t)] * GROW + d12
            x[H1, own, tile(t)] = h1
            x[H2, own, tile(t)] = h2
            x[H12, own, tile(t)] = 0.5 * h12 if final else h12
            m = mixes(h1, h2, h12)
            q = [pltpu.roll(v, 127, 1) for v in m]
            if held:
                emit(t - 1, *held, q)
            held = (m, q)
        emit(NT - 1, *held, None)

    def velocity_rows(r0, acc):
        own = pl.ds(r0, 8)
        rows = pl.ds(PAD + r0, 8)
        below = pl.ds(PAD + r0 + 1, 8)
        for t in range(NT):
            u, v, m8 = x[U_, own, tile(t)], x[V_, own, tile(t)], x[M8, own, tile(t)]
            fx = tx[t, below, :] - nx[t, rows, :]
            fy = ty[t, below, :] - ny[t, rows, :]
            nu, nv = drift(u, v, fx, fy, m8, x[FU, own, tile(t)], x[FV, own, tile(t)], x[CA, own, tile(t)], x[CB, own, tile(t)])
            x[U_, own, tile(t)] = nu
            x[V_, own, tile(t)] = nv
            if acc is not None:
                keep = (x[K_, own, tile(t)] > 0.0) & (row_in + r0 >= ITERS) & (row_in + r0 < R - ITERS)
                if t == 0:
                    keep = keep & (lane >= ITERS)
                if t == NT - 1:
                    keep = keep & (lane < 128 - ITERS)
                cu, cv = nu - u, nv - v
                acc[2 * (t % 2)] += jnp.where(keep, cu * cu + cv * cv, 0.0)
                acc[2 * (t % 2) + 1] += jnp.where(keep, m8 * (nu * nu + nv * nv), 0.0)

    sent = [0]

    def send(end):
        rows = pl.ds(sent[0], end - sent[0])
        for f, (ref, lead) in enumerate(((nvel, 0), (nvel, 1), (nstr, 0), (nstr, 1), (nstr, 2))):
            pltpu.make_async_copy(x.at[f, rows], ref.at[lead, rows], sem).start()
        sent[0] = end

    acc = [zero] * 4
    peel = -(-L2 // RB) * RB
    for it in range(ITERS):
        final = it == ITERS - 1
        for r in range(0, peel, 8):
            strain_rows(r)
            if r >= L1:
                rate_rows(r - L1, final)
            elif it:
                rate_rows(R + r - L1, False)
            if r >= L2:
                velocity_rows(r - L2, acc if final else None)
            elif it:
                velocity_rows(R + r - L2, None)

        def body(j, acc):
            r0 = pl.multiple_of(j * RB, RB)
            acc = list(acc) if final else None
            for r in range(0, RB, 8):
                strain_rows(r0 + r)
                rate_rows(r0 + (r - L1), final)
                velocity_rows(r0 + (r - L2), acc)
            return tuple(acc) if final else ()

        if not final:
            lax.fori_loop(peel // RB, R // RB, body, ())
            continue
        for j in range(peel // RB, R // RB, 2):
            acc = list(lax.fori_loop(j, min(j + 2, R // RB), body, tuple(acc)))
            send(min((j + 2) * RB, R) - L2)
    for r in range(0, L2, 8):
        if r < L1:
            rate_rows(R + r - L1, True)
        velocity_rows(R + r - L2, acc)
        if r + 8 == L2 // 2:
            send(R - L2 // 2)
    send(R)
    sums[0] = acc[0] + acc[2]
    sums[1] = acc[1] + acc[3]
    whole = x.at[pl.ds(0, 5)]
    pltpu.make_async_copy(whole, whole, sem).wait()


def strip_subcycles(ref, acc_ref, rows_axis, keep):
    cols_axis = 1 - rows_axis
    back = lambda x, axis: pltpu.roll(x, 1, axis)
    ahead = lambda x, axis: pltpu.roll(x, x.shape[axis] - 1, axis)
    w = jnp.where(ref[K_] > 0.0, 1.0, 0.0)
    ca, cb = coefs(ref[M8], w)
    ref[CA] = ca
    ref[CB] = cb

    def body(_, carry):
        u, v = ref[U_], ref[V_]
        a, b, g, d = strain(u, v, back(u, cols_axis), back(v, cols_axis))
        d1, d2, d12 = stress_rate(a, b, g, back(a, rows_axis), back(b, rows_axis), back(d, rows_axis), ref[K_])
        h1 = ref[H1] * GROW + d1
        h2 = ref[H2] * GROW + d2
        h12 = ref[H12] * GROW + d12
        ref[H1] = h1
        ref[H2] = h2
        ref[H12] = h12
        m = mixes(h1, h2, h12)
        xt, xn, yt, yn = spread(m, [ahead(v, cols_axis) for v in m])
        fx = ahead(xt, rows_axis) - xn
        fy = ahead(yt, rows_axis) - yn
        m8 = ref[M8]
        nu, nv = drift(u, v, fx, fy, m8, ref[FU], ref[FV], ref[CA], ref[CB])
        ref[U_] = nu
        ref[V_] = nv
        cu, cv = nu - u, nv - v
        inside = keep & (ref[K_] > 0.0)
        acc_ref[0] = jnp.where(inside, cu * cu + cv * cv, 0.0)
        acc_ref[1] = jnp.where(inside, m8 * (nu * nu + nv * nv), 0.0)
        return carry

    lax.fori_loop(0, ITERS, body, 0)
    return [jnp.sum(acc_ref[0]), jnp.sum(acc_ref[1])]


def strips_kernel(own, cols, ext, xa, xb, ya, yb, isums, rows_out, cols_out, msg, rs, cs, cacc, racc, *, R, C):
    even = is_even("gx")
    a, b = xa[...], xb[...]
    top = jnp.where(even, b, a)
    bot = jnp.where(even, a, b)
    even = is_even("gy")
    a, b = ya[...], yb[...]
    left = jnp.where(even, b, a)
    right = jnp.where(even, a, b)
    for f in range(NS):
        rs[f, 0:8, :] = unpair(top, f, True)
        rs[f, 8:16, :] = own[f, 0:8, :]
        rs[f, 16:24, :] = own[f, 8:16, :]
        rs[f, 24:32, :] = unpair(bot, f, False)
        cs[f, 0:8, :] = unpair(left, f, True)
        for side in range(2):
            base = 8 * (NS * side + f)
            cs[f, 8 + 8 * side : 16 + 8 * side, 0:R] = cols[base : base + 8, :]
            cs[f, 8 + 8 * side : 16 + 8 * side, R : R + 128] = ext[base : base + 8, :]
        cs[f, 24:32, :] = unpair(right, f, False)

    def rim(shape):
        sub = lax.broadcasted_iota(jnp.int32, shape, 0)
        return ((sub >= 8) & (sub < 12)) | ((sub >= 20) & (sub < 24)), lax.broadcasted_iota(jnp.int32, shape, 1)

    band, lane = rim(rs.shape[1:])
    row_sums = strip_subcycles(rs, racc, 0, band & (lane >= ITERS) & (lane < C - ITERS))
    band, lane = rim(cs.shape[1:])
    col_sums = strip_subcycles(cs, cacc, 1, band & (lane < R))
    lane = lax.broadcasted_iota(jnp.int32, msg.shape, 1)
    totals = [jnp.sum(isums[n]) + row_sums[n] + col_sums[n] for n in range(2)]
    msg[...] = jnp.where(lane == 0, totals[0], jnp.where(lane == 1, totals[1], 0.0))
    for f in range(5):
        half = 0.5 if f == H12 else 1.0
        rows_out[f] = half * rs[f, 8:24, :]
        cols_out[f] = half * cs[f, 8:24, 0:R]


def merge_kernel(rows_in, cols_in, nvel_in, nstr_in, nvel, nstr, edge, mid, sem):
    R, C = nvel.shape[1:]
    outs = ((nvel, 0), (nvel, 1), (nstr, 0), (nstr, 1), (nstr, 2))
    inner = pl.ds(128, C - 256)

    def places(f):
        ref, lead = outs[f]
        full = ref.at[lead]
        return (
            (full.at[:, pl.ds(0, 128)], edge.at[0, f]),
            (full.at[:, pl.ds(C - 128, 128)], edge.at[1, f]),
            (full.at[pl.ds(0, 8), inner], mid.at[0, f]),
            (full.at[pl.ds(R - 8, 8), inner], mid.at[1, f]),
        )

    for f in range(5):
        for n, (there, here) in enumerate(places(f)):
            pltpu.make_async_copy(there, here, sem.at[0, n // 2]).start()
    for n, buf in enumerate((edge, mid)):
        pltpu.make_async_copy(buf, buf, sem.at[0, n]).wait()
    low = lax.broadcasted_iota(jnp.int32, (8, C), 0) < 4
    for f in range(5):
        for part in range(2):
            x = rows_in[f, 8 * part : 8 * part + 8, :]
            keep = ~low if part == 0 else low
            rows = slice(part * (R - 8), part * (R - 8) + 8)
            mid[part, f] = jnp.where(keep[:, 128 : C - 128], mid[part, f], x[:, 128 : C - 128])
            for side in range(2):
                at = slice(side * (C - 128), side * (C - 128) + 128)
                edge[side, f, rows, :] = jnp.where(keep[:, at], edge[side, f, rows, :], x[:, at])
    lane = lax.broadcasted_iota(jnp.int32, (128, 128), 1)
    for c in range(R // 128):
        rows = slice(c * 128, c * 128 + 128)
        parts = [cols_in[f, 8 * side : 8 * side + 8, rows] for side in range(2) for f in range(5)]
        x = jnp.concatenate(parts + [jnp.zeros((48, 128), F32)], 0).T
        for side in range(2):
            for f in range(5):
                shift = (120 * side - 8 * (5 * side + f)) % 128
                y = pltpu.roll(x, shift, 1) if shift else x
                hit = lane >= 124 if side else lane < 4
                edge[side, f, rows, :] = jnp.where(hit, y, edge[side, f, rows, :])
    for f in range(5):
        for n, (there, here) in enumerate(places(f)):
            pltpu.make_async_copy(here, there, sem.at[1, n // 2]).start()
    for n, buf in enumerate((edge, mid)):
        pltpu.make_async_copy(buf, buf, sem.at[1, n]).wait()


def swaps(count):
    first = [(i, i ^ 1) for i in range(count)]
    second = [(i, i + 1) for i in range(1, count - 1, 2)] + [(i + 1, i) for i in range(1, count - 1, 2)]
    return first, second


def exchange(a, b, axis):
    first, second = swaps(lax.axis_size(axis))
    return lax.ppermute(a, axis, first), lax.ppermute(b, axis, second)


def sds(*shape):
    return jax.ShapeDtypeStruct(shape, F32)


def interior(x, RB=64, L1=64, L2=128, flags=None, mib=12):
    _, R, C = x.shape
    hbm = pl.BlockSpec(memory_space=pltpu.HBM)
    vmem = pl.BlockSpec(memory_space=pltpu.VMEM)
    return pl.pallas_call(
        functools.partial(interior_kernel, RB=RB, L1=L1, L2=L2),
        in_specs=[vmem],
        out_specs=(vmem, hbm, hbm, vmem),
        out_shape=(sds(*x.shape), sds(2, R, C), sds(3, R, C), sds(2, 8, 128)),
        scratch_shapes=[pltpu.VMEM((C // 128, R + 2 * PAD, 128), F32)] * 8 + [pltpu.SemaphoreType.DMA(())],
        input_output_aliases={0: 0},
        compiler_params=pltpu.CompilerParams(vmem_limit_bytes=mib * 2**20, flags=flags),
        name="interior",
    )(x)


def per_device(velocity, stress, strength, ice_mass, wind_stress, current, ice_mask, open_water):
    args = (velocity, stress, strength, ice_mass, wind_stress, current, ice_mask, open_water)
    R, C = strength.shape
    hbm = pl.BlockSpec(memory_space=pltpu.HBM)
    vmem = pl.BlockSpec(memory_space=pltpu.VMEM)

    def limit(mib):
        return pltpu.CompilerParams(vmem_limit_bytes=mib * 2**20)

    def blocks(shape, where):
        return [pl.BlockSpec((v.shape[0],) * (v.ndim - 2) + shape, functools.partial(lambda nd, *g: (0,) * (nd - 2) + where(*g), v.ndim)) for v in args]

    edges = [pltpu.with_memory_space_constraint(v, pltpu.HBM) for v in args]
    own, xa, xb = pl.pallas_call(
        rows_kernel,
        grid=(1,),
        in_specs=blocks((8, C), lambda i: (0, 0)) + blocks((8, C), lambda i: (R // 8 - 1, 0)),
        out_specs=[pl.BlockSpec((NS, 16, C), lambda i: (0, 0, 0)), pl.BlockSpec((40, C), lambda i: (0, 0)), pl.BlockSpec((40, C), lambda i: (0, 0))],
        out_shape=[sds(NS, 16, C), sds(40, C), sds(40, C)],
        compiler_params=limit(6),
        name="row_edges",
    )(*edges, *edges)
    xa, xb, *args = lax.optimization_barrier((xa, xb, *args))
    xa, xb = exchange(xa, xb, "gx")
    x, cols = pl.pallas_call(
        load_kernel,
        in_specs=[vmem] * 8,
        out_specs=(vmem, vmem),
        out_shape=(sds(NF, R, C), sds(16 * NS, R)),
        compiler_params=limit(16),
        name="load",
    )(*args)
    ya, yb, ext = pl.pallas_call(
        corners_kernel,
        in_specs=[vmem] * 3,
        out_specs=[vmem] * 3,
        out_shape=[sds(40, R + 128), sds(40, R + 128), sds(16 * NS, 128)],
        compiler_params=limit(6),
        name="corners",
    )(cols, xa, xb)
    ya, yb = exchange(ya, yb, "gy")
    _, nvel, nstr, isums = interior(x)
    ND = lax.axis_size(ALL)
    rows_out, cols_out, msg = pl.pallas_call(
        functools.partial(strips_kernel, R=R, C=C),
        in_specs=[vmem] * 8,
        out_specs=(vmem, vmem, vmem),
        out_shape=(sds(5, 16, C), sds(5, 16, R), sds(ND, 128)),
        scratch_shapes=[
            pltpu.VMEM((NF, 32, C), F32),
            pltpu.VMEM((NF, 32, R + 128), F32),
            pltpu.VMEM((2, 32, R + 128), F32),
            pltpu.VMEM((2, 32, C), F32),
        ],
        compiler_params=limit(12),
        name="strips",
    )(own, cols, ext, xa, xb, ya, yb, isums)
    parts = lax.all_to_all(msg, ALL, 0, 0, tiled=True)
    nvel, nstr = pl.pallas_call(
        merge_kernel,
        in_specs=[vmem] * 2 + [hbm] * 2,
        out_specs=(hbm, hbm),
        out_shape=(sds(2, R, C), sds(3, R, C)),
        scratch_shapes=[pltpu.VMEM((2, 5, R, 128), F32), pltpu.VMEM((2, 5, 8, C - 256), F32), pltpu.SemaphoreType.DMA((2, 2))],
        input_output_aliases={2: 0, 3: 1},
        compiler_params=limit(12),
        name="merge",
    )(rows_out, cols_out, nvel, nstr)
    total = jnp.sum(parts, axis=0)
    cells = R * lax.axis_size("gx") * C * lax.axis_size("gy")
    return nvel, nstr, total[0] / cells, total[1] * (0.0625 / cells)


def solution(mesh):
    whole, plane = P(None, "gx", "gy"), P("gx", "gy")
    return jax.shard_map(
        per_device,
        mesh=mesh,
        in_specs=(whole, whole, plane, plane, whole, whole, plane, plane),
        out_specs=(whole, whole, P(), P()),
        check_vma=False,
    )
```

time: 62.2 us -> 56.1 us (0.902)
  blocking collectives: 21.4 us -> 0 us
  starting transfers between devices: 7.33 us -> 19.7 us
  waiting for transfers between devices: 0.01 us -> 5.69 us
  Pallas kernels: 28.2 us -> 24.7 us
    all_to_all x1 -> x0, blocking collectives: 21.4 us -> none  [per_device(): parts = lax.all_to_all(msg, ALL, 0, 0, tiled=True)]
    all_to_all x0 -> x1, starting transfers between devices: none -> 11.8 us  [per_device(): parts = lax.all_to_all(msg, ALL, 0, 0, tiled=True)]
    all_to_all x0 -> x1, waiting for transfers between devices: none -> 5.68 us  [per_device(): parts = lax.all_to_all(msg, ALL, 0, 0, tiled=True)]
    pallas_call x3 -> x4, Pallas kernels: 27 us -> 23.4 us  [the longest x1 12.6 us: interior(): pl.pallas_call(functools.partial(interior_kernel, RB=RB, L1=L1, L2=L2), i...]
    ppermute x4, starting transfers between devices: 7.33 us -> 8 us  [exchange(): return (lax.ppermute(a, axis, first), lax.ppermute(b, axis, second))]
  transfers between devices with their start and end apart: 4 -> 5, of which waited for: 0 -> 1; matrix products, arithmetic and copies ran while one was open for 0% -> 0% of each run, Pallas kernels for 35% -> 35%
where the time goes in v2:
time: 56.1 us; the launch traced here: 55.9 us
  Pallas kernels  24.7 us (44%)
  starting transfers between devices  19.7 us (35%)
  waiting for transfers between devices  5.69 us (10%)
  between operations  4.39 us (8%)
  local copies, waits for them, and re-layouts  1.18 us (2%)
    pallas_call x1, Pallas kernels, interior(): pl.pallas_call(functools.partial(interior_kernel, RB=RB, L1=L1, L2=L2), i...  12.6 us
    all_to_all x1, starting transfers between devices, per_device(): parts = lax.all_to_all(msg, ALL, 0, 0, tiled=True)  11.8 us
    ppermute x4, starting transfers between devices, exchange(): return (lax.ppermute(a, axis, first), lax.ppermute(b, axis, second))  8 us
    all_to_all x1, waiting for transfers between devices, per_device(): parts = lax.all_to_all(msg, ALL, 0, 0, tiled=True)  5.68 us
    pallas_call x1, Pallas kernels, per_device(): pl.pallas_call(merge_kernel, in_specs=[vmem] * 2 + [hbm] * 2, out_specs=(...  4.13 us
    pallas_call x1, Pallas kernels, per_device(): pl.pallas_call(functools.partial(strips_kernel, R=R, C=C), in_specs=[vmem...  3.59 us
    pallas_call x1, Pallas kernels, per_device(): pl.pallas_call(load_kernel, in_specs=[vmem] * 8, out_specs=(vmem, vmem),...  3.11 us
    pallas_call x1, Pallas kernels, per_device(): pl.pallas_call(rows_kernel, grid=(1,), in_specs=blocks((8, C), lambda i:...  1.12 us
  transfers between devices with their start and end apart: 5, of which 1 were waited for; matrix products, arithmetic and copies ran while one was open for 0% of the time, Pallas kernels for 35%

profile of v2, /device:TPU:1, one launch (start us, length us, event | category | flops | bytes accessed | tf_op | source)
XLA Modules:
  0.0 55.9 jit_solution(3480104551467956726)
XLA Ops:
  0.6 0.0 copy-start.4
  0.6 0.0 copy-start.5
  0.7 0.0 copy-start.2
  0.7 0.0 copy-start.3
  0.7 0.0 copy-start.6
  0.7 1.1 %row_edges.1 = (f32[9,16,512]{2,1,0:T(8,128)S(1)}, f32[40,512]{1,0:T(8,128)S(1)}, f32[40,512]{1,0:T(8,128)S(1)}) custom-call(f32[2,512,512]{2,1,0:T(8,128)} %vel, f32[3,512,512]{2,1,0:T(8,128)} %strs, f32[512,512]{1,0:T(8,128)} %strength, f32[512,512]{1,0:T(8,128)} %mass, f32[2,512,512]{2,1,0:T(8,128)} %wind, f32[2,512,512]{2,1,0:T(8,128)} %cur, ...), custom_call_target="tpu_custom_call" | custom-call | tf_op jit(solution)/shard_map/row_edges/pallas_call | solution.py:470
  1.8 2.5 %collective-permute-start = (f32[40,512]{1,0:T(8,128)S(1)}, f32[40,512]{1,0:T(8,128)S(1)}, u32[]{:S(2)}, u32[]{:S(2)}) collective-permute-start(f32[40,512]{1,0:T(8,128)S(1)} %get-tuple-element.42), channel_id=1, source_target_pairs={{0,16},{16,0},{32,48},{48,32},{64,80},{80,64},{96,112},{112,96},{1... | collective-permute-start | bytes 245768 | tf_op jit(solution)/shard_map/ppermute | solution.py:434
  4.4 0.8 %collective-permute-start.1 = (f32[40,512]{1,0:T(8,128)S(1)}, f32[40,512]{1,0:T(8,128)S(1)}, u32[]{:S(2)}, u32[]{:S(2)}) collective-permute-start(f32[40,512]{1,0:T(8,128)S(1)} %get-tuple-element.43), channel_id=1, source_target_pairs={{16,32},{48,64},{80,96},{32,16},{64,48},{96,80},{17,33},{49,65},{8... | collective-permute-start | bytes 245768 | tf_op jit(solution)/shard_map/ppermute | solution.py:434
  5.2 0.6 %copy-done = f32[3,512,512]{2,1,0:T(8,128)S(1)} copy-done((f32[3,512,512]{2,1,0:T(8,128)S(1)}, f32[3,512,512]{2,1,0:T(8,128)}, u32[]{:S(2)}) %copy-start) | copy-done | bytes 3145752
  5.8 3.1 %load.1 = (f32[11,512,512]{2,1,0:T(8,128)S(1)}, f32[144,512]{1,0:T(8,128)S(1)}) custom-call(f32[2,512,512]{2,1,0:T(8,128)S(1)} %copy-done.1, f32[3,512,512]{2,1,0:T(8,128)S(1)} %copy-done, f32[512,512]{1,0:T(8,128)S(1)} %copy-done.4, f32[512,512]{1,0:T(8,128)S(1)} %copy-done.5, f32[2,512,512]{2,1,0:T(8,128)S(1)} %copy-done.2, f32[2,512,512]{2,1,0:T(8,128)S(1)} %copy-done.3, ...), custom_call_target="tpu_custom_call" | custom-call | tf_op jit(solution)/shard_map/load/pallas_call | solution.py:481
  8.9 0.0 collective-permute-done.xa
  8.9 0.0 collective-permute-done.1.xb
  8.9 0.2 corners.1
  9.1 1.5 %collective-permute-start.2 = (f32[40,640]{1,0:T(8,128)S(1)}, f32[40,640]{1,0:T(8,128)S(1)}, u32[]{:S(2)}, u32[]{:S(2)}) collective-permute-start(f32[40,640]{1,0:T(8,128)S(1)} %get-tuple-element.45), channel_id=1, source_target_pairs={{0,1},{1,0},{2,3},{3,2},{4,5},{5,4},{6,7},{7,6},{8,9},{9,8},{10,11... | collective-permute-start | bytes 307208 | tf_op jit(solution)/shard_map/ppermute | solution.py:434
  10.6 3.2 %collective-permute-start.3 = (f32[40,640]{1,0:T(8,128)S(1)}, f32[40,640]{1,0:T(8,128)S(1)}, u32[]{:S(2)}, u32[]{:S(2)}) collective-permute-start(f32[40,640]{1,0:T(8,128)S(1)} %get-tuple-element.46), channel_id=1, source_target_pairs={{1,2},{3,4},{5,6},{7,8},{9,10},{11,12},{13,14},{2,1},{4,3},{6,5},{... | collective-permute-start | bytes 307208 | tf_op jit(solution)/shard_map/ppermute | solution.py:434
  13.8 12.6 %interior.1 = (f32[11,512,512]{2,1,0:T(8,128)S(1)}, f32[2,512,512]{2,1,0:T(8,128)}, f32[3,512,512]{2,1,0:T(8,128)}, f32[2,8,128]{2,1,0:T(8,128)S(1)}) custom-call(f32[11,512,512]{2,1,0:T(8,128)S(1)} %get-tuple-element.47.x_in), custom_call_target="tpu_custom_call", output_to_operand_aliasing={{0}: (0, {})} | custom-call | tf_op jit(solution)/shard_map/interior/pallas_call | solution.py:445
  26.4 0.0 collective-permute-done.2.ya
  26.4 0.0 collective-permute-done.3.yb
  26.4 3.6 %strips.1 = (f32[5,16,512]{2,1,0:T(8,128)S(1)}, f32[5,16,512]{2,1,0:T(8,128)S(1)}, f32[128,128]{1,0:T(8,128)}) custom-call(f32[9,16,512]{2,1,0:T(8,128)S(1)} %get-tuple-element.30.own, f32[144,512]{1,0:T(8,128)S(1)} %get-tuple-element.41.cols, f32[144,128]{1,0:T(8,128)S(1)} %get-tuple-element.44.ext, f32[40,512]{1,0:T(8,128)S(1)} %collective-permute-done.xa, ...), custom_call_target="tpu_custom_call" | custom-call | tf_op jit(solution)/shard_map/strips/pallas_call | solution.py:500
  30.0 11.8 %all-to-all-start = ((f32[128,1,128]{2,1,0:T(1,128)}), f32[128,1,128]{2,1,0:T(1,128)S(1)}, u32[]{:S(2)}, u32[]{:S(2)}) async-start(f32[128,1,128]{2,1,0:T(1,128)} %bitcast.1), calls=%async_computation | async-start | bytes 131072 | tf_op jit(solution)/shard_map/all_to_all | solution.py:514
  41.7 4.1 %merge.1 = (f32[2,512,512]{2,1,0:T(8,128)}, f32[3,512,512]{2,1,0:T(8,128)}) custom-call(f32[5,16,512]{2,1,0:T(8,128)S(1)} %get-tuple-element.49.rows_in, f32[5,16,512]{2,1,0:T(8,128)S(1)} %get-tuple-element.50.cols_in, f32[2,512,512]{2,1,0:T(8,128)} %get-tuple-element.51.nvel_in, ...), custom_call_target="tpu_custom_call", output_to_operand_aliasing={{0}: (2, {}), {1}: (3, {})} | custom-call | tf_op jit(solution)/shard_map/merge/pallas_call | solution.py:515
  45.9 5.7 %all-to-all-done = f32[128,1,128]{2,1,0:T(1,128)S(1)} async-done(((f32[128,1,128]{2,1,0:T(1,128)}), f32[128,1,128]{2,1,0:T(1,128)S(1)}, u32[]{:S(2)}, u32[]{:S(2)}) %all-to-all-start) | async-done | bytes 65568 | tf_op jit(solution)/shard_map/all_to_all | solution.py:514
  51.6 0.2 reduce_sum.9
  51.7 0.6 %fusion = (f32[1]{0:T(128)}, f32[1]{0:T(128)}) fusion(f32[128]{0:T(128)S(1)} %reduce_sum.9), kind=kLoop, calls=%fused_computation | loop fusion | bytes 16 | tf_op jit(solution)/shard_map/slice | solution.py:527
  (10 shorter events, 0.0 us)
Async XLA Ops:
  0.6 4.5 %copy-start.4 = (f32[512,512]{1,0:T(8,128)S(1)}, f32[512,512]{1,0:T(8,128)}, u32[]{:S(2)}) copy-start(f32[512,512]{1,0:T(8,128)} %strength) | copy-start | bytes 3145732
  0.6 4.5 %copy-start.5 = (f32[512,512]{1,0:T(8,128)S(1)}, f32[512,512]{1,0:T(8,128)}, u32[]{:S(2)}) copy-start(f32[512,512]{1,0:T(8,128)} %mass) | copy-start | bytes 3145732
  0.7 4.5 %copy-start.2 = (f32[2,512,512]{2,1,0:T(8,128)S(1)}, f32[2,512,512]{2,1,0:T(8,128)}, u32[]{:S(2)}) copy-start(f32[2,512,512]{2,1,0:T(8,128)} %wind) | copy-start | bytes 6291460
  0.7 4.5 %copy-start.3 = (f32[2,512,512]{2,1,0:T(8,128)S(1)}, f32[2,512,512]{2,1,0:T(8,128)}, u32[]{:S(2)}) copy-start(f32[2,512,512]{2,1,0:T(8,128)} %cur) | copy-start | bytes 6291460
  0.7 4.5 %copy-start.6 = (s32[512,512]{1,0:T(8,128)S(1)}, s32[512,512]{1,0:T(8,128)}, u32[]{:S(2)}) copy-start(s32[512,512]{1,0:T(8,128)} %mask) | copy-start | bytes 3145732
  0.7 4.5 %copy-start.7 = (s32[512,512]{1,0:T(8,128)S(1)}, s32[512,512]{1,0:T(8,128)}, u32[]{:S(2)}) copy-start(s32[512,512]{1,0:T(8,128)} %openw) | copy-start | bytes 3145732
  0.7 4.5 %copy-start.1 = (f32[2,512,512]{2,1,0:T(8,128)S(1)}, f32[2,512,512]{2,1,0:T(8,128)}, u32[]{:S(2)}) copy-start(f32[2,512,512]{2,1,0:T(8,128)} %vel) | copy-start | bytes 6291460
  0.7 5.1 %copy-start = (f32[3,512,512]{2,1,0:T(8,128)S(1)}, f32[3,512,512]{2,1,0:T(8,128)}, u32[]{:S(2)}) copy-start(f32[3,512,512]{2,1,0:T(8,128)} %strs) | copy-start | bytes 9437188
  1.8 7.1 %collective-permute-start = (f32[40,512]{1,0:T(8,128)S(1)}, f32[40,512]{1,0:T(8,128)S(1)}, u32[]{:S(2)}, u32[]{:S(2)}) collective-permute-start(f32[40,512]{1,0:T(8,128)S(1)} %get-tuple-element.42), channel_id=1, source_target_pairs={{0,16},{16,0},{32,48},{48,32},{64,80},{80,64},{96,112},{112,96},{1... | collective-permute-start | bytes 245768 | tf_op jit(solution)/shard_map/ppermute | solution.py:434
  4.4 4.5 %collective-permute-start.1 = (f32[40,512]{1,0:T(8,128)S(1)}, f32[40,512]{1,0:T(8,128)S(1)}, u32[]{:S(2)}, u32[]{:S(2)}) collective-permute-start(f32[40,512]{1,0:T(8,128)S(1)} %get-tuple-element.43), channel_id=1, source_target_pairs={{16,32},{48,64},{80,96},{32,16},{64,48},{96,80},{17,33},{49,65},{8... | collective-permute-start | bytes 245768 | tf_op jit(solution)/shard_map/ppermute | solution.py:434
  9.1 17.2 %collective-permute-start.2 = (f32[40,640]{1,0:T(8,128)S(1)}, f32[40,640]{1,0:T(8,128)S(1)}, u32[]{:S(2)}, u32[]{:S(2)}) collective-permute-start(f32[40,640]{1,0:T(8,128)S(1)} %get-tuple-element.45), channel_id=1, source_target_pairs={{0,1},{1,0},{2,3},{3,2},{4,5},{5,4},{6,7},{7,6},{8,9},{9,8},{10,11... | collective-permute-start | bytes 307208 | tf_op jit(solution)/shard_map/ppermute | solution.py:434
  10.6 15.8 %collective-permute-start.3 = (f32[40,640]{1,0:T(8,128)S(1)}, f32[40,640]{1,0:T(8,128)S(1)}, u32[]{:S(2)}, u32[]{:S(2)}) collective-permute-start(f32[40,640]{1,0:T(8,128)S(1)} %get-tuple-element.46), channel_id=1, source_target_pairs={{1,2},{3,4},{5,6},{7,8},{9,10},{11,12},{13,14},{2,1},{4,3},{6,5},{... | collective-permute-start | bytes 307208 | tf_op jit(solution)/shard_map/ppermute | solution.py:434
  30.0 21.6 %all-to-all-start = ((f32[128,1,128]{2,1,0:T(1,128)}), f32[128,1,128]{2,1,0:T(1,128)S(1)}, u32[]{:S(2)}, u32[]{:S(2)}) async-start(f32[128,1,128]{2,1,0:T(1,128)} %bitcast.1), calls=%async_computation | async-start | bytes 131072 | tf_op jit(solution)/shard_map/all_to_all | solution.py:514

commit v3 on v2

--- a/solution.py
+++ b/solution.py
@@ -113,7 +113,6 @@
 
 def load_kernel(vel, strs, strength, mass, wind, cur, mask, openw, x, cols):
     R, C = strength.shape
-    lane = lax.broadcasted_iota(jnp.int32, (128, 128), 1)
 
     def prepare(r0):
         rows = pl.ds(r0, 8)
@@ -122,9 +121,8 @@
             w = weight_of(mask[at], openw[at])
             k, m8, fu, fv = consts(strength[at], mass[at], (wind[(0, *at)], wind[(1, *at)]), (cur[(0, *at)], cur[(1, *at)]), w)
             ca, cb = coefs(m8, w)
-            values = (vel[(0, *at)], vel[(1, *at)], strs[(0, *at)], strs[(1, *at)], 2.0 * strs[(2, *at)], k, m8, fu, fv, ca, cb)
-            for f in range(NF):
-                x[(f, *at)] = values[f]
+            for f, value in enumerate((k, m8, fu, fv, ca, cb)):
+                x[(f, *at)] = value
 
     def body(i, carry):
         for n in range(4):
@@ -132,20 +130,36 @@
         return carry
 
     lax.fori_loop(0, R // 32, body, 0)
-
-    def pack(p, side):
-        rows = pl.ds(p * 128, 128)
-        packed = jnp.zeros((128, 128), F32)
-        for f in range(NS):
-            shift = (8 * f - 120 * side) % 128
-            y = x[f, rows, side * (C - 128) : side * (C - 128) + 128]
-            y = pltpu.roll(y, shift, 1) if shift else y
-            packed = jnp.where((lane >= 8 * f) & (lane < 8 * f + 8), y, packed)
-        cols[8 * NS * side : 8 * NS * (side + 1), p * 128 : p * 128 + 128] = packed.T[0 : 8 * NS]
-
-    for p in range(R // 128):
-        for side in range(2):
-            pack(p, side)
+    lane = lax.broadcasted_iota(jnp.int32, (8, 128), 1)
+    low = lane < 64
+    fields = [(vel, 0), (vel, 1), (strs, 0), (strs, 1), (strs, 2)] + [(x, f - K_) for f in range(K_, NS)]
+
+    def pack(p, carry):
+        groups = ([], [])
+        for g in range(16):
+            rows = pl.ds(pl.multiple_of(p * 128 + 8 * g, 8), 8)
+            packed = [None, None]
+            for f, (ref, lead) in enumerate(fields):
+                y = jnp.where(low, ref[lead, rows, 0:128], ref[lead, rows, C - 128 : C])
+                if f == H12:
+                    y = 2.0 * y
+                if f:
+                    y = pltpu.roll(y, 8 * f, 1)
+                for side in range(2):
+                    begin = 8 * (f - side) % 128
+                    hit = (lane >= begin) & (lane < begin + 8)
+                    packed[side] = y if packed[side] is None else jnp.where(hit, y, packed[side])
+            for side in range(2):
+                groups[side].append(packed[side])
+        at = pl.ds(pl.multiple_of(p * 128, 128), 128)
+        y = jnp.concatenate(groups[0], 0).T
+        cols[0 : 8 * NS, at] = y[0 : 8 * NS]
+        y = jnp.concatenate(groups[1], 0).T
+        cols[8 * NS : 8 * NS + 8, at] = y[120:128]
+        cols[8 * NS + 8 : 16 * NS, at] = y[0 : 8 * (NS - 1)]
+        return carry
+
+    lax.fori_loop(0, R // 128, pack, 0)
 
 
 def corners_kernel(cols, xa, xb, ya, yb, ext):
@@ -174,9 +188,10 @@
     yb[...] = jnp.where(even, low, high)
 
 
-def interior_kernel(x_in, x, nvel, nstr, sums, al, be, ga, de, tx, ty, nx, ny, sem, *, RB, L1, L2):
+def interior_kernel(vel, strs, con, nvel, nstr, sums, x, al, be, ga, de, tx, ty, nx, ny, sem, *, RB, L1, L2):
     R, C = x.shape[1:]
     NT = C // 128
+    k, m8_, fu_, fv_, ca_, cb_ = range(6)
     zero = jnp.zeros((8, 128), F32)
     for t in range(NT):
         for ref in (al, be, de):
@@ -191,19 +206,19 @@
     def tile(t):
         return slice(128 * t, 128 * t + 128)
 
-    def strain_rows(r0):
+    def strain_rows(r0, src):
         own = pl.ds(r0, 8)
         rows = pl.ds(PAD + r0, 8)
         ru = rv = None
         for t in range(NT):
-            u, v = x[U_, own, tile(t)], x[V_, own, tile(t)]
+            u, v = src[0, own, tile(t)], src[1, own, tile(t)]
             qu, qv = pltpu.roll(u, 1, 1), pltpu.roll(v, 1, 1)
             um = jnp.where(first, ru, qu) if t else qu
             vm = jnp.where(first, rv, qv) if t else qv
             ru, rv = qu, qv
             al[t, rows, :], be[t, rows, :], ga[t, rows, :], de[t, rows, :] = strain(u, v, um, vm)
 
-    def rate_rows(r0, final):
+    def rate_rows(r0, it):
         own = pl.ds(r0, 8)
         rows = pl.ds(PAD + r0, 8)
         above = pl.ds(PAD + r0 - 1, 8)
@@ -214,13 +229,17 @@
 
         held = None
         for t in range(NT):
-            d1, d2, d12 = stress_rate(al[t, rows, :], be[t, rows, :], ga[t, rows, :], al[t, above, :], be[t, above, :], de[t, above, :], x[K_, own, tile(t)])
-            h1 = x[H1, own, tile(t)] * GROW + d1
-            h2 = x[H2, own, tile(t)] * GROW + d2
-            h12 = x[H12, own, tile(t)] * GROW + d12
+            d1, d2, d12 = stress_rate(al[t, rows, :], be[t, rows, :], ga[t, rows, :], al[t, above, :], be[t, above, :], de[t, above, :], con[k, own, tile(t)])
+            if it:
+                old = [x[f, own, tile(t)] for f in (H1, H2, H12)]
+            else:
+                old = [strs[f, own, tile(t)] for f in range(3)]
+            h1 = old[0] * GROW + d1
+            h2 = old[1] * GROW + d2
+            h12 = old[2] * (GROW if it else 2.0 * GROW) + d12
             x[H1, own, tile(t)] = h1
             x[H2, own, tile(t)] = h2
-            x[H12, own, tile(t)] = 0.5 * h12 if final else h12
+            x[H12, own, tile(t)] = 0.5 * h12 if it == ITERS - 1 else h12
             m = mixes(h1, h2, h12)
             q = [pltpu.roll(v, 127, 1) for v in m]
             if held:
@@ -228,19 +247,19 @@
             held = (m, q)
         emit(NT - 1, *held, None)
 
-    def velocity_rows(r0, acc):
+    def velocity_rows(r0, src, acc):
         own = pl.ds(r0, 8)
         rows = pl.ds(PAD + r0, 8)
         below = pl.ds(PAD + r0 + 1, 8)
         for t in range(NT):
-            u, v, m8 = x[U_, own, tile(t)], x[V_, own, tile(t)], x[M8, own, tile(t)]
+            u, v, m8 = src[0, own, tile(t)], src[1, own, tile(t)], con[m8_, own, tile(t)]
             fx = tx[t, below, :] - nx[t, rows, :]
             fy = ty[t, below, :] - ny[t, rows, :]
-            nu, nv = drift(u, v, fx, fy, m8, x[FU, own, tile(t)], x[FV, own, tile(t)], x[CA, own, tile(t)], x[CB, own, tile(t)])
+            nu, nv = drift(u, v, fx, fy, m8, con[fu_, own, tile(t)], con[fv_, own, tile(t)], con[ca_, own, tile(t)], con[cb_, own, tile(t)])
             x[U_, own, tile(t)] = nu
             x[V_, own, tile(t)] = nv
             if acc is not None:
-                keep = (x[K_, own, tile(t)] > 0.0) & (row_in + r0 >= ITERS) & (row_in + r0 < R - ITERS)
+                keep = (con[k, own, tile(t)] > 0.0) & (row_in + r0 >= ITERS) & (row_in + r0 < R - ITERS)
                 if t == 0:
                     keep = keep & (lane >= ITERS)
                 if t == NT - 1:
@@ -261,24 +280,25 @@
     peel = -(-L2 // RB) * RB
     for it in range(ITERS):
         final = it == ITERS - 1
+        src, before = (x if n > 0 else vel for n in (it, it - 1))
         for r in range(0, peel, 8):
-            strain_rows(r)
+            strain_rows(r, src)
             if r >= L1:
-                rate_rows(r - L1, final)
+                rate_rows(r - L1, it)
             elif it:
-                rate_rows(R + r - L1, False)
+                rate_rows(R + r - L1, it - 1)
             if r >= L2:
-                velocity_rows(r - L2, acc if final else None)
+                velocity_rows(r - L2, src, acc if final else None)
             elif it:
-                velocity_rows(R + r - L2, None)
+                velocity_rows(R + r - L2, before, None)
 
         def body(j, acc):
             r0 = pl.multiple_of(j * RB, RB)
             acc = list(acc) if final else None
             for r in range(0, RB, 8):
-                strain_rows(r0 + r)
-                rate_rows(r0 + (r - L1), final)
-                velocity_rows(r0 + (r - L2), acc)
+                strain_rows(r0 + r, src)
+                rate_rows(r0 + (r - L1), it)
+                velocity_rows(r0 + (r - L2), src, acc)
             return tuple(acc) if final else ()
 
         if not final:
@@ -289,55 +309,48 @@
             send(min((j + 2) * RB, R) - L2)
     for r in range(0, L2, 8):
         if r < L1:
-            rate_rows(R + r - L1, True)
-        velocity_rows(R + r - L2, acc)
+            rate_rows(R + r - L1, ITERS - 1)
+        velocity_rows(R + r - L2, x, acc)
         if r + 8 == L2 // 2:
             send(R - L2 // 2)
     send(R)
     sums[0] = acc[0] + acc[2]
     sums[1] = acc[1] + acc[3]
-    whole = x.at[pl.ds(0, 5)]
-    pltpu.make_async_copy(whole, whole, sem).wait()
-
-
-def strip_subcycles(ref, acc_ref, rows_axis, keep):
+    pltpu.make_async_copy(x, x, sem).wait()
+
+
+def strip_begin(ref):
+    w = jnp.where(ref[K_] > 0.0, 1.0, 0.0)
+    ref[CA], ref[CB] = coefs(ref[M8], w)
+
+
+def strip_subcycle(ref, rows_axis, keep=None):
     cols_axis = 1 - rows_axis
     back = lambda x, axis: pltpu.roll(x, 1, axis)
     ahead = lambda x, axis: pltpu.roll(x, x.shape[axis] - 1, axis)
-    w = jnp.where(ref[K_] > 0.0, 1.0, 0.0)
-    ca, cb = coefs(ref[M8], w)
-    ref[CA] = ca
-    ref[CB] = cb
-
-    def body(_, carry):
-        u, v = ref[U_], ref[V_]
-        a, b, g, d = strain(u, v, back(u, cols_axis), back(v, cols_axis))
-        d1, d2, d12 = stress_rate(a, b, g, back(a, rows_axis), back(b, rows_axis), back(d, rows_axis), ref[K_])
-        h1 = ref[H1] * GROW + d1
-        h2 = ref[H2] * GROW + d2
-        h12 = ref[H12] * GROW + d12
-        ref[H1] = h1
-        ref[H2] = h2
-        ref[H12] = h12
-        m = mixes(h1, h2, h12)
-        xt, xn, yt, yn = spread(m, [ahead(v, cols_axis) for v in m])
-        fx = ahead(xt, rows_axis) - xn
-        fy = ahead(yt, rows_axis) - yn
-        m8 = ref[M8]
-        nu, nv = drift(u, v, fx, fy, m8, ref[FU], ref[FV], ref[CA], ref[CB])
-        ref[U_] = nu
-        ref[V_] = nv
-        cu, cv = nu - u, nv - v
-        inside = keep & (ref[K_] > 0.0)
-        acc_ref[0] = jnp.where(inside, cu * cu + cv * cv, 0.0)
-        acc_ref[1] = jnp.where(inside, m8 * (nu * nu + nv * nv), 0.0)
-        return carry
-
-    lax.fori_loop(0, ITERS, body, 0)
-    return [jnp.sum(acc_ref[0]), jnp.sum(acc_ref[1])]
-
-
-def strips_kernel(own, cols, ext, xa, xb, ya, yb, isums, rows_out, cols_out, msg, rs, cs, cacc, racc, *, R, C):
+    u, v = ref[U_], ref[V_]
+    a, b, g, d = strain(u, v, back(u, cols_axis), back(v, cols_axis))
+    d1, d2, d12 = stress_rate(a, b, g, back(a, rows_axis), back(b, rows_axis), back(d, rows_axis), ref[K_])
+    h1 = ref[H1] * GROW + d1
+    h2 = ref[H2] * GROW + d2
+    h12 = ref[H12] * GROW + d12
+    ref[H1], ref[H2], ref[H12] = h1, h2, h12
+    m = mixes(h1, h2, h12)
+    xt, xn, yt, yn = spread(m, [ahead(v, cols_axis) for v in m])
+    fx = ahead(xt, rows_axis) - xn
+    fy = ahead(yt, rows_axis) - yn
+    m8 = ref[M8]
+    nu, nv = drift(u, v, fx, fy, m8, ref[FU], ref[FV], ref[CA], ref[CB])
+    ref[U_], ref[V_] = nu, nv
+    if keep is None:
+        return None
+    cu, cv = nu - u, nv - v
+    inside = keep & (ref[K_] > 0.0)
+    pair = (jnp.where(inside, cu * cu + cv * cv, 0.0), jnp.where(inside, m8 * (nu * nu + nv * nv), 0.0))
+    return [sum(p[i : i + 8, j : j + 128] for i in range(0, p.shape[0], 8) for j in range(0, p.shape[1], 128)) for p in pair]
+
+
+def strips_kernel(own, cols, ext, xa, xb, ya, yb, isums, rows_out, cols_out, msg, rs, cs, *, R, C):
     even = is_even("gx")
     a, b = xa[...], xb[...]
     top = jnp.where(even, b, a)
@@ -362,12 +375,21 @@
         sub = lax.broadcasted_iota(jnp.int32, shape, 0)
         return ((sub >= 8) & (sub < 12)) | ((sub >= 20) & (sub < 24)), lax.broadcasted_iota(jnp.int32, shape, 1)
 
+    strip_begin(rs)
+    strip_begin(cs)
+
+    def body(_, carry):
+        strip_subcycle(rs, 0)
+        strip_subcycle(cs, 1)
+        return carry
+
+    lax.fori_loop(0, ITERS - 1, body, 0)
     band, lane = rim(rs.shape[1:])
-    row_sums = strip_subcycles(rs, racc, 0, band & (lane >= ITERS) & (lane < C - ITERS))
+    row_sums = strip_subcycle(rs, 0, band & (lane >= ITERS) & (lane < C - ITERS))
     band, lane = rim(cs.shape[1:])
-    col_sums = strip_subcycles(cs, cacc, 1, band & (lane < R))
+    col_sums = strip_subcycle(cs, 1, band & (lane < R))
     lane = lax.broadcasted_iota(jnp.int32, msg.shape, 1)
-    totals = [jnp.sum(isums[n]) + row_sums[n] + col_sums[n] for n in range(2)]
+    totals = [jnp.sum(isums[n] + row_sums[n] + col_sums[n]) for n in range(2)]
     msg[...] = jnp.where(lane == 0, totals[0], jnp.where(lane == 1, totals[1], 0.0))
     for f in range(5):
         half = 0.5 if f == H12 else 1.0
@@ -438,20 +460,19 @@
     return jax.ShapeDtypeStruct(shape, F32)
 
 
-def interior(x, RB=64, L1=64, L2=128, flags=None, mib=12):
-    _, R, C = x.shape
+def interior(vel, strs, con, RB=64, L1=64, L2=128, flags=None, mib=16):
+    _, R, C = con.shape
     hbm = pl.BlockSpec(memory_space=pltpu.HBM)
     vmem = pl.BlockSpec(memory_space=pltpu.VMEM)
     return pl.pallas_call(
         functools.partial(interior_kernel, RB=RB, L1=L1, L2=L2),
-        in_specs=[vmem],
-        out_specs=(vmem, hbm, hbm, vmem),
-        out_shape=(sds(*x.shape), sds(2, R, C), sds(3, R, C), sds(2, 8, 128)),
-        scratch_shapes=[pltpu.VMEM((C // 128, R + 2 * PAD, 128), F32)] * 8 + [pltpu.SemaphoreType.DMA(())],
-        input_output_aliases={0: 0},
+        in_specs=[vmem] * 3,
+        out_specs=(hbm, hbm, vmem),
+        out_shape=(sds(2, R, C), sds(3, R, C), sds(2, 8, 128)),
+        scratch_shapes=[pltpu.VMEM((5, R, C), F32)] + [pltpu.VMEM((C // 128, R + 2 * PAD, 128), F32)] * 8 + [pltpu.SemaphoreType.DMA(())],
         compiler_params=pltpu.CompilerParams(vmem_limit_bytes=mib * 2**20, flags=flags),
         name="interior",
-    )(x)
+    )(vel, strs, con)
 
 
 def per_device(velocity, stress, strength, ice_mass, wind_stress, current, ice_mask, open_water):
@@ -478,11 +499,11 @@
     )(*edges, *edges)
     xa, xb, *args = lax.optimization_barrier((xa, xb, *args))
     xa, xb = exchange(xa, xb, "gx")
-    x, cols = pl.pallas_call(
+    con, cols = pl.pallas_call(
         load_kernel,
         in_specs=[vmem] * 8,
         out_specs=(vmem, vmem),
-        out_shape=(sds(NF, R, C), sds(16 * NS, R)),
+        out_shape=(sds(6, R, C), sds(16 * NS, R)),
         compiler_params=limit(16),
         name="load",
     )(*args)
@@ -495,7 +516,7 @@
         name="corners",
     )(cols, xa, xb)
     ya, yb = exchange(ya, yb, "gy")
-    _, nvel, nstr, isums = interior(x)
+    nvel, nstr, isums = interior(args[0], args[1], con)
     ND = lax.axis_size(ALL)
     rows_out, cols_out, msg = pl.pallas_call(
         functools.partial(strips_kernel, R=R, C=C),
@@ -505,8 +526,6 @@
         scratch_shapes=[
             pltpu.VMEM((NF, 32, C), F32),
             pltpu.VMEM((NF, 32, R + 128), F32),
-            pltpu.VMEM((2, 32, R + 128), F32),
-            pltpu.VMEM((2, 32, C), F32),
         ],
         compiler_params=limit(12),
         name="strips",

time: 56.1 us -> 55.9 us (level)
  Pallas kernels: 24.7 us -> 23.6 us
  starting transfers between devices: 19.7 us -> 20.6 us
    pallas_call x1, Pallas kernels: 3.11 us -> 2.22 us  [per_device(): pl.pallas_call(load_kernel, in_specs=[vmem] * 8, out_specs=(vmem, vmem),...]
    all_to_all x1, starting transfers between devices: 11.8 us -> 12.6 us  [per_device(): parts = lax.all_to_all(msg, ALL, 0, 0, tiled=True)]
    pallas_call x1, Pallas kernels: 3.59 us -> 2.94 us  [per_device(): pl.pallas_call(functools.partial(strips_kernel, R=R, C=C), in_specs=[vmem...]
where the time goes in v3:
time: 55.9 us; the launch traced here: 55.6 us
  Pallas kernels  23.6 us (42%)
  starting transfers between devices  20.6 us (37%)
  waiting for transfers between devices  5.69 us (10%)
  between operations  4.4 us (8%)
  local copies, waits for them, and re-layouts  1.18 us (2%)
    pallas_call x1, Pallas kernels, interior(): pl.pallas_call(functools.partial(interior_kernel, RB=RB, L1=L1, L2=L2), i...  13 us
    all_to_all x1, starting transfers between devices, per_device(): parts = lax.all_to_all(msg, ALL, 0, 0, tiled=True)  12.6 us
    ppermute x4, starting transfers between devices, exchange(): return (lax.ppermute(a, axis, first), lax.ppermute(b, axis, second))  8 us
    all_to_all x1, waiting for transfers between devices, per_device(): parts = lax.all_to_all(msg, ALL, 0, 0, tiled=True)  5.68 us
    pallas_call x1, Pallas kernels, per_device(): pl.pallas_call(merge_kernel, in_specs=[vmem] * 2 + [hbm] * 2, out_specs=(...  4.13 us
    pallas_call x1, Pallas kernels, per_device(): pl.pallas_call(functools.partial(strips_kernel, R=R, C=C), in_specs=[vmem...  2.94 us
    pallas_call x1, Pallas kernels, per_device(): pl.pallas_call(load_kernel, in_specs=[vmem] * 8, out_specs=(vmem, vmem),...  2.22 us
    pallas_call x1, Pallas kernels, per_device(): pl.pallas_call(rows_kernel, grid=(1,), in_specs=blocks((8, C), lambda i:...  1.12 us
  transfers between devices with their start and end apart: 5, of which 1 were waited for; matrix products, arithmetic and copies ran while one was open for 0% of the time, Pallas kernels for 35%

profile of v3, /device:TPU:1, one launch (start us, length us, event | category | flops | bytes accessed | tf_op | source)
XLA Modules:
  0.0 55.6 jit_solution(13720521758294400128)
XLA Ops:
  0.6 0.0 copy-start.7
  0.6 0.0 copy-start.6
  0.7 0.0 copy-start.3
  0.7 0.0 copy-start.2
  0.7 0.0 copy-start.5
  0.7 1.1 %row_edges.1 = (f32[9,16,512]{2,1,0:T(8,128)S(1)}, f32[40,512]{1,0:T(8,128)S(1)}, f32[40,512]{1,0:T(8,128)S(1)}) custom-call(f32[2,512,512]{2,1,0:T(8,128)} %vel.1, f32[3,512,512]{2,1,0:T(8,128)} %strs.1, f32[512,512]{1,0:T(8,128)} %strength, f32[512,512]{1,0:T(8,128)} %mass, f32[2,512,512]{2,1,0:T(8,128)} %wind, f32[2,512,512]{2,1,0:T(8,128)} %cur, ...), custom_call_target="tpu_custom_call" | custom-call | tf_op jit(solution)/shard_map/row_edges/pallas_call | solution.py:491
  1.8 2.5 %collective-permute-start = (f32[40,512]{1,0:T(8,128)S(1)}, f32[40,512]{1,0:T(8,128)S(1)}, u32[]{:S(2)}, u32[]{:S(2)}) collective-permute-start(f32[40,512]{1,0:T(8,128)S(1)} %get-tuple-element.42), channel_id=1, source_target_pairs={{0,16},{16,0},{32,48},{48,32},{64,80},{80,64},{96,112},{112,96},{1... | collective-permute-start | bytes 245768 | tf_op jit(solution)/shard_map/ppermute | solution.py:456
  4.4 0.8 %collective-permute-start.1 = (f32[40,512]{1,0:T(8,128)S(1)}, f32[40,512]{1,0:T(8,128)S(1)}, u32[]{:S(2)}, u32[]{:S(2)}) collective-permute-start(f32[40,512]{1,0:T(8,128)S(1)} %get-tuple-element.43), channel_id=1, source_target_pairs={{16,32},{48,64},{80,96},{32,16},{64,48},{96,80},{17,33},{49,65},{8... | collective-permute-start | bytes 245768 | tf_op jit(solution)/shard_map/ppermute | solution.py:456
  5.2 0.6 %copy-done.1 = f32[2,512,512]{2,1,0:T(8,128)S(1)} copy-done((f32[2,512,512]{2,1,0:T(8,128)S(1)}, f32[2,512,512]{2,1,0:T(8,128)}, u32[]{:S(2)}) %copy-start.1) | copy-done | bytes 2097176
  5.8 2.2 %load.1 = (f32[6,512,512]{2,1,0:T(8,128)S(1)}, f32[144,512]{1,0:T(8,128)S(1)}) custom-call(f32[2,512,512]{2,1,0:T(8,128)S(1)} %copy-done.1, f32[3,512,512]{2,1,0:T(8,128)S(1)} %copy-done, f32[512,512]{1,0:T(8,128)S(1)} %copy-done.4, f32[512,512]{1,0:T(8,128)S(1)} %copy-done.5, f32[2,512,512]{2,1,0:T(8,128)S(1)} %copy-done.2, f32[2,512,512]{2,1,0:T(8,128)S(1)} %copy-done.3, ...), custom_call_target="tpu_custom_call" | custom-call | tf_op jit(solution)/shard_map/load/pallas_call | solution.py:502
  8.0 0.0 collective-permute-done.xa
  8.0 0.0 collective-permute-done.1.xb
  8.0 0.2 corners.1
  8.3 1.5 %collective-permute-start.2 = (f32[40,640]{1,0:T(8,128)S(1)}, f32[40,640]{1,0:T(8,128)S(1)}, u32[]{:S(2)}, u32[]{:S(2)}) collective-permute-start(f32[40,640]{1,0:T(8,128)S(1)} %get-tuple-element.45), channel_id=1, source_target_pairs={{0,1},{1,0},{2,3},{3,2},{4,5},{5,4},{6,7},{7,6},{8,9},{9,8},{10,11... | collective-permute-start | bytes 307208 | tf_op jit(solution)/shard_map/ppermute | solution.py:456
  9.7 3.2 %collective-permute-start.3 = (f32[40,640]{1,0:T(8,128)S(1)}, f32[40,640]{1,0:T(8,128)S(1)}, u32[]{:S(2)}, u32[]{:S(2)}) collective-permute-start(f32[40,640]{1,0:T(8,128)S(1)} %get-tuple-element.46), channel_id=1, source_target_pairs={{1,2},{3,4},{5,6},{7,8},{9,10},{11,12},{13,14},{2,1},{4,3},{6,5},{... | collective-permute-start | bytes 307208 | tf_op jit(solution)/shard_map/ppermute | solution.py:456
  12.9 13.0 %interior.1 = (f32[2,512,512]{2,1,0:T(8,128)}, f32[3,512,512]{2,1,0:T(8,128)}, f32[2,8,128]{2,1,0:T(8,128)S(1)}) custom-call(f32[2,512,512]{2,1,0:T(8,128)S(1)} %copy-done.1, f32[3,512,512]{2,1,0:T(8,128)S(1)} %copy-done, f32[6,512,512]{2,1,0:T(8,128)S(1)} %get-tuple-element.47.con), custom_call_target="tpu_custom_call" | custom-call | tf_op jit(solution)/shard_map/interior/pallas_call | solution.py:467
  25.9 0.0 collective-permute-done.2.ya
  25.9 0.0 collective-permute-done.3.yb
  25.9 2.9 %strips.1 = (f32[5,16,512]{2,1,0:T(8,128)S(1)}, f32[5,16,512]{2,1,0:T(8,128)S(1)}, f32[128,128]{1,0:T(8,128)}) custom-call(f32[9,16,512]{2,1,0:T(8,128)S(1)} %get-tuple-element.30.own, f32[144,512]{1,0:T(8,128)S(1)} %get-tuple-element.41.cols, f32[144,128]{1,0:T(8,128)S(1)} %get-tuple-element.44.ext, f32[40,512]{1,0:T(8,128)S(1)} %collective-permute-done.xa, ...), custom_call_target="tpu_custom_call" | custom-call | tf_op jit(solution)/shard_map/strips/pallas_call | solution.py:521
  28.9 12.6 %all-to-all-start = ((f32[128,1,128]{2,1,0:T(1,128)}), f32[128,1,128]{2,1,0:T(1,128)S(1)}, u32[]{:S(2)}, u32[]{:S(2)}) async-start(f32[128,1,128]{2,1,0:T(1,128)} %bitcast.1), calls=%async_computation | async-start | bytes 131072 | tf_op jit(solution)/shard_map/all_to_all | solution.py:533
  41.5 4.1 %merge.1 = (f32[2,512,512]{2,1,0:T(8,128)}, f32[3,512,512]{2,1,0:T(8,128)}) custom-call(f32[5,16,512]{2,1,0:T(8,128)S(1)} %get-tuple-element.49.rows_in, f32[5,16,512]{2,1,0:T(8,128)S(1)} %get-tuple-element.50.cols_in, f32[2,512,512]{2,1,0:T(8,128)} %get-tuple-element.51.nvel_in, ...), custom_call_target="tpu_custom_call", output_to_operand_aliasing={{0}: (2, {}), {1}: (3, {})} | custom-call | tf_op jit(solution)/shard_map/merge/pallas_call | solution.py:534
  45.6 5.7 %all-to-all-done = f32[128,1,128]{2,1,0:T(1,128)S(1)} async-done(((f32[128,1,128]{2,1,0:T(1,128)}), f32[128,1,128]{2,1,0:T(1,128)S(1)}, u32[]{:S(2)}, u32[]{:S(2)}) %all-to-all-start) | async-done | bytes 65568 | tf_op jit(solution)/shard_map/all_to_all | solution.py:533
  51.3 0.2 reduce_sum.9
  51.5 0.6 %fusion = (f32[1]{0:T(128)}, f32[1]{0:T(128)}) fusion(f32[128]{0:T(128)S(1)} %reduce_sum.9), kind=kLoop, calls=%fused_computation | loop fusion | bytes 16 | tf_op jit(solution)/shard_map/slice | solution.py:546
  (10 shorter events, 0.0 us)
Async XLA Ops:
  0.6 4.5 %copy-start.7 = (s32[512,512]{1,0:T(8,128)S(1)}, s32[512,512]{1,0:T(8,128)}, u32[]{:S(2)}) copy-start(s32[512,512]{1,0:T(8,128)} %openw) | copy-start | bytes 3145732
  0.6 4.5 %copy-start.6 = (s32[512,512]{1,0:T(8,128)S(1)}, s32[512,512]{1,0:T(8,128)}, u32[]{:S(2)}) copy-start(s32[512,512]{1,0:T(8,128)} %mask) | copy-start | bytes 3145732
  0.7 4.5 %copy-start.3 = (f32[2,512,512]{2,1,0:T(8,128)S(1)}, f32[2,512,512]{2,1,0:T(8,128)}, u32[]{:S(2)}) copy-start(f32[2,512,512]{2,1,0:T(8,128)} %cur) | copy-start | bytes 6291460
  0.7 4.5 %copy-start.2 = (f32[2,512,512]{2,1,0:T(8,128)S(1)}, f32[2,512,512]{2,1,0:T(8,128)}, u32[]{:S(2)}) copy-start(f32[2,512,512]{2,1,0:T(8,128)} %wind) | copy-start | bytes 6291460
  0.7 4.5 %copy-start.5 = (f32[512,512]{1,0:T(8,128)S(1)}, f32[512,512]{1,0:T(8,128)}, u32[]{:S(2)}) copy-start(f32[512,512]{1,0:T(8,128)} %mass) | copy-start | bytes 3145732
  0.7 4.5 %copy-start.4 = (f32[512,512]{1,0:T(8,128)S(1)}, f32[512,512]{1,0:T(8,128)}, u32[]{:S(2)}) copy-start(f32[512,512]{1,0:T(8,128)} %strength) | copy-start | bytes 3145732
  0.7 4.5 %copy-start = (f32[3,512,512]{2,1,0:T(8,128)S(1)}, f32[3,512,512]{2,1,0:T(8,128)}, u32[]{:S(2)}) copy-start(f32[3,512,512]{2,1,0:T(8,128)} %strs.1) | copy-start | bytes 9437188
  0.7 5.1 %copy-start.1 = (f32[2,512,512]{2,1,0:T(8,128)S(1)}, f32[2,512,512]{2,1,0:T(8,128)}, u32[]{:S(2)}) copy-start(f32[2,512,512]{2,1,0:T(8,128)} %vel.1) | copy-start | bytes 6291460
  1.8 6.2 %collective-permute-start = (f32[40,512]{1,0:T(8,128)S(1)}, f32[40,512]{1,0:T(8,128)S(1)}, u32[]{:S(2)}, u32[]{:S(2)}) collective-permute-start(f32[40,512]{1,0:T(8,128)S(1)} %get-tuple-element.42), channel_id=1, source_target_pairs={{0,16},{16,0},{32,48},{48,32},{64,80},{80,64},{96,112},{112,96},{1... | collective-permute-start | bytes 245768 | tf_op jit(solution)/shard_map/ppermute | solution.py:456
  4.4 3.7 %collective-permute-start.1 = (f32[40,512]{1,0:T(8,128)S(1)}, f32[40,512]{1,0:T(8,128)S(1)}, u32[]{:S(2)}, u32[]{:S(2)}) collective-permute-start(f32[40,512]{1,0:T(8,128)S(1)} %get-tuple-element.43), channel_id=1, source_target_pairs={{16,32},{48,64},{80,96},{32,16},{64,48},{96,80},{17,33},{49,65},{8... | collective-permute-start | bytes 245768 | tf_op jit(solution)/shard_map/ppermute | solution.py:456
  8.3 17.7 %collective-permute-start.2 = (f32[40,640]{1,0:T(8,128)S(1)}, f32[40,640]{1,0:T(8,128)S(1)}, u32[]{:S(2)}, u32[]{:S(2)}) collective-permute-start(f32[40,640]{1,0:T(8,128)S(1)} %get-tuple-element.45), channel_id=1, source_target_pairs={{0,1},{1,0},{2,3},{3,2},{4,5},{5,4},{6,7},{7,6},{8,9},{9,8},{10,11... | collective-permute-start | bytes 307208 | tf_op jit(solution)/shard_map/ppermute | solution.py:456
  9.7 16.2 %collective-permute-start.3 = (f32[40,640]{1,0:T(8,128)S(1)}, f32[40,640]{1,0:T(8,128)S(1)}, u32[]{:S(2)}, u32[]{:S(2)}) collective-permute-start(f32[40,640]{1,0:T(8,128)S(1)} %get-tuple-element.46), channel_id=1, source_target_pairs={{1,2},{3,4},{5,6},{7,8},{9,10},{11,12},{13,14},{2,1},{4,3},{6,5},{... | collective-permute-start | bytes 307208 | tf_op jit(solution)/shard_map/ppermute | solution.py:456
  28.9 22.5 %all-to-all-start = ((f32[128,1,128]{2,1,0:T(1,128)}), f32[128,1,128]{2,1,0:T(1,128)S(1)}, u32[]{:S(2)}, u32[]{:S(2)}) async-start(f32[128,1,128]{2,1,0:T(1,128)} %bitcast.1), calls=%async_computation | async-start | bytes 131072 | tf_op jit(solution)/shard_map/all_to_all | solution.py:533

commit v4 on v3

--- a/solution.py
+++ b/solution.py
@@ -188,7 +188,7 @@
     yb[...] = jnp.where(even, low, high)
 
 
-def interior_kernel(vel, strs, con, nvel, nstr, sums, x, al, be, ga, de, tx, ty, nx, ny, sem, *, RB, L1, L2):
+def sweep_subcycles(its, vel, strs, con, x, nvel, nstr, sums, al, be, ga, de, tx, ty, nx, ny, sem, *, RB, L1, L2):
     R, C = x.shape[1:]
     NT = C // 128
     k, m8_, fu_, fv_, ca_, cb_ = range(6)
@@ -278,18 +278,19 @@
 
     acc = [zero] * 4
     peel = -(-L2 // RB) * RB
-    for it in range(ITERS):
+    for it in its:
+        start = it == its[0]
         final = it == ITERS - 1
         src, before = (x if n > 0 else vel for n in (it, it - 1))
         for r in range(0, peel, 8):
             strain_rows(r, src)
             if r >= L1:
                 rate_rows(r - L1, it)
-            elif it:
+            elif not start:
                 rate_rows(R + r - L1, it - 1)
             if r >= L2:
                 velocity_rows(r - L2, src, acc if final else None)
-            elif it:
+            elif not start:
                 velocity_rows(R + r - L2, before, None)
 
         def body(j, acc):
@@ -309,14 +310,24 @@
             send(min((j + 2) * RB, R) - L2)
     for r in range(0, L2, 8):
         if r < L1:
-            rate_rows(R + r - L1, ITERS - 1)
-        velocity_rows(R + r - L2, x, acc)
-        if r + 8 == L2 // 2:
+            rate_rows(R + r - L1, its[-1])
+        velocity_rows(R + r - L2, src, acc if final else None)
+        if final and r + 8 == L2 // 2:
             send(R - L2 // 2)
+    if not final:
+        return
     send(R)
     sums[0] = acc[0] + acc[2]
     sums[1] = acc[1] + acc[3]
     pltpu.make_async_copy(x, x, sem).wait()
+
+
+def first_kernel(vel, strs, con, x, *work, **kw):
+    sweep_subcycles([0], vel, strs, con, x, None, None, None, *work, None, **kw)
+
+
+def rest_kernel(x_in, con, x, nvel, nstr, sums, *work, **kw):
+    sweep_subcycles(list(range(1, ITERS)), None, None, con, x, nvel, nstr, sums, *work, **kw)
 
 
 def strip_begin(ref):
@@ -460,19 +471,34 @@
     return jax.ShapeDtypeStruct(shape, F32)
 
 
-def interior(vel, strs, con, RB=64, L1=64, L2=128, flags=None, mib=16):
+def interior_first(vel, strs, con, RB=64, L1=64, L2=128):
+    _, R, C = con.shape
+    vmem = pl.BlockSpec(memory_space=pltpu.VMEM)
+    return pl.pallas_call(
+        functools.partial(first_kernel, RB=RB, L1=L1, L2=L2),
+        in_specs=[vmem] * 3,
+        out_specs=vmem,
+        out_shape=sds(5, R, C),
+        scratch_shapes=[pltpu.VMEM((C // 128, R + 2 * PAD, 128), F32)] * 8,
+        compiler_params=pltpu.CompilerParams(vmem_limit_bytes=12 * 2**20),
+        name="first",
+    )(vel, strs, con)
+
+
+def interior_rest(x, con, RB=64, L1=64, L2=128):
     _, R, C = con.shape
     hbm = pl.BlockSpec(memory_space=pltpu.HBM)
     vmem = pl.BlockSpec(memory_space=pltpu.VMEM)
     return pl.pallas_call(
-        functools.partial(interior_kernel, RB=RB, L1=L1, L2=L2),
-        in_specs=[vmem] * 3,
-        out_specs=(hbm, hbm, vmem),
-        out_shape=(sds(2, R, C), sds(3, R, C), sds(2, 8, 128)),
-        scratch_shapes=[pltpu.VMEM((5, R, C), F32)] + [pltpu.VMEM((C // 128, R + 2 * PAD, 128), F32)] * 8 + [pltpu.SemaphoreType.DMA(())],
-        compiler_params=pltpu.CompilerParams(vmem_limit_bytes=mib * 2**20, flags=flags),
-        name="interior",
-    )(vel, strs, con)
+        functools.partial(rest_kernel, RB=RB, L1=L1, L2=L2),
+        in_specs=[vmem] * 2,
+        out_specs=(vmem, hbm, hbm, vmem),
+        out_shape=(sds(5, R, C), sds(2, R, C), sds(3, R, C), sds(2, 8, 128)),
+        scratch_shapes=[pltpu.VMEM((C // 128, R + 2 * PAD, 128), F32)] * 8 + [pltpu.SemaphoreType.DMA(())],
+        input_output_aliases={0: 0},
+        compiler_params=pltpu.CompilerParams(vmem_limit_bytes=12 * 2**20),
+        name="rest",
+    )(x, con)
 
 
 def per_device(velocity, stress, strength, ice_mass, wind_stress, current, ice_mask, open_water):
@@ -507,6 +533,8 @@
         compiler_params=limit(16),
         name="load",
     )(*args)
+    x = interior_first(args[0], args[1], con)
+    cols, x = lax.optimization_barrier((cols, x))
     ya, yb, ext = pl.pallas_call(
         corners_kernel,
         in_specs=[vmem] * 3,
@@ -516,7 +544,7 @@
         name="corners",
     )(cols, xa, xb)
     ya, yb = exchange(ya, yb, "gy")
-    nvel, nstr, isums = interior(args[0], args[1], con)
+    _, nvel, nstr, isums = interior_rest(x, con)
     ND = lax.axis_size(ALL)
     rows_out, cols_out, msg = pl.pallas_call(
         functools.partial(strips_kernel, R=R, C=C),

time: 55.9 us -> 54.1 us (0.968)
  starting transfers between devices: 20.6 us -> 18.8 us
    all_to_all x1, starting transfers between devices: 12.6 us -> 10.8 us  [per_device(): parts = lax.all_to_all(msg, ALL, 0, 0, tiled=True)]
    pallas_call x1 -> x2, Pallas kernels: 13 us -> 12.9 us  [the longest x1 10.1 us: interior_rest(): pl.pallas_call(functools.partial(rest_kernel, RB=RB, L1=L1, L2=L2), in_sp...]
  transfers between devices with their start and end apart: 5 -> 5, of which waited for: 1 -> 1; matrix products, arithmetic and copies ran while one was open for 0% -> 0% of each run, Pallas kernels for 35% -> 36%
where the time goes in v4:
time: 54.1 us; the launch traced here: 53.8 us
  Pallas kernels  23.5 us (43%)
  starting transfers between devices  18.8 us (35%)
  waiting for transfers between devices  5.69 us (11%)
  between operations  4.4 us (8%)
  local copies, waits for them, and re-layouts  1.18 us (2%)
    all_to_all x1, starting transfers between devices, per_device(): parts = lax.all_to_all(msg, ALL, 0, 0, tiled=True)  10.8 us
    pallas_call x1, Pallas kernels, interior_rest(): pl.pallas_call(functools.partial(rest_kernel, RB=RB, L1=L1, L2=L2), in_sp...  10.1 us
    ppermute x4, starting transfers between devices, exchange(): return (lax.ppermute(a, axis, first), lax.ppermute(b, axis, second))  8 us
    all_to_all x1, waiting for transfers between devices, per_device(): parts = lax.all_to_all(msg, ALL, 0, 0, tiled=True)  5.68 us
    pallas_call x1, Pallas kernels, per_device(): pl.pallas_call(merge_kernel, in_specs=[vmem] * 2 + [hbm] * 2, out_specs=(...  4.13 us
    pallas_call x1, Pallas kernels, per_device(): pl.pallas_call(functools.partial(strips_kernel, R=R, C=C), in_specs=[vmem...  2.94 us
    pallas_call x1, Pallas kernels, interior_first(): pl.pallas_call(functools.partial(first_kernel, RB=RB, L1=L1, L2=L2), in_s...  2.79 us
    pallas_call x1, Pallas kernels, per_device(): pl.pallas_call(load_kernel, in_specs=[vmem] * 8, out_specs=(vmem, vmem),...  2.22 us
  transfers between devices with their start and end apart: 5, of which 1 were waited for; matrix products, arithmetic and copies ran while one was open for 0% of the time, Pallas kernels for 36%

profile of v4, /device:TPU:1, one launch (start us, length us, event | category | flops | bytes accessed | tf_op | source)
XLA Modules:
  0.0 53.8 jit_solution(13434955790478510983)
XLA Ops:
  0.6 0.0 copy-start.7
  0.6 0.0 copy-start.6
  0.7 0.0 copy-start.3
  0.7 0.0 copy-start.2
  0.7 1.1 %row_edges.1 = (f32[9,16,512]{2,1,0:T(8,128)S(1)}, f32[40,512]{1,0:T(8,128)S(1)}, f32[40,512]{1,0:T(8,128)S(1)}) custom-call(f32[2,512,512]{2,1,0:T(8,128)} %vel.1, f32[3,512,512]{2,1,0:T(8,128)} %strs.1, f32[512,512]{1,0:T(8,128)} %strength, f32[512,512]{1,0:T(8,128)} %mass, f32[2,512,512]{2,1,0:T(8,128)} %wind, f32[2,512,512]{2,1,0:T(8,128)} %cur, ...), custom_call_target="tpu_custom_call" | custom-call | tf_op jit(solution)/shard_map/row_edges/pallas_call | solution.py:517
  1.8 2.5 %collective-permute-start = (f32[40,512]{1,0:T(8,128)S(1)}, f32[40,512]{1,0:T(8,128)S(1)}, u32[]{:S(2)}, u32[]{:S(2)}) collective-permute-start(f32[40,512]{1,0:T(8,128)S(1)} %get-tuple-element.46), channel_id=1, source_target_pairs={{0,16},{16,0},{32,48},{48,32},{64,80},{80,64},{96,112},{112,96},{1... | collective-permute-start | bytes 245768 | tf_op jit(solution)/shard_map/ppermute | solution.py:467
  4.4 0.8 %collective-permute-start.1 = (f32[40,512]{1,0:T(8,128)S(1)}, f32[40,512]{1,0:T(8,128)S(1)}, u32[]{:S(2)}, u32[]{:S(2)}) collective-permute-start(f32[40,512]{1,0:T(8,128)S(1)} %get-tuple-element.47), channel_id=1, source_target_pairs={{16,32},{48,64},{80,96},{32,16},{64,48},{96,80},{17,33},{49,65},{8... | collective-permute-start | bytes 245768 | tf_op jit(solution)/shard_map/ppermute | solution.py:467
  5.2 0.6 %copy-done.1 = f32[2,512,512]{2,1,0:T(8,128)S(1)} copy-done((f32[2,512,512]{2,1,0:T(8,128)S(1)}, f32[2,512,512]{2,1,0:T(8,128)}, u32[]{:S(2)}) %copy-start.1) | copy-done | bytes 2097176
  5.8 2.2 %load.1 = (f32[6,512,512]{2,1,0:T(8,128)S(1)}, f32[144,512]{1,0:T(8,128)S(1)}) custom-call(f32[2,512,512]{2,1,0:T(8,128)S(1)} %copy-done.1, f32[3,512,512]{2,1,0:T(8,128)S(1)} %copy-done, f32[512,512]{1,0:T(8,128)S(1)} %copy-done.4, f32[512,512]{1,0:T(8,128)S(1)} %copy-done.5, f32[2,512,512]{2,1,0:T(8,128)S(1)} %copy-done.2, f32[2,512,512]{2,1,0:T(8,128)S(1)} %copy-done.3, ...), custom_call_target="tpu_custom_call" | custom-call | tf_op jit(solution)/shard_map/load/pallas_call | solution.py:528
  8.0 2.8 %first.1.x_in = f32[5,512,512]{2,1,0:T(8,128)S(1)} custom-call(f32[2,512,512]{2,1,0:T(8,128)S(1)} %copy-done.1, f32[3,512,512]{2,1,0:T(8,128)S(1)} %copy-done, f32[6,512,512]{2,1,0:T(8,128)S(1)} %get-tuple-element.44.con), custom_call_target="tpu_custom_call" | custom-call | tf_op jit(solution)/shard_map/first/pallas_call | solution.py:477
  10.8 0.0 collective-permute-done.xa
  10.8 0.0 collective-permute-done.1.xb
  10.8 0.2 corners.1
  11.1 1.5 %collective-permute-start.2 = (f32[40,640]{1,0:T(8,128)S(1)}, f32[40,640]{1,0:T(8,128)S(1)}, u32[]{:S(2)}, u32[]{:S(2)}) collective-permute-start(f32[40,640]{1,0:T(8,128)S(1)} %get-tuple-element.49), channel_id=1, source_target_pairs={{0,1},{1,0},{2,3},{3,2},{4,5},{5,4},{6,7},{7,6},{8,9},{9,8},{10,11... | collective-permute-start | bytes 307208 | tf_op jit(solution)/shard_map/ppermute | solution.py:467
  12.5 3.2 %collective-permute-start.3 = (f32[40,640]{1,0:T(8,128)S(1)}, f32[40,640]{1,0:T(8,128)S(1)}, u32[]{:S(2)}, u32[]{:S(2)}) collective-permute-start(f32[40,640]{1,0:T(8,128)S(1)} %get-tuple-element.50), channel_id=1, source_target_pairs={{1,2},{3,4},{5,6},{7,8},{9,10},{11,12},{13,14},{2,1},{4,3},{6,5},{... | collective-permute-start | bytes 307208 | tf_op jit(solution)/shard_map/ppermute | solution.py:467
  15.7 10.1 %rest.1 = (f32[5,512,512]{2,1,0:T(8,128)S(1)}, f32[2,512,512]{2,1,0:T(8,128)}, f32[3,512,512]{2,1,0:T(8,128)}, f32[2,8,128]{2,1,0:T(8,128)S(1)}) custom-call(f32[5,512,512]{2,1,0:T(8,128)S(1)} %first.1.x_in, f32[6,512,512]{2,1,0:T(8,128)S(1)} %get-tuple-element.44.con), custom_call_target="tpu_custom_call", output_to_operand_aliasing={{0}: (0, {})} | custom-call | tf_op jit(solution)/shard_map/rest/pallas_call | solution.py:492
  25.9 0.0 collective-permute-done.2.ya
  25.9 0.0 collective-permute-done.3.yb
  25.9 2.9 %strips.1 = (f32[5,16,512]{2,1,0:T(8,128)S(1)}, f32[5,16,512]{2,1,0:T(8,128)S(1)}, f32[128,128]{1,0:T(8,128)}) custom-call(f32[9,16,512]{2,1,0:T(8,128)S(1)} %get-tuple-element.32.own, f32[144,512]{1,0:T(8,128)S(1)} %get-tuple-element.45.cols, f32[144,128]{1,0:T(8,128)S(1)} %get-tuple-element.48.ext, f32[40,512]{1,0:T(8,128)S(1)} %collective-permute-done.xa, ...), custom_call_target="tpu_custom_call" | custom-call | tf_op jit(solution)/shard_map/strips/pallas_call | solution.py:549
  28.8 10.8 %all-to-all-start = ((f32[128,1,128]{2,1,0:T(1,128)}), f32[128,1,128]{2,1,0:T(1,128)S(1)}, u32[]{:S(2)}, u32[]{:S(2)}) async-start(f32[128,1,128]{2,1,0:T(1,128)} %bitcast.1), calls=%async_computation | async-start | bytes 131072 | tf_op jit(solution)/shard_map/all_to_all | solution.py:561
  39.7 4.1 %merge.1 = (f32[2,512,512]{2,1,0:T(8,128)}, f32[3,512,512]{2,1,0:T(8,128)}) custom-call(f32[5,16,512]{2,1,0:T(8,128)S(1)} %get-tuple-element.53.rows_in, f32[5,16,512]{2,1,0:T(8,128)S(1)} %get-tuple-element.54.cols_in, f32[2,512,512]{2,1,0:T(8,128)} %get-tuple-element.55.nvel_in, ...), custom_call_target="tpu_custom_call", output_to_operand_aliasing={{0}: (2, {}), {1}: (3, {})} | custom-call | tf_op jit(solution)/shard_map/merge/pallas_call | solution.py:562
  43.8 5.7 %all-to-all-done = f32[128,1,128]{2,1,0:T(1,128)S(1)} async-done(((f32[128,1,128]{2,1,0:T(1,128)}), f32[128,1,128]{2,1,0:T(1,128)S(1)}, u32[]{:S(2)}, u32[]{:S(2)}) %all-to-all-start) | async-done | bytes 65568 | tf_op jit(solution)/shard_map/all_to_all | solution.py:561
  49.5 0.2 reduce_sum.9
  49.7 0.6 %fusion = (f32[1]{0:T(128)}, f32[1]{0:T(128)}) fusion(f32[128]{0:T(128)S(1)} %reduce_sum.9), kind=kLoop, calls=%fused_computation | loop fusion | bytes 16 | tf_op jit(solution)/shard_map/slice | solution.py:574
  (11 shorter events, 0.0 us)
Async XLA Ops:
  0.6 4.5 %copy-start.7 = (s32[512,512]{1,0:T(8,128)S(1)}, s32[512,512]{1,0:T(8,128)}, u32[]{:S(2)}) copy-start(s32[512,512]{1,0:T(8,128)} %openw) | copy-start | bytes 3145732
  0.6 4.5 %copy-start.6 = (s32[512,512]{1,0:T(8,128)S(1)}, s32[512,512]{1,0:T(8,128)}, u32[]{:S(2)}) copy-start(s32[512,512]{1,0:T(8,128)} %mask) | copy-start | bytes 3145732
  0.7 4.5 %copy-start.3 = (f32[2,512,512]{2,1,0:T(8,128)S(1)}, f32[2,512,512]{2,1,0:T(8,128)}, u32[]{:S(2)}) copy-start(f32[2,512,512]{2,1,0:T(8,128)} %cur) | copy-start | bytes 6291460
  0.7 4.5 %copy-start.2 = (f32[2,512,512]{2,1,0:T(8,128)S(1)}, f32[2,512,512]{2,1,0:T(8,128)}, u32[]{:S(2)}) copy-start(f32[2,512,512]{2,1,0:T(8,128)} %wind) | copy-start | bytes 6291460
  0.7 4.5 %copy-start.5 = (f32[512,512]{1,0:T(8,128)S(1)}, f32[512,512]{1,0:T(8,128)}, u32[]{:S(2)}) copy-start(f32[512,512]{1,0:T(8,128)} %mass) | copy-start | bytes 3145732
  0.7 4.5 %copy-start.4 = (f32[512,512]{1,0:T(8,128)S(1)}, f32[512,512]{1,0:T(8,128)}, u32[]{:S(2)}) copy-start(f32[512,512]{1,0:T(8,128)} %strength) | copy-start | bytes 3145732
  0.7 4.5 %copy-start = (f32[3,512,512]{2,1,0:T(8,128)S(1)}, f32[3,512,512]{2,1,0:T(8,128)}, u32[]{:S(2)}) copy-start(f32[3,512,512]{2,1,0:T(8,128)} %strs.1) | copy-start | bytes 9437188
  0.7 5.1 %copy-start.1 = (f32[2,512,512]{2,1,0:T(8,128)S(1)}, f32[2,512,512]{2,1,0:T(8,128)}, u32[]{:S(2)}) copy-start(f32[2,512,512]{2,1,0:T(8,128)} %vel.1) | copy-start | bytes 6291460
  1.8 9.0 %collective-permute-start = (f32[40,512]{1,0:T(8,128)S(1)}, f32[40,512]{1,0:T(8,128)S(1)}, u32[]{:S(2)}, u32[]{:S(2)}) collective-permute-start(f32[40,512]{1,0:T(8,128)S(1)} %get-tuple-element.46), channel_id=1, source_target_pairs={{0,16},{16,0},{32,48},{48,32},{64,80},{80,64},{96,112},{112,96},{1... | collective-permute-start | bytes 245768 | tf_op jit(solution)/shard_map/ppermute | solution.py:467
  4.4 6.5 %collective-permute-start.1 = (f32[40,512]{1,0:T(8,128)S(1)}, f32[40,512]{1,0:T(8,128)S(1)}, u32[]{:S(2)}, u32[]{:S(2)}) collective-permute-start(f32[40,512]{1,0:T(8,128)S(1)} %get-tuple-element.47), channel_id=1, source_target_pairs={{16,32},{48,64},{80,96},{32,16},{64,48},{96,80},{17,33},{49,65},{8... | collective-permute-start | bytes 245768 | tf_op jit(solution)/shard_map/ppermute | solution.py:467
  11.1 14.8 %collective-permute-start.2 = (f32[40,640]{1,0:T(8,128)S(1)}, f32[40,640]{1,0:T(8,128)S(1)}, u32[]{:S(2)}, u32[]{:S(2)}) collective-permute-start(f32[40,640]{1,0:T(8,128)S(1)} %get-tuple-element.49), channel_id=1, source_target_pairs={{0,1},{1,0},{2,3},{3,2},{4,5},{5,4},{6,7},{7,6},{8,9},{9,8},{10,11... | collective-permute-start | bytes 307208 | tf_op jit(solution)/shard_map/ppermute | solution.py:467
  12.5 13.4 %collective-permute-start.3 = (f32[40,640]{1,0:T(8,128)S(1)}, f32[40,640]{1,0:T(8,128)S(1)}, u32[]{:S(2)}, u32[]{:S(2)}) collective-permute-start(f32[40,640]{1,0:T(8,128)S(1)} %get-tuple-element.50), channel_id=1, source_target_pairs={{1,2},{3,4},{5,6},{7,8},{9,10},{11,12},{13,14},{2,1},{4,3},{6,5},{... | collective-permute-start | bytes 307208 | tf_op jit(solution)/shard_map/ppermute | solution.py:467
  28.8 20.7 %all-to-all-start = ((f32[128,1,128]{2,1,0:T(1,128)}), f32[128,1,128]{2,1,0:T(1,128)S(1)}, u32[]{:S(2)}, u32[]{:S(2)}) async-start(f32[128,1,128]{2,1,0:T(1,128)} %bitcast.1), calls=%async_computation | async-start | bytes 131072 | tf_op jit(solution)/shard_map/all_to_all | solution.py:561

commit v5 on v4

--- a/solution.py
+++ b/solution.py
@@ -454,6 +454,13 @@
             pltpu.make_async_copy(here, there, sem.at[1, n // 2]).start()
     for n, buf in enumerate((edge, mid)):
         pltpu.make_async_copy(buf, buf, sem.at[1, n]).wait()
+
+
+def total_kernel(parts, residual, kinetic, *, cells):
+    lane = lax.broadcasted_iota(jnp.int32, parts.shape, 1)
+    x = parts[...]
+    residual[0] = jnp.sum(jnp.where(lane == 0, x, 0.0)) * (1.0 / cells)
+    kinetic[0] = jnp.sum(jnp.where(lane == 1, x, 0.0)) * (0.0625 / cells)
 
 
 def swaps(count):
@@ -558,6 +565,7 @@
         compiler_params=limit(12),
         name="strips",
     )(own, cols, ext, xa, xb, ya, yb, isums)
+    msg = pltpu.with_memory_space_constraint(msg, pltpu.VMEM)
     parts = lax.all_to_all(msg, ALL, 0, 0, tiled=True)
     nvel, nstr = pl.pallas_call(
         merge_kernel,
@@ -569,9 +577,17 @@
         compiler_params=limit(12),
         name="merge",
     )(rows_out, cols_out, nvel, nstr)
-    total = jnp.sum(parts, axis=0)
     cells = R * lax.axis_size("gx") * C * lax.axis_size("gy")
-    return nvel, nstr, total[0] / cells, total[1] * (0.0625 / cells)
+    smem = pl.BlockSpec(memory_space=pltpu.SMEM)
+    residual, kinetic = pl.pallas_call(
+        functools.partial(total_kernel, cells=cells),
+        in_specs=[vmem],
+        out_specs=(smem, smem),
+        out_shape=(sds(1), sds(1)),
+        compiler_params=limit(2),
+        name="total",
+    )(parts)
+    return nvel, nstr, residual.reshape(()), kinetic.reshape(())
 
 
 def solution(mesh):

time: 54.1 us -> 50.4 us (0.932)
  between operations: 4.4 us -> 0.85 us
  Pallas kernels: 23.5 us -> 24.2 us
  local copies, waits for them, and re-layouts: 1.18 us -> 0.59 us
    pallas_call x0 -> x1, Pallas kernels: none -> 0.66 us  [per_device(): pl.pallas_call(functools.partial(total_kernel, cells=cells), in_specs=[vm...]
    slice x1 -> x0, local copies, waits for them, and re-layouts: 0.59 us -> none  [per_device(): return (nvel, nstr, total[0] / cells, total[1] * (0.0625 / cells))]
  transfers between devices with their start and end apart: 5 -> 5, of which waited for: 1 -> 1; matrix products, arithmetic and copies ran while one was open for 0% -> 0% of each run, Pallas kernels for 36% -> 38%
where the time goes in v5:
time: 50.4 us; the launch traced here: 50.1 us
  Pallas kernels  24.2 us (48%)
  starting transfers between devices  18.8 us (37%)
  waiting for transfers between devices  5.65 us (11%)
  between operations  0.85 us (2%)
  local copies, waits for them, and re-layouts  0.59 us (1%)
    all_to_all x1, starting transfers between devices, per_device(): parts = lax.all_to_all(msg, ALL, 0, 0, tiled=True)  10.8 us
    pallas_call x1, Pallas kernels, interior_rest(): pl.pallas_call(functools.partial(rest_kernel, RB=RB, L1=L1, L2=L2), in_sp...  10.1 us
    ppermute x4, starting transfers between devices, exchange(): return (lax.ppermute(a, axis, first), lax.ppermute(b, axis, second))  8 us
    all_to_all x1, waiting for transfers between devices, per_device(): parts = lax.all_to_all(msg, ALL, 0, 0, tiled=True)  5.64 us
    pallas_call x1, Pallas kernels, per_device(): pl.pallas_call(merge_kernel, in_specs=[vmem] * 2 + [hbm] * 2, out_specs=(...  4.13 us
    pallas_call x1, Pallas kernels, per_device(): pl.pallas_call(functools.partial(strips_kernel, R=R, C=C), in_specs=[vmem...  2.92 us
    pallas_call x1, Pallas kernels, interior_first(): pl.pallas_call(functools.partial(first_kernel, RB=RB, L1=L1, L2=L2), in_s...  2.79 us
    pallas_call x1, Pallas kernels, per_device(): pl.pallas_call(load_kernel, in_specs=[vmem] * 8, out_specs=(vmem, vmem),...  2.22 us
  transfers between devices with their start and end apart: 5, of which 1 were waited for; matrix products, arithmetic and copies ran while one was open for 0% of the time, Pallas kernels for 38%

profile of v5, /device:TPU:1, one launch (start us, length us, event | category | flops | bytes accessed | tf_op | source)
XLA Modules:
  0.0 50.1 jit_solution(7431994112250993454)
XLA Ops:
  0.6 0.0 copy-start.7
  0.6 0.0 copy-start.6
  0.7 0.0 copy-start.3
  0.7 0.0 copy-start.2
  0.7 0.0 copy-start.5
  0.7 1.1 %row_edges.1 = (f32[9,16,512]{2,1,0:T(8,128)S(1)}, f32[40,512]{1,0:T(8,128)S(1)}, f32[40,512]{1,0:T(8,128)S(1)}) custom-call(f32[2,512,512]{2,1,0:T(8,128)} %vel.1, f32[3,512,512]{2,1,0:T(8,128)} %strs.1, f32[512,512]{1,0:T(8,128)} %strength, f32[512,512]{1,0:T(8,128)} %mass, f32[2,512,512]{2,1,0:T(8,128)} %wind, f32[2,512,512]{2,1,0:T(8,128)} %cur, ...), custom_call_target="tpu_custom_call" | custom-call | tf_op jit(solution)/shard_map/row_edges/pallas_call | solution.py:524
  1.8 2.5 %collective-permute-start = (f32[40,512]{1,0:T(8,128)S(1)}, f32[40,512]{1,0:T(8,128)S(1)}, u32[]{:S(2)}, u32[]{:S(2)}) collective-permute-start(f32[40,512]{1,0:T(8,128)S(1)} %get-tuple-element.48), channel_id=1, source_target_pairs={{0,16},{16,0},{32,48},{48,32},{64,80},{80,64},{96,112},{112,96},{1... | collective-permute-start | bytes 245768 | tf_op jit(solution)/shard_map/ppermute | solution.py:474
  4.4 0.8 %collective-permute-start.1 = (f32[40,512]{1,0:T(8,128)S(1)}, f32[40,512]{1,0:T(8,128)S(1)}, u32[]{:S(2)}, u32[]{:S(2)}) collective-permute-start(f32[40,512]{1,0:T(8,128)S(1)} %get-tuple-element.49), channel_id=1, source_target_pairs={{16,32},{48,64},{80,96},{32,16},{64,48},{96,80},{17,33},{49,65},{8... | collective-permute-start | bytes 245768 | tf_op jit(solution)/shard_map/ppermute | solution.py:474
  5.2 0.6 %copy-done.1 = f32[2,512,512]{2,1,0:T(8,128)S(1)} copy-done((f32[2,512,512]{2,1,0:T(8,128)S(1)}, f32[2,512,512]{2,1,0:T(8,128)}, u32[]{:S(2)}) %copy-start.1) | copy-done | bytes 2097176
  5.8 2.2 %load.1 = (f32[6,512,512]{2,1,0:T(8,128)S(1)}, f32[144,512]{1,0:T(8,128)S(1)}) custom-call(f32[2,512,512]{2,1,0:T(8,128)S(1)} %copy-done.1, f32[3,512,512]{2,1,0:T(8,128)S(1)} %copy-done, f32[512,512]{1,0:T(8,128)S(1)} %copy-done.4, f32[512,512]{1,0:T(8,128)S(1)} %copy-done.5, f32[2,512,512]{2,1,0:T(8,128)S(1)} %copy-done.2, f32[2,512,512]{2,1,0:T(8,128)S(1)} %copy-done.3, ...), custom_call_target="tpu_custom_call" | custom-call | tf_op jit(solution)/shard_map/load/pallas_call | solution.py:535
  8.0 2.8 %first.1.x_in = f32[5,512,512]{2,1,0:T(8,128)S(1)} custom-call(f32[2,512,512]{2,1,0:T(8,128)S(1)} %copy-done.1, f32[3,512,512]{2,1,0:T(8,128)S(1)} %copy-done, f32[6,512,512]{2,1,0:T(8,128)S(1)} %get-tuple-element.46.con), custom_call_target="tpu_custom_call" | custom-call | tf_op jit(solution)/shard_map/first/pallas_call | solution.py:484
  10.8 0.0 collective-permute-done.xa
  10.8 0.0 collective-permute-done.1.xb
  10.8 0.2 corners.1
  11.1 1.5 %collective-permute-start.2 = (f32[40,640]{1,0:T(8,128)S(1)}, f32[40,640]{1,0:T(8,128)S(1)}, u32[]{:S(2)}, u32[]{:S(2)}) collective-permute-start(f32[40,640]{1,0:T(8,128)S(1)} %get-tuple-element.51), channel_id=1, source_target_pairs={{0,1},{1,0},{2,3},{3,2},{4,5},{5,4},{6,7},{7,6},{8,9},{9,8},{10,11... | collective-permute-start | bytes 307208 | tf_op jit(solution)/shard_map/ppermute | solution.py:474
  12.5 3.2 %collective-permute-start.3 = (f32[40,640]{1,0:T(8,128)S(1)}, f32[40,640]{1,0:T(8,128)S(1)}, u32[]{:S(2)}, u32[]{:S(2)}) collective-permute-start(f32[40,640]{1,0:T(8,128)S(1)} %get-tuple-element.52), channel_id=1, source_target_pairs={{1,2},{3,4},{5,6},{7,8},{9,10},{11,12},{13,14},{2,1},{4,3},{6,5},{... | collective-permute-start | bytes 307208 | tf_op jit(solution)/shard_map/ppermute | solution.py:474
  15.7 10.1 %rest.1 = (f32[5,512,512]{2,1,0:T(8,128)S(1)}, f32[2,512,512]{2,1,0:T(8,128)}, f32[3,512,512]{2,1,0:T(8,128)}, f32[2,8,128]{2,1,0:T(8,128)S(1)}) custom-call(f32[5,512,512]{2,1,0:T(8,128)S(1)} %first.1.x_in, f32[6,512,512]{2,1,0:T(8,128)S(1)} %get-tuple-element.46.con), custom_call_target="tpu_custom_call", output_to_operand_aliasing={{0}: (0, {})} | custom-call | tf_op jit(solution)/shard_map/rest/pallas_call | solution.py:499
  25.9 0.0 collective-permute-done.2.ya
  25.9 0.0 collective-permute-done.3.yb
  25.9 2.9 %strips.1 = (f32[5,16,512]{2,1,0:T(8,128)S(1)}, f32[5,16,512]{2,1,0:T(8,128)S(1)}, f32[128,128]{1,0:T(8,128)}) custom-call(f32[9,16,512]{2,1,0:T(8,128)S(1)} %get-tuple-element.34.own, f32[144,512]{1,0:T(8,128)S(1)} %get-tuple-element.47.cols, f32[144,128]{1,0:T(8,128)S(1)} %get-tuple-element.50.ext, f32[40,512]{1,0:T(8,128)S(1)} %collective-permute-done.xa, ...), custom_call_target="tpu_custom_call" | custom-call | tf_op jit(solution)/shard_map/strips/pallas_call | solution.py:556
  28.8 10.8 %all-to-all-start = ((f32[128,1,128]{2,1,0:T(1,128)}), f32[128,1,128]{2,1,0:T(1,128)S(1)}, u32[]{:S(2)}, u32[]{:S(2)}) async-start(f32[128,1,128]{2,1,0:T(1,128)} %bitcast.1), calls=%async_computation | async-start | bytes 131072 | tf_op jit(solution)/shard_map/all_to_all | solution.py:569
  39.7 4.1 %merge.1 = (f32[2,512,512]{2,1,0:T(8,128)}, f32[3,512,512]{2,1,0:T(8,128)}) custom-call(f32[5,16,512]{2,1,0:T(8,128)S(1)} %get-tuple-element.55.rows_in, f32[5,16,512]{2,1,0:T(8,128)S(1)} %get-tuple-element.56.cols_in, f32[2,512,512]{2,1,0:T(8,128)} %get-tuple-element.57.nvel_in, ...), custom_call_target="tpu_custom_call", output_to_operand_aliasing={{0}: (2, {}), {1}: (3, {})} | custom-call | tf_op jit(solution)/shard_map/merge/pallas_call | solution.py:570
  43.8 5.6 %all-to-all-done = f32[128,1,128]{2,1,0:T(1,128)S(1)} async-done(((f32[128,1,128]{2,1,0:T(1,128)}), f32[128,1,128]{2,1,0:T(1,128)S(1)}, u32[]{:S(2)}, u32[]{:S(2)}) %all-to-all-start) | async-done | bytes 65568 | tf_op jit(solution)/shard_map/all_to_all | solution.py:569
  49.5 0.7 %total.1 = (f32[1]{0:T(128)}, f32[1]{0:T(128)}) custom-call(f32[128,128]{1,0:T(8,128)S(1)} %bitcast.6), custom_call_target="tpu_custom_call" | custom-call | tf_op jit(solution)/shard_map/total/pallas_call | solution.py:582
  (10 shorter events, 0.0 us)
Async XLA Ops:
  0.6 4.5 %copy-start.7 = (s32[512,512]{1,0:T(8,128)S(1)}, s32[512,512]{1,0:T(8,128)}, u32[]{:S(2)}) copy-start(s32[512,512]{1,0:T(8,128)} %openw) | copy-start | bytes 3145732
  0.6 4.5 %copy-start.6 = (s32[512,512]{1,0:T(8,128)S(1)}, s32[512,512]{1,0:T(8,128)}, u32[]{:S(2)}) copy-start(s32[512,512]{1,0:T(8,128)} %mask) | copy-start | bytes 3145732
  0.7 4.5 %copy-start.3 = (f32[2,512,512]{2,1,0:T(8,128)S(1)}, f32[2,512,512]{2,1,0:T(8,128)}, u32[]{:S(2)}) copy-start(f32[2,512,512]{2,1,0:T(8,128)} %cur) | copy-start | bytes 6291460
  0.7 4.5 %copy-start.2 = (f32[2,512,512]{2,1,0:T(8,128)S(1)}, f32[2,512,512]{2,1,0:T(8,128)}, u32[]{:S(2)}) copy-start(f32[2,512,512]{2,1,0:T(8,128)} %wind) | copy-start | bytes 6291460
  0.7 4.5 %copy-start.5 = (f32[512,512]{1,0:T(8,128)S(1)}, f32[512,512]{1,0:T(8,128)}, u32[]{:S(2)}) copy-start(f32[512,512]{1,0:T(8,128)} %mass) | copy-start | bytes 3145732
  0.7 4.5 %copy-start.4 = (f32[512,512]{1,0:T(8,128)S(1)}, f32[512,512]{1,0:T(8,128)}, u32[]{:S(2)}) copy-start(f32[512,512]{1,0:T(8,128)} %strength) | copy-start | bytes 3145732
  0.7 4.5 %copy-start = (f32[3,512,512]{2,1,0:T(8,128)S(1)}, f32[3,512,512]{2,1,0:T(8,128)}, u32[]{:S(2)}) copy-start(f32[3,512,512]{2,1,0:T(8,128)} %strs.1) | copy-start | bytes 9437188
  0.7 5.1 %copy-start.1 = (f32[2,512,512]{2,1,0:T(8,128)S(1)}, f32[2,512,512]{2,1,0:T(8,128)}, u32[]{:S(2)}) copy-start(f32[2,512,512]{2,1,0:T(8,128)} %vel.1) | copy-start | bytes 6291460
  1.8 9.0 %collective-permute-start = (f32[40,512]{1,0:T(8,128)S(1)}, f32[40,512]{1,0:T(8,128)S(1)}, u32[]{:S(2)}, u32[]{:S(2)}) collective-permute-start(f32[40,512]{1,0:T(8,128)S(1)} %get-tuple-element.48), channel_id=1, source_target_pairs={{0,16},{16,0},{32,48},{48,32},{64,80},{80,64},{96,112},{112,96},{1... | collective-permute-start | bytes 245768 | tf_op jit(solution)/shard_map/ppermute | solution.py:474
  4.4 6.5 %collective-permute-start.1 = (f32[40,512]{1,0:T(8,128)S(1)}, f32[40,512]{1,0:T(8,128)S(1)}, u32[]{:S(2)}, u32[]{:S(2)}) collective-permute-start(f32[40,512]{1,0:T(8,128)S(1)} %get-tuple-element.49), channel_id=1, source_target_pairs={{16,32},{48,64},{80,96},{32,16},{64,48},{96,80},{17,33},{49,65},{8... | collective-permute-start | bytes 245768 | tf_op jit(solution)/shard_map/ppermute | solution.py:474
  11.1 14.8 %collective-permute-start.2 = (f32[40,640]{1,0:T(8,128)S(1)}, f32[40,640]{1,0:T(8,128)S(1)}, u32[]{:S(2)}, u32[]{:S(2)}) collective-permute-start(f32[40,640]{1,0:T(8,128)S(1)} %get-tuple-element.51), channel_id=1, source_target_pairs={{0,1},{1,0},{2,3},{3,2},{4,5},{5,4},{6,7},{7,6},{8,9},{9,8},{10,11... | collective-permute-start | bytes 307208 | tf_op jit(solution)/shard_map/ppermute | solution.py:474
  12.5 13.4 %collective-permute-start.3 = (f32[40,640]{1,0:T(8,128)S(1)}, f32[40,640]{1,0:T(8,128)S(1)}, u32[]{:S(2)}, u32[]{:S(2)}) collective-permute-start(f32[40,640]{1,0:T(8,128)S(1)} %get-tuple-element.52), channel_id=1, source_target_pairs={{1,2},{3,4},{5,6},{7,8},{9,10},{11,12},{13,14},{2,1},{4,3},{6,5},{... | collective-permute-start | bytes 307208 | tf_op jit(solution)/shard_map/ppermute | solution.py:474
  28.8 20.6 %all-to-all-start = ((f32[128,1,128]{2,1,0:T(1,128)}), f32[128,1,128]{2,1,0:T(1,128)S(1)}, u32[]{:S(2)}, u32[]{:S(2)}) async-start(f32[128,1,128]{2,1,0:T(1,128)} %bitcast.1), calls=%async_computation | async-start | bytes 131072 | tf_op jit(solution)/shard_map/all_to_all | solution.py:569

commit v6 on v5

--- a/solution.py
+++ b/solution.py
@@ -247,7 +247,7 @@
             held = (m, q)
         emit(NT - 1, *held, None)
 
-    def velocity_rows(r0, src, acc):
+    def velocity_rows(r0, src, acc, may_start=False):
         own = pl.ds(r0, 8)
         rows = pl.ds(PAD + r0, 8)
         below = pl.ds(PAD + r0 + 1, 8)
@@ -259,7 +259,11 @@
             x[U_, own, tile(t)] = nu
             x[V_, own, tile(t)] = nv
             if acc is not None:
-                keep = (con[k, own, tile(t)] > 0.0) & (row_in + r0 >= ITERS) & (row_in + r0 < R - ITERS)
+                keep = con[k, own, tile(t)] > 0.0
+                if may_start if not isinstance(r0, int) else r0 == 0:
+                    keep = keep & (row_in + r0 >= ITERS)
+                if isinstance(r0, int) and r0 == R - 8:
+                    keep = keep & (row_in < 8 - ITERS)
                 if t == 0:
                     keep = keep & (lane >= ITERS)
                 if t == NT - 1:
@@ -299,7 +303,7 @@
             for r in range(0, RB, 8):
                 strain_rows(r0 + r, src)
                 rate_rows(r0 + (r - L1), it)
-                velocity_rows(r0 + (r - L2), src, acc)
+                velocity_rows(r0 + (r - L2), src, acc, r == L2 % RB)
             return tuple(acc) if final else ()
 
         if not final:
@@ -312,8 +316,8 @@
         if r < L1:
             rate_rows(R + r - L1, its[-1])
         velocity_rows(R + r - L2, src, acc if final else None)
-        if final and r + 8 == L2 // 2:
-            send(R - L2 // 2)
+        if final and (r + 8) % 32 == 0 and r + 8 < L2:
+            send(R - L2 + r + 8)
     if not final:
         return
     send(R)
@@ -370,17 +374,16 @@
     a, b = ya[...], yb[...]
     left = jnp.where(even, b, a)
     right = jnp.where(even, a, b)
+    half_r = lax.broadcasted_iota(jnp.int32, (8, C), 0) < 4
+    half_c = lax.broadcasted_iota(jnp.int32, (8, R + 128), 0) < 4
     for f in range(NS):
-        rs[f, 0:8, :] = unpair(top, f, True)
-        rs[f, 8:16, :] = own[f, 0:8, :]
-        rs[f, 16:24, :] = own[f, 8:16, :]
-        rs[f, 24:32, :] = unpair(bot, f, False)
-        cs[f, 0:8, :] = unpair(left, f, True)
+        rs[f, 0:8, :] = jnp.where(half_r, unpair(bot, f, False), unpair(top, f, True))
+        rs[f, 8:24, :] = own[f]
+        cs[f, 0:8, :] = jnp.where(half_c, unpair(right, f, False), unpair(left, f, True))
         for side in range(2):
             base = 8 * (NS * side + f)
             cs[f, 8 + 8 * side : 16 + 8 * side, 0:R] = cols[base : base + 8, :]
             cs[f, 8 + 8 * side : 16 + 8 * side, R : R + 128] = ext[base : base + 8, :]
-        cs[f, 24:32, :] = unpair(right, f, False)
 
     def rim(shape):
         sub = lax.broadcasted_iota(jnp.int32, shape, 0)
@@ -559,13 +562,12 @@
         out_specs=(vmem, vmem, vmem),
         out_shape=(sds(5, 16, C), sds(5, 16, R), sds(ND, 128)),
         scratch_shapes=[
-            pltpu.VMEM((NF, 32, C), F32),
-            pltpu.VMEM((NF, 32, R + 128), F32),
+            pltpu.VMEM((NF, 24, C), F32),
+            pltpu.VMEM((NF, 24, R + 128), F32),
         ],
         compiler_params=limit(12),
         name="strips",
     )(own, cols, ext, xa, xb, ya, yb, isums)
-    msg = pltpu.with_memory_space_constraint(msg, pltpu.VMEM)
     parts = lax.all_to_all(msg, ALL, 0, 0, tiled=True)
     nvel, nstr = pl.pallas_call(
         merge_kernel,

time: 50.4 us -> 49.9 us (0.990)
  transfers between devices with their start and end apart: 5 -> 5, of which waited for: 1 -> 1; matrix products, arithmetic and copies ran while one was open for 0% -> 0% of each run, Pallas kernels for 38% -> 39%
where the time goes in v6:
time: 49.9 us; the launch traced here: 49.7 us
  Pallas kernels  23.7 us (47%)
  starting transfers between devices  18.8 us (38%)
  waiting for transfers between devices  5.65 us (11%)
  between operations  0.85 us (2%)
  local copies, waits for them, and re-layouts  0.59 us (1%)
    all_to_all x1, starting transfers between devices, per_device(): parts = lax.all_to_all(msg, ALL, 0, 0, tiled=True)  10.8 us
    pallas_call x1, Pallas kernels, interior_rest(): pl.pallas_call(functools.partial(rest_kernel, RB=RB, L1=L1, L2=L2), in_sp...  10.1 us
    ppermute x4, starting transfers between devices, exchange(): return (lax.ppermute(a, axis, first), lax.ppermute(b, axis, second))  8 us
    all_to_all x1, waiting for transfers between devices, per_device(): parts = lax.all_to_all(msg, ALL, 0, 0, tiled=True)  5.64 us
    pallas_call x1, Pallas kernels, per_device(): pl.pallas_call(merge_kernel, in_specs=[vmem] * 2 + [hbm] * 2, out_specs=(...  4.13 us
    pallas_call x1, Pallas kernels, interior_first(): pl.pallas_call(functools.partial(first_kernel, RB=RB, L1=L1, L2=L2), in_s...  2.79 us
    pallas_call x1, Pallas kernels, per_device(): pl.pallas_call(functools.partial(strips_kernel, R=R, C=C), in_specs=[vmem...  2.49 us
    pallas_call x1, Pallas kernels, per_device(): pl.pallas_call(load_kernel, in_specs=[vmem] * 8, out_specs=(vmem, vmem),...  2.22 us
  transfers between devices with their start and end apart: 5, of which 1 were waited for; matrix products, arithmetic and copies ran while one was open for 0% of the time, Pallas kernels for 39%

profile of v6, /device:TPU:1, one launch (start us, length us, event | category | flops | bytes accessed | tf_op | source)
XLA Modules:
  0.0 49.7 jit_solution(5324864658818392517)
XLA Ops:
  0.6 0.0 copy-start.7
  0.6 0.0 copy-start.6
  0.7 0.0 copy-start.3
  0.7 0.0 copy-start.2
  0.7 0.0 copy-start.5
  0.7 1.1 %row_edges.1 = (f32[9,16,512]{2,1,0:T(8,128)S(1)}, f32[40,512]{1,0:T(8,128)S(1)}, f32[40,512]{1,0:T(8,128)S(1)}) custom-call(f32[2,512,512]{2,1,0:T(8,128)} %vel.1, f32[3,512,512]{2,1,0:T(8,128)} %strs.1, f32[512,512]{1,0:T(8,128)} %strength, f32[512,512]{1,0:T(8,128)} %mass, f32[2,512,512]{2,1,0:T(8,128)} %wind, f32[2,512,512]{2,1,0:T(8,128)} %cur, ...), custom_call_target="tpu_custom_call" | custom-call | tf_op jit(solution)/shard_map/row_edges/pallas_call | solution.py:527
  1.8 2.5 %collective-permute-start = (f32[40,512]{1,0:T(8,128)S(1)}, f32[40,512]{1,0:T(8,128)S(1)}, u32[]{:S(2)}, u32[]{:S(2)}) collective-permute-start(f32[40,512]{1,0:T(8,128)S(1)} %get-tuple-element.48), channel_id=1, source_target_pairs={{0,16},{16,0},{32,48},{48,32},{64,80},{80,64},{96,112},{112,96},{1... | collective-permute-start | bytes 245768 | tf_op jit(solution)/shard_map/ppermute | solution.py:477
  4.4 0.8 %collective-permute-start.1 = (f32[40,512]{1,0:T(8,128)S(1)}, f32[40,512]{1,0:T(8,128)S(1)}, u32[]{:S(2)}, u32[]{:S(2)}) collective-permute-start(f32[40,512]{1,0:T(8,128)S(1)} %get-tuple-element.49), channel_id=1, source_target_pairs={{16,32},{48,64},{80,96},{32,16},{64,48},{96,80},{17,33},{49,65},{8... | collective-permute-start | bytes 245768 | tf_op jit(solution)/shard_map/ppermute | solution.py:477
  5.2 0.6 %copy-done.1 = f32[2,512,512]{2,1,0:T(8,128)S(1)} copy-done((f32[2,512,512]{2,1,0:T(8,128)S(1)}, f32[2,512,512]{2,1,0:T(8,128)}, u32[]{:S(2)}) %copy-start.1) | copy-done | bytes 2097176
  5.8 2.2 %load.1 = (f32[6,512,512]{2,1,0:T(8,128)S(1)}, f32[144,512]{1,0:T(8,128)S(1)}) custom-call(f32[2,512,512]{2,1,0:T(8,128)S(1)} %copy-done.1, f32[3,512,512]{2,1,0:T(8,128)S(1)} %copy-done, f32[512,512]{1,0:T(8,128)S(1)} %copy-done.4, f32[512,512]{1,0:T(8,128)S(1)} %copy-done.5, f32[2,512,512]{2,1,0:T(8,128)S(1)} %copy-done.2, f32[2,512,512]{2,1,0:T(8,128)S(1)} %copy-done.3, ...), custom_call_target="tpu_custom_call" | custom-call | tf_op jit(solution)/shard_map/load/pallas_call | solution.py:538
  8.0 2.8 %first.1.x_in = f32[5,512,512]{2,1,0:T(8,128)S(1)} custom-call(f32[2,512,512]{2,1,0:T(8,128)S(1)} %copy-done.1, f32[3,512,512]{2,1,0:T(8,128)S(1)} %copy-done, f32[6,512,512]{2,1,0:T(8,128)S(1)} %get-tuple-element.46.con), custom_call_target="tpu_custom_call" | custom-call | tf_op jit(solution)/shard_map/first/pallas_call | solution.py:487
  10.8 0.0 collective-permute-done.xa
  10.8 0.0 collective-permute-done.1.xb
  10.8 0.2 corners.1
  11.1 1.5 %collective-permute-start.2 = (f32[40,640]{1,0:T(8,128)S(1)}, f32[40,640]{1,0:T(8,128)S(1)}, u32[]{:S(2)}, u32[]{:S(2)}) collective-permute-start(f32[40,640]{1,0:T(8,128)S(1)} %get-tuple-element.51), channel_id=1, source_target_pairs={{0,1},{1,0},{2,3},{3,2},{4,5},{5,4},{6,7},{7,6},{8,9},{9,8},{10,11... | collective-permute-start | bytes 307208 | tf_op jit(solution)/shard_map/ppermute | solution.py:477
  12.5 3.2 %collective-permute-start.3 = (f32[40,640]{1,0:T(8,128)S(1)}, f32[40,640]{1,0:T(8,128)S(1)}, u32[]{:S(2)}, u32[]{:S(2)}) collective-permute-start(f32[40,640]{1,0:T(8,128)S(1)} %get-tuple-element.52), channel_id=1, source_target_pairs={{1,2},{3,4},{5,6},{7,8},{9,10},{11,12},{13,14},{2,1},{4,3},{6,5},{... | collective-permute-start | bytes 307208 | tf_op jit(solution)/shard_map/ppermute | solution.py:477
  15.7 10.1 %rest.1 = (f32[5,512,512]{2,1,0:T(8,128)S(1)}, f32[2,512,512]{2,1,0:T(8,128)}, f32[3,512,512]{2,1,0:T(8,128)}, f32[2,8,128]{2,1,0:T(8,128)S(1)}) custom-call(f32[5,512,512]{2,1,0:T(8,128)S(1)} %first.1.x_in, f32[6,512,512]{2,1,0:T(8,128)S(1)} %get-tuple-element.46.con), custom_call_target="tpu_custom_call", output_to_operand_aliasing={{0}: (0, {})} | custom-call | tf_op jit(solution)/shard_map/rest/pallas_call | solution.py:502
  25.9 0.0 collective-permute-done.2.ya
  25.9 0.0 collective-permute-done.3.yb
  25.9 2.5 %strips.1 = (f32[5,16,512]{2,1,0:T(8,128)S(1)}, f32[5,16,512]{2,1,0:T(8,128)S(1)}, f32[128,128]{1,0:T(8,128)}) custom-call(f32[9,16,512]{2,1,0:T(8,128)S(1)} %get-tuple-element.34.own, f32[144,512]{1,0:T(8,128)S(1)} %get-tuple-element.47.cols, f32[144,128]{1,0:T(8,128)S(1)} %get-tuple-element.50.ext, f32[40,512]{1,0:T(8,128)S(1)} %collective-permute-done.xa, ...), custom_call_target="tpu_custom_call" | custom-call | tf_op jit(solution)/shard_map/strips/pallas_call | solution.py:559
  28.4 10.8 %all-to-all-start = ((f32[128,1,128]{2,1,0:T(1,128)}), f32[128,1,128]{2,1,0:T(1,128)S(1)}, u32[]{:S(2)}, u32[]{:S(2)}) async-start(f32[128,1,128]{2,1,0:T(1,128)} %bitcast.1), calls=%async_computation | async-start | bytes 131072 | tf_op jit(solution)/shard_map/all_to_all | solution.py:571
  39.2 4.1 %merge.1 = (f32[2,512,512]{2,1,0:T(8,128)}, f32[3,512,512]{2,1,0:T(8,128)}) custom-call(f32[5,16,512]{2,1,0:T(8,128)S(1)} %get-tuple-element.55.rows_in, f32[5,16,512]{2,1,0:T(8,128)S(1)} %get-tuple-element.56.cols_in, f32[2,512,512]{2,1,0:T(8,128)} %get-tuple-element.57.nvel_in, ...), custom_call_target="tpu_custom_call", output_to_operand_aliasing={{0}: (2, {}), {1}: (3, {})} | custom-call | tf_op jit(solution)/shard_map/merge/pallas_call | solution.py:572
  43.4 5.6 %all-to-all-done = f32[128,1,128]{2,1,0:T(1,128)S(1)} async-done(((f32[128,1,128]{2,1,0:T(1,128)}), f32[128,1,128]{2,1,0:T(1,128)S(1)}, u32[]{:S(2)}, u32[]{:S(2)}) %all-to-all-start) | async-done | bytes 65568 | tf_op jit(solution)/shard_map/all_to_all | solution.py:571
  49.0 0.7 %total.1 = (f32[1]{0:T(128)}, f32[1]{0:T(128)}) custom-call(f32[128,128]{1,0:T(8,128)S(1)} %bitcast.6), custom_call_target="tpu_custom_call" | custom-call | tf_op jit(solution)/shard_map/total/pallas_call | solution.py:584
  (10 shorter events, 0.0 us)
Async XLA Ops:
  0.6 4.5 %copy-start.7 = (s32[512,512]{1,0:T(8,128)S(1)}, s32[512,512]{1,0:T(8,128)}, u32[]{:S(2)}) copy-start(s32[512,512]{1,0:T(8,128)} %openw) | copy-start | bytes 3145732
  0.6 4.5 %copy-start.6 = (s32[512,512]{1,0:T(8,128)S(1)}, s32[512,512]{1,0:T(8,128)}, u32[]{:S(2)}) copy-start(s32[512,512]{1,0:T(8,128)} %mask) | copy-start | bytes 3145732
  0.7 4.5 %copy-start.3 = (f32[2,512,512]{2,1,0:T(8,128)S(1)}, f32[2,512,512]{2,1,0:T(8,128)}, u32[]{:S(2)}) copy-start(f32[2,512,512]{2,1,0:T(8,128)} %cur) | copy-start | bytes 6291460
  0.7 4.5 %copy-start.2 = (f32[2,512,512]{2,1,0:T(8,128)S(1)}, f32[2,512,512]{2,1,0:T(8,128)}, u32[]{:S(2)}) copy-start(f32[2,512,512]{2,1,0:T(8,128)} %wind) | copy-start | bytes 6291460
  0.7 4.5 %copy-start.5 = (f32[512,512]{1,0:T(8,128)S(1)}, f32[512,512]{1,0:T(8,128)}, u32[]{:S(2)}) copy-start(f32[512,512]{1,0:T(8,128)} %mass) | copy-start | bytes 3145732
  0.7 4.5 %copy-start.4 = (f32[512,512]{1,0:T(8,128)S(1)}, f32[512,512]{1,0:T(8,128)}, u32[]{:S(2)}) copy-start(f32[512,512]{1,0:T(8,128)} %strength) | copy-start | bytes 3145732
  0.7 4.5 %copy-start = (f32[3,512,512]{2,1,0:T(8,128)S(1)}, f32[3,512,512]{2,1,0:T(8,128)}, u32[]{:S(2)}) copy-start(f32[3,512,512]{2,1,0:T(8,128)} %strs.1) | copy-start | bytes 9437188
  0.7 5.1 %copy-start.1 = (f32[2,512,512]{2,1,0:T(8,128)S(1)}, f32[2,512,512]{2,1,0:T(8,128)}, u32[]{:S(2)}) copy-start(f32[2,512,512]{2,1,0:T(8,128)} %vel.1) | copy-start | bytes 6291460
  1.8 9.0 %collective-permute-start = (f32[40,512]{1,0:T(8,128)S(1)}, f32[40,512]{1,0:T(8,128)S(1)}, u32[]{:S(2)}, u32[]{:S(2)}) collective-permute-start(f32[40,512]{1,0:T(8,128)S(1)} %get-tuple-element.48), channel_id=1, source_target_pairs={{0,16},{16,0},{32,48},{48,32},{64,80},{80,64},{96,112},{112,96},{1... | collective-permute-start | bytes 245768 | tf_op jit(solution)/shard_map/ppermute | solution.py:477
  4.4 6.5 %collective-permute-start.1 = (f32[40,512]{1,0:T(8,128)S(1)}, f32[40,512]{1,0:T(8,128)S(1)}, u32[]{:S(2)}, u32[]{:S(2)}) collective-permute-start(f32[40,512]{1,0:T(8,128)S(1)} %get-tuple-element.49), channel_id=1, source_target_pairs={{16,32},{48,64},{80,96},{32,16},{64,48},{96,80},{17,33},{49,65},{8... | collective-permute-start | bytes 245768 | tf_op jit(solution)/shard_map/ppermute | solution.py:477
  11.1 14.8 %collective-permute-start.2 = (f32[40,640]{1,0:T(8,128)S(1)}, f32[40,640]{1,0:T(8,128)S(1)}, u32[]{:S(2)}, u32[]{:S(2)}) collective-permute-start(f32[40,640]{1,0:T(8,128)S(1)} %get-tuple-element.51), channel_id=1, source_target_pairs={{0,1},{1,0},{2,3},{3,2},{4,5},{5,4},{6,7},{7,6},{8,9},{9,8},{10,11... | collective-permute-start | bytes 307208 | tf_op jit(solution)/shard_map/ppermute | solution.py:477
  12.5 13.4 %collective-permute-start.3 = (f32[40,640]{1,0:T(8,128)S(1)}, f32[40,640]{1,0:T(8,128)S(1)}, u32[]{:S(2)}, u32[]{:S(2)}) collective-permute-start(f32[40,640]{1,0:T(8,128)S(1)} %get-tuple-element.52), channel_id=1, source_target_pairs={{1,2},{3,4},{5,6},{7,8},{9,10},{11,12},{13,14},{2,1},{4,3},{6,5},{... | collective-permute-start | bytes 307208 | tf_op jit(solution)/shard_map/ppermute | solution.py:477
  28.4 20.6 %all-to-all-start = ((f32[128,1,128]{2,1,0:T(1,128)}), f32[128,1,128]{2,1,0:T(1,128)S(1)}, u32[]{:S(2)}, u32[]{:S(2)}) async-start(f32[128,1,128]{2,1,0:T(1,128)} %bitcast.1), calls=%async_computation | async-start | bytes 131072 | tf_op jit(solution)/shard_map/all_to_all | solution.py:571

commit v7 on v6

--- a/solution.py
+++ b/solution.py
@@ -12,6 +12,7 @@
 GROW = 1.0 / (1.0 + RELAX)
 KAPPA = RELAX / (1.0 + RELAX)
 PAD = 8
+TAIL = 32
 F32 = jnp.float32
 (U_, V_, H1, H2, H12, K_, M8, FU, FV, CA, CB) = range(11)
 NS = 9
@@ -188,7 +189,7 @@
     yb[...] = jnp.where(even, low, high)
 
 
-def sweep_subcycles(its, vel, strs, con, x, nvel, nstr, sums, al, be, ga, de, tx, ty, nx, ny, sem, *, RB, L1, L2):
+def sweep_subcycles(its, vel, strs, con, x, nvel, nstr, sums, tail, al, be, ga, de, tx, ty, nx, ny, sem, *, RB, L1, L2):
     R, C = x.shape[1:]
     NT = C // 128
     k, m8_, fu_, fv_, ca_, cb_ = range(6)
@@ -316,22 +317,24 @@
         if r < L1:
             rate_rows(R + r - L1, its[-1])
         velocity_rows(R + r - L2, src, acc if final else None)
-        if final and (r + 8) % 32 == 0 and r + 8 < L2:
+        if final and (r + 8) % TAIL == 0 and r + 8 < L2:
             send(R - L2 + r + 8)
     if not final:
         return
-    send(R)
+    for f in range(5):
+        tail[f] = x[f, R - TAIL : R, :]
     sums[0] = acc[0] + acc[2]
     sums[1] = acc[1] + acc[3]
-    pltpu.make_async_copy(x, x, sem).wait()
+    whole = x.at[:, pl.ds(0, R - TAIL)]
+    pltpu.make_async_copy(whole, whole, sem).wait()
 
 
 def first_kernel(vel, strs, con, x, *work, **kw):
-    sweep_subcycles([0], vel, strs, con, x, None, None, None, *work, None, **kw)
-
-
-def rest_kernel(x_in, con, x, nvel, nstr, sums, *work, **kw):
-    sweep_subcycles(list(range(1, ITERS)), None, None, con, x, nvel, nstr, sums, *work, **kw)
+    sweep_subcycles([0], vel, strs, con, x, None, None, None, None, *work, None, **kw)
+
+
+def rest_kernel(x_in, con, x, nvel, nstr, sums, tail, *work, **kw):
+    sweep_subcycles(list(range(1, ITERS)), None, None, con, x, nvel, nstr, sums, tail, *work, **kw)
 
 
 def strip_begin(ref):
@@ -411,7 +414,7 @@
         cols_out[f] = half * cs[f, 8:24, 0:R]
 
 
-def merge_kernel(rows_in, cols_in, nvel_in, nstr_in, nvel, nstr, edge, mid, sem):
+def merge_kernel(rows_in, cols_in, tail, nvel_in, nstr_in, nvel, nstr, edge, mid, sem):
     R, C = nvel.shape[1:]
     outs = ((nvel, 0), (nvel, 1), (nstr, 0), (nstr, 1), (nstr, 2))
     inner = pl.ds(128, C - 256)
@@ -429,8 +432,15 @@
     for f in range(5):
         for n, (there, here) in enumerate(places(f)):
             pltpu.make_async_copy(there, here, sem.at[0, n // 2]).start()
+    held = tail.at[:, pl.ds(0, TAIL - 8), inner]
+    for f, (ref, lead) in enumerate(outs):
+        pltpu.make_async_copy(held.at[f], ref.at[lead, pl.ds(R - TAIL, TAIL - 8), inner], sem.at[2, 0]).start()
     for n, buf in enumerate((edge, mid)):
         pltpu.make_async_copy(buf, buf, sem.at[0, n]).wait()
+    for f in range(5):
+        mid[1, f] = tail[f, TAIL - 8 : TAIL, 128 : C - 128]
+        edge[0, f, R - TAIL : R, :] = tail[f, :, 0:128]
+        edge[1, f, R - TAIL : R, :] = tail[f, :, C - 128 : C]
     low = lax.broadcasted_iota(jnp.int32, (8, C), 0) < 4
     for f in range(5):
         for part in range(2):
@@ -457,6 +467,7 @@
             pltpu.make_async_copy(here, there, sem.at[1, n // 2]).start()
     for n, buf in enumerate((edge, mid)):
         pltpu.make_async_copy(buf, buf, sem.at[1, n]).wait()
+    pltpu.make_async_copy(held, held, sem.at[2, 0]).wait()
 
 
 def total_kernel(parts, residual, kinetic, *, cells):
@@ -502,8 +513,8 @@
     return pl.pallas_call(
         functools.partial(rest_kernel, RB=RB, L1=L1, L2=L2),
         in_specs=[vmem] * 2,
-        out_specs=(vmem, hbm, hbm, vmem),
-        out_shape=(sds(5, R, C), sds(2, R, C), sds(3, R, C), sds(2, 8, 128)),
+        out_specs=(vmem, hbm, hbm, vmem, vmem),
+        out_shape=(sds(5, R, C), sds(2, R, C), sds(3, R, C), sds(2, 8, 128), sds(5, TAIL, C)),
         scratch_shapes=[pltpu.VMEM((C // 128, R + 2 * PAD, 128), F32)] * 8 + [pltpu.SemaphoreType.DMA(())],
         input_output_aliases={0: 0},
         compiler_params=pltpu.CompilerParams(vmem_limit_bytes=12 * 2**20),
@@ -554,7 +565,7 @@
         name="corners",
     )(cols, xa, xb)
     ya, yb = exchange(ya, yb, "gy")
-    _, nvel, nstr, isums = interior_rest(x, con)
+    _, nvel, nstr, isums, tail = interior_rest(x, con)
     ND = lax.axis_size(ALL)
     rows_out, cols_out, msg = pl.pallas_call(
         functools.partial(strips_kernel, R=R, C=C),
@@ -571,14 +582,14 @@
     parts = lax.all_to_all(msg, ALL, 0, 0, tiled=True)
     nvel, nstr = pl.pallas_call(
         merge_kernel,
-        in_specs=[vmem] * 2 + [hbm] * 2,
+        in_specs=[vmem] * 3 + [hbm] * 2,
         out_specs=(hbm, hbm),
         out_shape=(sds(2, R, C), sds(3, R, C)),
-        scratch_shapes=[pltpu.VMEM((2, 5, R, 128), F32), pltpu.VMEM((2, 5, 8, C - 256), F32), pltpu.SemaphoreType.DMA((2, 2))],
-        input_output_aliases={2: 0, 3: 1},
+        scratch_shapes=[pltpu.VMEM((2, 5, R, 128), F32), pltpu.VMEM((2, 5, 8, C - 256), F32), pltpu.SemaphoreType.DMA((3, 2))],
+        input_output_aliases={3: 0, 4: 1},
         compiler_params=limit(12),
         name="merge",
-    )(rows_out, cols_out, nvel, nstr)
+    )(rows_out, cols_out, tail, nvel, nstr)
     cells = R * lax.axis_size("gx") * C * lax.axis_size("gy")
     smem = pl.BlockSpec(memory_space=pltpu.SMEM)
     residual, kinetic = pl.pallas_call(

time: 49.9 us -> 49.9 us (level)
  no operation moved by 1% of the time
where the time goes in v7:
time: 49.9 us; the launch traced here: 49.6 us
  Pallas kernels  23.7 us (47%)
  starting transfers between devices  18.8 us (38%)
  waiting for transfers between devices  5.59 us (11%)
  between operations  0.85 us (2%)
  local copies, waits for them, and re-layouts  0.59 us (1%)
    all_to_all x1, starting transfers between devices, per_device(): parts = lax.all_to_all(msg, ALL, 0, 0, tiled=True)  10.8 us
    pallas_call x1, Pallas kernels, interior_rest(): pl.pallas_call(functools.partial(rest_kernel, RB=RB, L1=L1, L2=L2), in_sp...  10.1 us
    ppermute x4, starting transfers between devices, exchange(): return (lax.ppermute(a, axis, first), lax.ppermute(b, axis, second))  8 us
    all_to_all x1, waiting for transfers between devices, per_device(): parts = lax.all_to_all(msg, ALL, 0, 0, tiled=True)  5.58 us
    pallas_call x1, Pallas kernels, per_device(): pl.pallas_call(merge_kernel, in_specs=[vmem] * 3 + [hbm] * 2, out_specs=(...  4.19 us
    pallas_call x1, Pallas kernels, interior_first(): pl.pallas_call(functools.partial(first_kernel, RB=RB, L1=L1, L2=L2), in_s...  2.79 us
    pallas_call x1, Pallas kernels, per_device(): pl.pallas_call(functools.partial(strips_kernel, R=R, C=C), in_specs=[vmem...  2.49 us
    pallas_call x1, Pallas kernels, per_device(): pl.pallas_call(load_kernel, in_specs=[vmem] * 8, out_specs=(vmem, vmem),...  2.22 us
  transfers between devices with their start and end apart: 5, of which 1 were waited for; matrix products, arithmetic and copies ran while one was open for 0% of the time, Pallas kernels for 39%

profile of v7, /device:TPU:1, one launch (start us, length us, event | category | flops | bytes accessed | tf_op | source)
XLA Modules:
  0.0 49.6 jit_solution(3688792591236653013)
XLA Ops:
  0.6 0.0 copy-start.7
  0.6 0.0 copy-start.6
  0.7 0.0 copy-start.3
  0.7 0.0 copy-start.2
  0.7 0.0 copy-start.5
  0.7 1.1 %row_edges.1 = (f32[9,16,512]{2,1,0:T(8,128)S(1)}, f32[40,512]{1,0:T(8,128)S(1)}, f32[40,512]{1,0:T(8,128)S(1)}) custom-call(f32[2,512,512]{2,1,0:T(8,128)} %vel.1, f32[3,512,512]{2,1,0:T(8,128)} %strs.1, f32[512,512]{1,0:T(8,128)} %strength, f32[512,512]{1,0:T(8,128)} %mass, f32[2,512,512]{2,1,0:T(8,128)} %wind, f32[2,512,512]{2,1,0:T(8,128)} %cur, ...), custom_call_target="tpu_custom_call" | custom-call | tf_op jit(solution)/shard_map/row_edges/pallas_call | solution.py:538
  1.8 2.5 %collective-permute-start = (f32[40,512]{1,0:T(8,128)S(1)}, f32[40,512]{1,0:T(8,128)S(1)}, u32[]{:S(2)}, u32[]{:S(2)}) collective-permute-start(f32[40,512]{1,0:T(8,128)S(1)} %get-tuple-element.49), channel_id=1, source_target_pairs={{0,16},{16,0},{32,48},{48,32},{64,80},{80,64},{96,112},{112,96},{1... | collective-permute-start | bytes 245768 | tf_op jit(solution)/shard_map/ppermute | solution.py:488
  4.4 0.8 %collective-permute-start.1 = (f32[40,512]{1,0:T(8,128)S(1)}, f32[40,512]{1,0:T(8,128)S(1)}, u32[]{:S(2)}, u32[]{:S(2)}) collective-permute-start(f32[40,512]{1,0:T(8,128)S(1)} %get-tuple-element.50), channel_id=1, source_target_pairs={{16,32},{48,64},{80,96},{32,16},{64,48},{96,80},{17,33},{49,65},{8... | collective-permute-start | bytes 245768 | tf_op jit(solution)/shard_map/ppermute | solution.py:488
  5.2 0.6 %copy-done.1 = f32[2,512,512]{2,1,0:T(8,128)S(1)} copy-done((f32[2,512,512]{2,1,0:T(8,128)S(1)}, f32[2,512,512]{2,1,0:T(8,128)}, u32[]{:S(2)}) %copy-start.1) | copy-done | bytes 2097176
  5.8 2.2 %load.1 = (f32[6,512,512]{2,1,0:T(8,128)S(1)}, f32[144,512]{1,0:T(8,128)S(1)}) custom-call(f32[2,512,512]{2,1,0:T(8,128)S(1)} %copy-done.1, f32[3,512,512]{2,1,0:T(8,128)S(1)} %copy-done, f32[512,512]{1,0:T(8,128)S(1)} %copy-done.4, f32[512,512]{1,0:T(8,128)S(1)} %copy-done.5, f32[2,512,512]{2,1,0:T(8,128)S(1)} %copy-done.2, f32[2,512,512]{2,1,0:T(8,128)S(1)} %copy-done.3, ...), custom_call_target="tpu_custom_call" | custom-call | tf_op jit(solution)/shard_map/load/pallas_call | solution.py:549
  8.0 2.8 %first.1.x_in = f32[5,512,512]{2,1,0:T(8,128)S(1)} custom-call(f32[2,512,512]{2,1,0:T(8,128)S(1)} %copy-done.1, f32[3,512,512]{2,1,0:T(8,128)S(1)} %copy-done, f32[6,512,512]{2,1,0:T(8,128)S(1)} %get-tuple-element.47.con), custom_call_target="tpu_custom_call" | custom-call | tf_op jit(solution)/shard_map/first/pallas_call | solution.py:498
  10.8 0.0 collective-permute-done.xa
  10.8 0.0 collective-permute-done.1.xb
  10.8 0.2 corners.1
  11.1 1.5 %collective-permute-start.2 = (f32[40,640]{1,0:T(8,128)S(1)}, f32[40,640]{1,0:T(8,128)S(1)}, u32[]{:S(2)}, u32[]{:S(2)}) collective-permute-start(f32[40,640]{1,0:T(8,128)S(1)} %get-tuple-element.52), channel_id=1, source_target_pairs={{0,1},{1,0},{2,3},{3,2},{4,5},{5,4},{6,7},{7,6},{8,9},{9,8},{10,11... | collective-permute-start | bytes 307208 | tf_op jit(solution)/shard_map/ppermute | solution.py:488
  12.5 3.2 %collective-permute-start.3 = (f32[40,640]{1,0:T(8,128)S(1)}, f32[40,640]{1,0:T(8,128)S(1)}, u32[]{:S(2)}, u32[]{:S(2)}) collective-permute-start(f32[40,640]{1,0:T(8,128)S(1)} %get-tuple-element.53), channel_id=1, source_target_pairs={{1,2},{3,4},{5,6},{7,8},{9,10},{11,12},{13,14},{2,1},{4,3},{6,5},{... | collective-permute-start | bytes 307208 | tf_op jit(solution)/shard_map/ppermute | solution.py:488
  15.7 10.1 %rest.1 = (f32[5,512,512]{2,1,0:T(8,128)S(1)}, f32[2,512,512]{2,1,0:T(8,128)}, f32[3,512,512]{2,1,0:T(8,128)}, f32[2,8,128]{2,1,0:T(8,128)S(1)}, f32[5,32,512]{2,1,0:T(8,128)S(1)}) custom-call(f32[5,512,512]{2,1,0:T(8,128)S(1)} %first.1.x_in, f32[6,512,512]{2,1,0:T(8,128)S(1)} %get-tuple-element.47.con), custom_call_target="tpu_custom_call", output_to_operand_aliasing={{0}: (0, {})} | custom-call | tf_op jit(solution)/shard_map/rest/pallas_call | solution.py:513
  25.8 0.0 collective-permute-done.2.ya
  25.8 0.0 collective-permute-done.3.yb
  25.8 2.5 %strips.1 = (f32[5,16,512]{2,1,0:T(8,128)S(1)}, f32[5,16,512]{2,1,0:T(8,128)S(1)}, f32[128,128]{1,0:T(8,128)}) custom-call(f32[9,16,512]{2,1,0:T(8,128)S(1)} %get-tuple-element.35.own, f32[144,512]{1,0:T(8,128)S(1)} %get-tuple-element.48.cols, f32[144,128]{1,0:T(8,128)S(1)} %get-tuple-element.51.ext, f32[40,512]{1,0:T(8,128)S(1)} %collective-permute-done.xa, ...), custom_call_target="tpu_custom_call" | custom-call | tf_op jit(solution)/shard_map/strips/pallas_call | solution.py:570
  28.3 10.8 %all-to-all-start = ((f32[128,1,128]{2,1,0:T(1,128)}), f32[128,1,128]{2,1,0:T(1,128)S(1)}, u32[]{:S(2)}, u32[]{:S(2)}) async-start(f32[128,1,128]{2,1,0:T(1,128)} %bitcast.1), calls=%async_computation | async-start | bytes 131072 | tf_op jit(solution)/shard_map/all_to_all | solution.py:582
  39.2 4.2 %merge.1 = (f32[2,512,512]{2,1,0:T(8,128)}, f32[3,512,512]{2,1,0:T(8,128)}) custom-call(f32[5,16,512]{2,1,0:T(8,128)S(1)} %get-tuple-element.56.rows_in, f32[5,16,512]{2,1,0:T(8,128)S(1)} %get-tuple-element.57.cols_in, f32[5,32,512]{2,1,0:T(8,128)S(1)} %get-tuple-element.58.tail, ...), custom_call_target="tpu_custom_call", output_to_operand_aliasing={{0}: (3, {}), {1}: (4, {})} | custom-call | tf_op jit(solution)/shard_map/merge/pallas_call | solution.py:583
  43.4 5.6 %all-to-all-done = f32[128,1,128]{2,1,0:T(1,128)S(1)} async-done(((f32[128,1,128]{2,1,0:T(1,128)}), f32[128,1,128]{2,1,0:T(1,128)S(1)}, u32[]{:S(2)}, u32[]{:S(2)}) %all-to-all-start) | async-done | bytes 65568 | tf_op jit(solution)/shard_map/all_to_all | solution.py:582
  49.0 0.7 %total.1 = (f32[1]{0:T(128)}, f32[1]{0:T(128)}) custom-call(f32[128,128]{1,0:T(8,128)S(1)} %bitcast.6), custom_call_target="tpu_custom_call" | custom-call | tf_op jit(solution)/shard_map/total/pallas_call | solution.py:595
  (10 shorter events, 0.0 us)
Async XLA Ops:
  0.6 4.5 %copy-start.7 = (s32[512,512]{1,0:T(8,128)S(1)}, s32[512,512]{1,0:T(8,128)}, u32[]{:S(2)}) copy-start(s32[512,512]{1,0:T(8,128)} %openw) | copy-start | bytes 3145732
  0.6 4.5 %copy-start.6 = (s32[512,512]{1,0:T(8,128)S(1)}, s32[512,512]{1,0:T(8,128)}, u32[]{:S(2)}) copy-start(s32[512,512]{1,0:T(8,128)} %mask) | copy-start | bytes 3145732
  0.7 4.5 %copy-start.3 = (f32[2,512,512]{2,1,0:T(8,128)S(1)}, f32[2,512,512]{2,1,0:T(8,128)}, u32[]{:S(2)}) copy-start(f32[2,512,512]{2,1,0:T(8,128)} %cur) | copy-start | bytes 6291460
  0.7 4.5 %copy-start.2 = (f32[2,512,512]{2,1,0:T(8,128)S(1)}, f32[2,512,512]{2,1,0:T(8,128)}, u32[]{:S(2)}) copy-start(f32[2,512,512]{2,1,0:T(8,128)} %wind) | copy-start | bytes 6291460
  0.7 4.5 %copy-start.5 = (f32[512,512]{1,0:T(8,128)S(1)}, f32[512,512]{1,0:T(8,128)}, u32[]{:S(2)}) copy-start(f32[512,512]{1,0:T(8,128)} %mass) | copy-start | bytes 3145732
  0.7 4.5 %copy-start.4 = (f32[512,512]{1,0:T(8,128)S(1)}, f32[512,512]{1,0:T(8,128)}, u32[]{:S(2)}) copy-start(f32[512,512]{1,0:T(8,128)} %strength) | copy-start | bytes 3145732
  0.7 4.5 %copy-start = (f32[3,512,512]{2,1,0:T(8,128)S(1)}, f32[3,512,512]{2,1,0:T(8,128)}, u32[]{:S(2)}) copy-start(f32[3,512,512]{2,1,0:T(8,128)} %strs.1) | copy-start | bytes 9437188
  0.7 5.1 %copy-start.1 = (f32[2,512,512]{2,1,0:T(8,128)S(1)}, f32[2,512,512]{2,1,0:T(8,128)}, u32[]{:S(2)}) copy-start(f32[2,512,512]{2,1,0:T(8,128)} %vel.1) | copy-start | bytes 6291460
  1.8 9.0 %collective-permute-start = (f32[40,512]{1,0:T(8,128)S(1)}, f32[40,512]{1,0:T(8,128)S(1)}, u32[]{:S(2)}, u32[]{:S(2)}) collective-permute-start(f32[40,512]{1,0:T(8,128)S(1)} %get-tuple-element.49), channel_id=1, source_target_pairs={{0,16},{16,0},{32,48},{48,32},{64,80},{80,64},{96,112},{112,96},{1... | collective-permute-start | bytes 245768 | tf_op jit(solution)/shard_map/ppermute | solution.py:488
  4.4 6.5 %collective-permute-start.1 = (f32[40,512]{1,0:T(8,128)S(1)}, f32[40,512]{1,0:T(8,128)S(1)}, u32[]{:S(2)}, u32[]{:S(2)}) collective-permute-start(f32[40,512]{1,0:T(8,128)S(1)} %get-tuple-element.50), channel_id=1, source_target_pairs={{16,32},{48,64},{80,96},{32,16},{64,48},{96,80},{17,33},{49,65},{8... | collective-permute-start | bytes 245768 | tf_op jit(solution)/shard_map/ppermute | solution.py:488
  11.1 14.8 %collective-permute-start.2 = (f32[40,640]{1,0:T(8,128)S(1)}, f32[40,640]{1,0:T(8,128)S(1)}, u32[]{:S(2)}, u32[]{:S(2)}) collective-permute-start(f32[40,640]{1,0:T(8,128)S(1)} %get-tuple-element.52), channel_id=1, source_target_pairs={{0,1},{1,0},{2,3},{3,2},{4,5},{5,4},{6,7},{7,6},{8,9},{9,8},{10,11... | collective-permute-start | bytes 307208 | tf_op jit(solution)/shard_map/ppermute | solution.py:488
  12.5 13.3 %collective-permute-start.3 = (f32[40,640]{1,0:T(8,128)S(1)}, f32[40,640]{1,0:T(8,128)S(1)}, u32[]{:S(2)}, u32[]{:S(2)}) collective-permute-start(f32[40,640]{1,0:T(8,128)S(1)} %get-tuple-element.53), channel_id=1, source_target_pairs={{1,2},{3,4},{5,6},{7,8},{9,10},{11,12},{13,14},{2,1},{4,3},{6,5},{... | collective-permute-start | bytes 307208 | tf_op jit(solution)/shard_map/ppermute | solution.py:488
  28.3 20.6 %all-to-all-start = ((f32[128,1,128]{2,1,0:T(1,128)}), f32[128,1,128]{2,1,0:T(1,128)S(1)}, u32[]{:S(2)}, u32[]{:S(2)}) async-start(f32[128,1,128]{2,1,0:T(1,128)} %bitcast.1), calls=%async_computation | async-start | bytes 131072 | tf_op jit(solution)/shard_map/all_to_all | solution.py:582
